TPU v7x, 128 devices: a whole 4x4x4 slice. The times are simulated.
128 devices in a mesh: cls: 4 (over z), site: 32 (over x, y, core).
Axes of the slice: x: 4, y: 4, z: 4, core: 2. Of those that a mesh axis runs over, the one named last changes fastest.
Arguments:
- tip_codes: int32 [1024, 32768], P('cls', 'site'), may hold values from 0 to 3
- counts: int32 [32768], P('site'), may hold values from 1 to 5
- children: int32 [1023, 2], replicated, may hold values from 0 to 2045, as said below
- lengths: float32 [4, 2046], replicated, may hold values from 0.01 to 1
- frequencies: float32 [4, 4], replicated, may hold values from 0.25 to 1.75
- weights: float32 [4], replicated, may hold values from 0.2 to 1
Outputs:
- site_loglik: float32 [4, 8192], P('cls', 'site')
- new_weights: float32 [4], P('cls')
- mean_loglik: float32 [], replicated
Inputs may be any that keep to these rules, and one draw needn't show every extreme that they name: Row k lists the two children of internal node 1024 + k as node ids. Give the tips height 0 and the root height 10. The nodes of height h + 1 have exactly the nodes of height h as children, each once, and the root is node 2046. For every height h from 0 to 5, split the parents (height h + 1) and the children (height h) into 16 equal aligned blocks: the children of parent block j are child block j, so the tips j * 64 onward form clade j.
All inputs are finite; a program needn't handle non-finite values.
Results may differ from a plain program's by a relative error of at most 0.0003.
Values sent between devices are 32-bit elements; how exact they have to be, the bound alone decides.
No kernel may reach another device: no remote copies, remote signals or barrier semaphores. Data moves between devices by JAX's collectives and lax.ppermute only.
A program may use at most 64 MiB of HBM per device.

v0:
```python
import functools

import jax
import jax.numpy as jnp
from jax import lax
from jax.sharding import Mesh
from jax.sharding import PartitionSpec as P

LEVELS = 10
TOP = 4
SITE = ("site_0", "site_1", "site_2")


def all_in_one(array, axis):
    leaves = jax.tree.leaves(array)
    sequence = sorted(range(len(leaves)), key=lambda k: -leaves[k].size)
    width = (1, *leaves[sequence[0]].shape)[-1]
    lines = [
        jnp.pad(leaves[k].reshape(-1), (0, -leaves[k].size % width)).reshape(-1, width)
        for k in sequence
    ]
    both, at, found = (lax.all_gather(jnp.concatenate(lines), axis), 0, {})
    for k, line in zip(sequence, lines):
        share = both[:, at : at + len(line)].reshape(len(both), -1)
        found[k] = share[:, : leaves[k].size].reshape(-1, *leaves[k].shape)
        at += len(line)
    numbers = iter(range(len(leaves)))
    return jax.tree.map(lambda _: found[next(numbers)], array)


def combined_all(part, axis, combine):
    gathered = all_in_one(part, axis)

    def take(source):
        return jax.tree.map(lambda a: lax.dynamic_index_in_dim(a, source, 0, False), gathered)

    return lax.fori_loop(
        1, lax.axis_size(axis), lambda source, state: combine(state, take(source)), take(0)
    )


def one_axis_at_a_time(array, axes):
    return functools.reduce(lax.psum, axes, array)


def transit(values, decays, stationary):
    average = jnp.sum(stationary[:, None, None] * values, axis=0, keepdims=True)
    return decays[None, :, None] * values + (1.0 - decays)[None, :, None] * average


def join_pair(left_part, right_part, scale_sum):
    parent = left_part * right_part
    largest = jnp.max(parent, axis=0, keepdims=True)
    return (parent / largest, scale_sum + jnp.log(largest))


def rate_of(stationary):
    return 1.0 / (1.0 - jnp.sum(stationary * stationary))


def selector(child_ids, anchor, previous):
    both_rows = jnp.concatenate([child_ids[:, 0], child_ids[:, 1]]) - anchor
    columns = jnp.arange(previous, dtype=jnp.int32)
    return (both_rows[:, None] == columns[None, :]).astype(jnp.float32)


def pick_rows(select, source):
    return jnp.einsum("kn,ans->aks", select, source, precision=lax.Precision.HIGHEST)


def decays_of(child_ids, length_row, rate_scale):
    left_decay = jnp.exp(-rate_scale * jnp.take(length_row, child_ids[:, 0]))
    right_decay = jnp.exp(-rate_scale * jnp.take(length_row, child_ids[:, 1]))
    return (left_decay, right_decay)


def tip_level(code_floats, child_ids, anchor, length_row, stationary, rate_scale):
    node_count = child_ids.shape[0]
    select = selector(child_ids, anchor, code_floats.shape[0])
    picked = jnp.dot(select, code_floats, precision=lax.Precision.HIGHEST)
    states = jnp.arange(4, dtype=jnp.float32)
    onehot = (picked[None, :, :] == states[:, None, None]).astype(jnp.float32)
    left_decay, right_decay = decays_of(child_ids, length_row, rate_scale)
    left_part = transit(onehot[:, :node_count], left_decay, stationary)
    right_part = transit(onehot[:, node_count:], right_decay, stationary)
    scale_sum = jnp.zeros((1, node_count, code_floats.shape[1]), jnp.float32)
    return join_pair(left_part, right_part, scale_sum)


def level_up(values, scales, child_ids, anchor, length_row, stationary, rate_scale):
    node_count = child_ids.shape[0]
    select = selector(child_ids, anchor, values.shape[1])
    picked_values = pick_rows(select, values)
    picked_scales = pick_rows(select, scales)
    left_decay, right_decay = decays_of(child_ids, length_row, rate_scale)
    left_part = transit(picked_values[:, :node_count], left_decay, stationary)
    right_part = transit(picked_values[:, node_count:], right_decay, stationary)
    scale_sum = picked_scales[:, :node_count] + picked_scales[:, node_count:]
    return join_pair(left_part, right_part, scale_sum)


def lower_tree(code_floats, children, length_row, stationary, group_index, groups, taxa_count):
    rate_scale = rate_of(stationary)
    values = None
    scales = None
    for tree_level in range(LEVELS - TOP):
        node_count = (taxa_count >> tree_level + 1) // groups
        first_row = taxa_count - (taxa_count >> tree_level) + group_index * node_count
        child_ids = lax.dynamic_slice_in_dim(children, first_row, node_count, 0)
        if tree_level == 0:
            anchor = group_index * code_floats.shape[0]
            values, scales = tip_level(
                code_floats, child_ids, anchor, length_row, stationary, rate_scale
            )
        else:
            anchor = (
                taxa_count
                + taxa_count
                - (taxa_count >> tree_level - 1)
                + group_index * ((taxa_count >> tree_level) // groups)
            )
            values, scales = level_up(
                values, scales, child_ids, anchor, length_row, stationary, rate_scale
            )
    return (values, scales)


def upper_tree(values, scales, children, length_row, stationary, taxa_count):
    rate_scale = rate_of(stationary)
    for tree_level in range(LEVELS - TOP, LEVELS):
        node_count = taxa_count >> tree_level + 1
        offset = taxa_count - (taxa_count >> tree_level)
        child_ids = children[offset : offset + node_count]
        anchor = taxa_count + taxa_count - (taxa_count >> tree_level - 1)
        values, scales = level_up(
            values, scales, child_ids, anchor, length_row, stationary, rate_scale
        )
    return scales[0, 0] + jnp.log(jnp.sum(stationary[:, None] * values[:, 0], axis=0))


def combine_parts(earlier, later_one):
    largest = jnp.maximum(earlier[0], later_one[0])
    mass = earlier[1] * jnp.exp(earlier[0] - largest) + later_one[1] * jnp.exp(
        later_one[0] - largest
    )
    return (largest, mass)


def per_device(tip_codes, counts, children, lengths, frequencies, weights):
    groups = lax.axis_size("cls")
    group_index = lax.axis_index("cls")
    taxa_count = tip_codes.shape[0] * groups
    site_count = tip_codes.shape[1]
    quarter = site_count // groups
    classes = lengths.shape[0]
    stationary = frequencies / jnp.sum(frequencies, axis=1, keepdims=True)
    log_weight = jnp.log(weights / jnp.sum(weights))
    code_floats = tip_codes.astype(jnp.float32)
    low_values = []
    low_scales = []
    for class_no in range(classes):
        part_values, part_scales = lower_tree(
            code_floats,
            children,
            lengths[class_no],
            stationary[class_no],
            group_index,
            groups,
            taxa_count,
        )
        low_values.append(part_values)
        low_scales.append(part_scales)
    stacked_values = jnp.stack(low_values)
    stacked_scales = jnp.stack(low_scales)
    pattern_weight = counts.astype(jnp.float32)
    clade_values, clade_scales = (
        lax.all_to_all(stacked_values, "cls", split_axis=0, concat_axis=2, tiled=True),
        lax.all_to_all(stacked_scales, "cls", split_axis=0, concat_axis=2, tiled=True),
    )
    own_lengths = lax.dynamic_index_in_dim(lengths, group_index, 0, keepdims=False)
    own_stationary = lax.dynamic_index_in_dim(stationary, group_index, 0, keepdims=False)
    class_ll = upper_tree(
        clade_values[0], clade_scales[0], children, own_lengths, own_stationary, taxa_count
    )
    shifted = class_ll + lax.dynamic_index_in_dim(log_weight, group_index, 0, keepdims=False)
    largest, mass = combined_all((shifted, jnp.ones_like(shifted)), "cls", combine_parts)
    site_total = largest + jnp.log(mass)
    posterior = jnp.exp(shifted - site_total)
    sum_loglik, class_mass, all_count = (
        one_axis_at_a_time(jnp.sum(pattern_weight * site_total), SITE),
        one_axis_at_a_time(jnp.sum(pattern_weight * posterior), SITE),
        one_axis_at_a_time(jnp.sum(pattern_weight), SITE),
    )
    new_weights = (class_mass / all_count).reshape(1)
    own_sites = lax.dynamic_slice_in_dim(site_total, group_index * quarter, quarter, 0)
    per_taxon = (own_sites / taxa_count).reshape(1, quarter)
    mean_loglik = sum_loglik / (all_count * taxa_count)
    return (per_taxon, new_weights, mean_loglik)


def solution(mesh):
    finer = Mesh(
        mesh.devices.reshape(mesh.shape["cls"], 4, 4, 2), ("cls", "site_0", "site_1", "site_2")
    )
    in_specs = (P("cls", SITE), P(SITE), P(), P(), P(), P())
    out_specs = (P("cls", SITE), P("cls"), P())
    return jax.shard_map(
        per_device, mesh=finer, in_specs=in_specs, out_specs=out_specs, check_vma=False
    )
```

profile of v0, /device:TPU:1, one launch (start us, length us, event | category | flops | bytes accessed | tf_op | source)
XLA Modules:
  0.0 169.3 jit_solution(9036038780284599451)
XLA Ops:
  0.7 0.8 constant_dynamic-slice_fusion.8
  1.5 0.8 constant_dynamic-slice_fusion.9
  2.3 1.0 constant_dynamic-slice_fusion.2
  3.3 1.1 gather_fusion
  4.5 1.1 gather_fusion.1
  5.6 1.1 gather_fusion.24
  6.8 1.1 gather_fusion.25
  7.9 1.1 gather_fusion.36
  9.1 1.1 gather_fusion.37
  10.5 0.7 multiply_reduce_fusion.58
  11.2 1.1 gather_fusion.13
  12.5 0.8 gather_fusion.3
  13.3 0.8 gather_fusion.15
  14.1 0.8 gather_fusion.2
  14.8 0.8 gather_fusion.26
  15.6 0.8 gather_fusion.27
  16.4 0.8 gather_fusion.38
  17.2 0.8 gather_fusion.39
  18.8 0.7 gather_fusion.17
  19.5 0.7 gather_fusion.4
  20.2 0.7 gather_fusion.28
  20.9 0.7 gather_fusion.29
  21.6 0.7 gather_fusion.40
  37.0 1.1 gather_fusion.12
  38.1 0.8 gather_fusion.14
  44.3 0.7 fusion.29
  45.6 1.4 multiply_reduce_fusion.7
  47.7 3.6 %fusion.346 = (f32[128,1024]{1,0:T(8,128)S(1)}, f32[4,128,1024]{2,1,0:T(8,128)S(1)}, f32[128,1024]{1,0:T(8,128)S(1)}, f32[4,128,1024]{2,1,0:T(8,128)}, f32[128,1024]{1,0:T(8,128)S(1)}, /*index=5*/f32[4,128,1024]{2,1,0:T(8,128)}) fusion(f32[128,1024]{1,0:T(8,128)S(1)} %broadcast_multiply_fusion.6, f32[4,256,1024]{2,1,0:T(8,128)S(1)} %fusion, ...), kind=kLoop, calls=%fused_computation.786 | loop fusion | flops 9043968 | bytes 15207424 | tf_op jit(solution)/shard_map/reduce_max | solution.py:53
  51.8 1.6 fusion.9
  54.7 0.7 convolution_bitcast_fusion.3
  59.0 3.0 %fusion.364 = (f32[128,1024]{1,0:T(8,128)S(1)}, f32[4,128,1024]{2,1,0:T(8,128)S(1)}) fusion(f32[128,1024]{1,0:T(8,128)S(1)} %broadcast_multiply_fusion.4, f32[4,256,1024]{2,1,0:T(8,128)} %copy-done, f32[128]{0:T(128)S(1)} %get-tuple-element.538, f32[128,1024]{1,0:T(8,128)S(1)} %broadcast_multiply_fusion.5, f32[128]{0:T(128)S(1)} %get-tuple-element.351), kind=kLoop, calls=%fused_computation.792 | loop fusion | flops 3014656 | bytes 7865344 | tf_op jit(solution)/shard_map/reduce_max | solution.py:53
  62.5 1.6 fusion.12
  65.4 0.7 convolution_bitcast_fusion.2
  69.8 1.8 %fusion.15 = f32[4,128,1024]{2,1,0:T(8,128)S(1)} fusion(f32[4,128,1024]{2,1,0:T(8,128)S(1)} %copy-done.2, f32[128,1024]{1,0:T(8,128)S(1)} %get-tuple-element.428, s32[128]{0:T(128)S(1)} %get-tuple-element.575), kind=kOutput, calls=%fused_computation.81 | convolution fusion | flops 805847040 | bytes 4719104 | tf_op jit(solution)/shard_map/kn,ans->aks/dot_general | solution.py:68
  72.9 0.7 convolution_bitcast_fusion.1
  77.3 1.6 fusion.18
  80.2 0.7 convolution_bitcast_fusion
  85.8 5.8 %all-to-all-start = ((f32[4,1,4,1024]{3,2,1,0:T(4,128)}), f32[4,1,4,1024]{3,2,1,0:T(4,128)S(1)}, u32[]{:S(2)}, u32[]{:S(2)}) async-start(f32[4,1,4,1024]{3,2,1,0:T(4,128)} %pad_maximum_fusion.1), calls=%async_computation | async-start | bytes 131072 | tf_op jit(solution)/shard_map/all_to_all | solution.py:178
  95.9 1.4 compare_select_fusion.1
  100.2 0.8 pad_maximum_fusion
  105.1 1.4 fusion.405
  108.3 4.2 %all-to-all-start.1 = ((f32[4,4,4,1024]{3,2,1,0:T(4,128)}), f32[4,4,4,1024]{3,2,1,0:T(4,128)S(1)}, u32[]{:S(2)}, u32[]{:S(2)}) async-start(f32[4,4,4,1024]{3,2,1,0:T(4,128)} %pad_maximum_fusion), calls=%async_computation.1 | async-start | bytes 524288 | tf_op jit(solution)/shard_map/all_to_all | solution.py:177
  112.9 5.2 %all-to-all-done.1 = f32[4,4,4,1024]{3,2,1,0:T(4,128)S(1)} async-done(((f32[4,4,4,1024]{3,2,1,0:T(4,128)}), f32[4,4,4,1024]{3,2,1,0:T(4,128)S(1)}, u32[]{:S(2)}, u32[]{:S(2)}) %all-to-all-start.1) | async-done | bytes 262176 | tf_op jit(solution)/shard_map/all_to_all | solution.py:177
  122.2 9.0 %all-gather.1 = f32[4,2,1024]{2,1,0:T(2,128)S(1)} all-gather(f32[1,2,1024]{2,1,0:T(2,128)S(1)} %pad_bitcast_fusion), channel_id=2, replica_groups=mesh['cls'=4,'site_0'=4,'site_1'=4,'site_2'=2] {'cls'}, dimensions={0}, use_global_device_ids=true | all-gather | bytes 40960 | tf_op jit(solution)/shard_map/all_gather | solution.py:22
  131.5 1.3 multiply_reduce_fusion.56
  132.8 9.1 %all-reduce.2 = (f32[]{:T(128)}, f32[]{:T(128)}, f32[]{:T(128)}) all-reduce(f32[]{:T(128)} %get-tuple-element.230, f32[]{:T(128)} %get-tuple-element.231, f32[]{:T(128)} %get-tuple-element.229), channel_id=1, replica_groups=mesh['cls'=4,'site_0'=4,'site_1'=4,'site_2'=2] {'site_0'}, use_global_device_ids=true, to_apply=%region_95.103 | all-reduce | flops 3 | bytes 24 | tf_op jit(solution)/shard_map/psum | solution.py:43
  141.9 9.3 %all-reduce.1 = (f32[]{:T(128)}, f32[]{:T(128)}, f32[]{:T(128)}) all-reduce(f32[]{:T(128)} %get-tuple-element.249, f32[]{:T(128)} %get-tuple-element.250, f32[]{:T(128)} %get-tuple-element.251), channel_id=1, replica_groups=mesh['cls'=4,'site_0'=4,'site_1'=4,'site_2'=2] {'site_1'}, use_global_device_ids=true, to_apply=%region_96.104 | all-reduce | flops 3 | bytes 24 | tf_op jit(solution)/shard_map/psum | solution.py:43
  151.3 12.4 %all-reduce.3 = (f32[]{:T(128)}, f32[]{:T(128)}, f32[]{:T(128)}) all-reduce(f32[]{:T(128)} %get-tuple-element.246, f32[]{:T(128)} %get-tuple-element.247, f32[]{:T(128)} %get-tuple-element.248), channel_id=1, replica_groups=mesh['cls'=4,'site_0'=4,'site_1'=4,'site_2'=2] {'site_2'}, use_global_device_ids=true, to_apply=%region_97.105 | all-reduce | flops 3 | bytes 24 | tf_op jit(solution)/shard_map/psum | solution.py:43
  (288 shorter events, 53.4 us)
Async XLA Ops:
  0.6 11.7 %copy-start.4 = (s32[1023,2]{0,1:T(2,128)S(1)}, s32[1023,2]{0,1:T(2,128)}, u32[]{:S(2)}) copy-start(s32[1023,2]{0,1:T(2,128)} %param.24) | copy-start | bytes 24556
  0.6 9.6 %copy-start.5 = (f32[4,4]{1,0:T(4,128)S(1)}, f32[4,4]{1,0:T(4,128)}, u32[]{:S(2)}) copy-start(f32[4,4]{1,0:T(4,128)} %param.26) | copy-start | bytes 196
  35.7 8.6 %copy-start.3 = (s32[256,1024]{1,0:T(8,128)S(1)}, s32[256,1024]{1,0:T(8,128)}, u32[]{:S(2)}) copy-start(s32[256,1024]{1,0:T(8,128)} %param.22) | copy-start | bytes 3145732
  45.6 2.1 %copy-start = (f32[4,256,1024]{2,1,0:T(8,128)}, f32[4,256,1024]{2,1,0:T(8,128)S(1)}, u32[]{:S(2)}) copy-start(f32[4,256,1024]{2,1,0:T(8,128)S(1)} %fusion) | copy-start | bytes 12582916
  67.8 2.0 %copy-start.2 = (f32[4,128,1024]{2,1,0:T(8,128)S(1)}, f32[4,128,1024]{2,1,0:T(8,128)}, u32[]{:S(2)}) copy-start(f32[4,128,1024]{2,1,0:T(8,128)} %get-tuple-element.429) | copy-start | bytes 6291460
  75.3 2.0 %copy-start.1 = (f32[4,128,1024]{2,1,0:T(8,128)S(1)}, f32[4,128,1024]{2,1,0:T(8,128)}, u32[]{:S(2)}) copy-start(f32[4,128,1024]{2,1,0:T(8,128)} %get-tuple-element.431) | copy-start | bytes 6291460
  85.2 13.5 %copy-start.7 = (f32[4]{0:T(128)S(1)}, f32[4]{0:T(128)}, u32[]{:S(2)}) copy-start(f32[4]{0:T(128)} %param.27) | copy-start | bytes 52
  85.8 22.5 %all-to-all-start = ((f32[4,1,4,1024]{3,2,1,0:T(4,128)}), f32[4,1,4,1024]{3,2,1,0:T(4,128)S(1)}, u32[]{:S(2)}, u32[]{:S(2)}) async-start(f32[4,1,4,1024]{3,2,1,0:T(4,128)} %pad_maximum_fusion.1), calls=%async_computation | async-start | bytes 131072 | tf_op jit(solution)/shard_map/all_to_all | solution.py:178
  108.3 9.8 %all-to-all-start.1 = ((f32[4,4,4,1024]{3,2,1,0:T(4,128)}), f32[4,4,4,1024]{3,2,1,0:T(4,128)S(1)}, u32[]{:S(2)}, u32[]{:S(2)}) async-start(f32[4,4,4,1024]{3,2,1,0:T(4,128)} %pad_maximum_fusion), calls=%async_computation.1 | async-start | bytes 524288 | tf_op jit(solution)/shard_map/all_to_all | solution.py:177
  118.7 12.8 %copy-start.6 = (s32[1024]{0:T(1024)S(1)}, s32[1024]{0:T(1024)}, u32[]{:S(2)}) copy-start(s32[1024]{0:T(1024)} %param.23) | copy-start | bytes 12292
where the time goes:
time: 170 us; the launch traced here: 169 us
  local copies, waits for them, and re-layouts  46.3 us (27%)
  blocking collectives  39.9 us (23%)
  other arithmetic  30 us (18%)
  matrix products  22.2 us (13%)
  between operations  15.5 us (9%)
  starting transfers between devices  10.1 us (6%)
  waiting for transfers between devices  5.2 us (3%)
    psum x3, blocking collectives, one_axis_at_a_time(): return functools.reduce(lax.psum, axes, array)  30.8 us
    gather x28, local copies, waits for them, and re-layouts, decays_of(): left_decay = jnp.exp(-rate_scale * jnp.take(length_row, child_ids[:, 0]))  21.5 us
    dot_general x48, matrix products, pick_rows(): jnp.einsum('kn,ans->aks', select, source, precision=lax.Precision.HIGHEST)  21.4 us
    gather x27, local copies, waits for them, and re-layouts, decays_of(): right_decay = jnp.exp(-rate_scale * jnp.take(length_row, child_ids[:, 1]))  20.1 us
    reduce_max x26, other arithmetic, join_pair(): largest = jnp.max(parent, axis=0, keepdims=True)  11.1 us
    all_gather x1, blocking collectives, all_in_one(): both, at, found = (lax.all_gather(jnp.concatenate(lines), axis), 0, {})  9.04 us
    all_to_all x1, starting transfers between devices, per_device(): lax.all_to_all(stacked_scales, 'cls', split_axis=0, concat_axis=2, tiled=...  5.84 us
    all_to_all x1, waiting for transfers between devices, per_device(): lax.all_to_all(stacked_values, 'cls', split_axis=0, concat_axis=2, tiled=...  5.2 us
  transfers between devices with their start and end apart: 2, of which 1 were waited for; matrix products, arithmetic and copies ran while one was open for 6% of the time, Pallas kernels for 0%

commit v1 on v0

v1 whole, which is shorter than its diff:
```python
import jax
import jax.numpy as jnp
from jax import lax
from jax.experimental import pallas as pl
from jax.experimental.pallas import tpu as pltpu
from jax.sharding import PartitionSpec as P

CLS = 4
STATES = 4
PAD = 2048
SMEM = pltpu.MemorySpace.SMEM
VMEM = pltpu.MemorySpace.VMEM


def mean_state(pi, values):
    return (pi[0] * values[0] + pi[1] * values[1]) + (pi[2] * values[2] + pi[3] * values[3])


def moved(values, rate, average):
    step = rate * average
    return [value + step for value in values]


def product(left, right):
    return [a * b for a, b in zip(left, right)]


def lower_kernel(group_ref, child_ref, rate_ref, pi_ref, codes_ref, out_ref, mid_ref, log_ref):
    group = group_ref[0]
    pis = [[pi_ref[4 * c + i] for i in range(STATES)] for c in range(CLS)]

    def pair_of(row):
        return child_ref[2 * row], child_ref[2 * row + 1]

    def tip_codes(tip):
        local = tip - group * 256
        start = lax.shift_left(lax.shift_right_logical(local, 3), 6) + lax.bitwise_and(local, 7)
        return codes_ref[pl.ds(start, 8, stride=8), :]

    def tip_part(code, c, rate):
        pi = pis[c]
        odd = lax.bitwise_and(code, 1) == 1
        high = code >= 2
        freq = jnp.where(high, jnp.where(odd, pi[3], pi[2]), jnp.where(odd, pi[1], pi[0]))
        step = rate * freq
        own = step + 1.0
        return [jnp.where(code == i, own, step) for i in range(STATES)]

    def small_tree(n, _):
        row = 768 + group * 32 + n
        tops = pair_of(row)
        pairs = [pair for top in tops for pair in pair_of(top - 1024)]
        tips = [tip for pair in pairs for tip in pair_of(pair - 1024)]
        codes = [tip_codes(tip) for tip in tips]
        for c in range(CLS):
            pi = pis[c]

            def rate(node):
                return rate_ref[PAD * c + node]

            halves = []
            for h in range(2):
                quads = []
                for p in range(2):
                    at = 2 * h + p
                    joined = product(
                        tip_part(codes[2 * at], c, rate(tips[2 * at])),
                        tip_part(codes[2 * at + 1], c, rate(tips[2 * at + 1])),
                    )
                    quads.append(moved(joined, rate(pairs[at]), mean_state(pi, joined)))
                joined = product(quads[0], quads[1])
                halves.append(moved(joined, rate(tops[h]), mean_state(pi, joined)))
            joined = product(halves[0], halves[1])
            average = mean_state(pi, joined)
            inverse = 1.0 / average
            own_rate = rate(1024 + row)
            for i in range(STATES):
                mid_ref[n, c, i] = joined[i] * inverse + own_rate
            log_ref[n, c] = jnp.log(average)
        return 0

    lax.fori_loop(0, 32, small_tree, 0)

    def clade(j, _):
        root = 992 + group * 4 + j
        tops = pair_of(root)
        pairs = [pair for top in tops for pair in pair_of(top - 1024)]
        leaves = [leaf - 1792 - group * 32 for pair in pairs for leaf in pair_of(pair - 1024)]
        for c in range(CLS):
            pi = pis[c]

            def rate(node):
                return rate_ref[PAD * c + node]

            scale = log_ref[leaves[0], c]
            for leaf in leaves[1:]:
                scale = scale + log_ref[leaf, c]
            halves = []
            for h in range(2):
                quads = []
                for p in range(2):
                    at = 2 * h + p
                    joined = [
                        mid_ref[leaves[2 * at], c, i] * mid_ref[leaves[2 * at + 1], c, i]
                        for i in range(STATES)
                    ]
                    quads.append(moved(joined, rate(pairs[at]), mean_state(pi, joined)))
                joined = product(quads[0], quads[1])
                halves.append(moved(joined, rate(tops[h]), mean_state(pi, joined)))
            joined = product(halves[0], halves[1])
            inverse = 1.0 / joined[3]
            sent = [joined[0] * inverse, joined[1] * inverse, joined[2] * inverse]
            sent.append(scale + jnp.log(joined[3]))
            for v in range(4):
                for q in range(4):
                    out_ref[q, j, v, 2 * c : 2 * c + 2, :] = sent[v][2 * q : 2 * q + 2, :]
        return 0

    lax.fori_loop(0, 4, clade, 0)


def upper_kernel(
    group_ref, child_ref, clade_ref, rate_ref, pi_ref, const_ref, count_ref, site_ref, part_ref, node_ref
):
    pi = [pi_ref[i] for i in range(STATES)]
    scale = const_ref[...]
    for k in range(16):
        values = [clade_ref[k, 0], clade_ref[k, 1], clade_ref[k, 2]]
        scale = scale + clade_ref[k, 3]
        average = (pi[0] * values[0] + pi[1] * values[1]) + (pi[2] * values[2] + pi[3])
        step = rate_ref[k] * average
        for i in range(3):
            node_ref[k, i] = values[i] + step
        node_ref[k, 3] = step + 1.0
    at = 16
    for level, count in ((6, 8), (7, 4), (8, 2), (9, 1)):
        first = 1024 - (1024 >> level)
        for k in range(count):
            left = child_ref[2 * (first + k)] - 2016
            right = child_ref[2 * (first + k) + 1] - 2016
            joined = [node_ref[left, i] * node_ref[right, i] for i in range(STATES)]
            average = mean_state(pi, joined)
            if level == 6:
                scale = scale + jnp.log(average)
                inverse = 1.0 / average
                for i in range(STATES):
                    node_ref[at, i] = joined[i] * inverse + rate_ref[at]
            elif level < 9:
                step = rate_ref[at] * average
                for i in range(STATES):
                    node_ref[at, i] = joined[i] + step
            else:
                scale = scale + jnp.log(average)
            at += 1
    top = jnp.maximum(scale, pltpu.roll(scale, 2, 0))
    top = jnp.maximum(top, pltpu.roll(top, 4, 0))
    share = jnp.exp(scale - top)
    mass = share + pltpu.roll(share, 2, 0)
    mass = mass + pltpu.roll(mass, 4, 0)
    total = top + jnp.log(mass)
    site_ref[...] = total[0:2] * (1.0 / 1024.0)
    quarter = count_ref[pl.ds(2 * group_ref[0], 2), :].astype(jnp.float32)
    weight = jnp.concatenate([quarter, quarter, quarter, quarter], axis=0)
    classes = weight * (share / mass)
    row = lax.broadcasted_iota(jnp.int32, (8, 128), 0)
    column = lax.broadcasted_iota(jnp.int32, (1, 128), 1)
    sums = [jnp.sum(jnp.where(lax.shift_right_logical(row, 1) == c, classes, 0.0), keepdims=True) for c in range(CLS)]
    sums.append(jnp.sum(jnp.where(row < 2, weight * total, 0.0), keepdims=True))
    sums.append(jnp.sum(jnp.where(row < 2, weight, 0.0), keepdims=True))
    line = jnp.zeros((1, 128), jnp.float32)
    for k, value in enumerate(sums):
        line = jnp.where(column == k, value, line)
    part_ref[...] = line


def per_device(tip_codes, counts, children, lengths, frequencies, weights):
    group = lax.axis_index("cls").astype(jnp.int32)
    group_line = group.reshape(1)
    stationary = frequencies / jnp.sum(frequencies, axis=1, keepdims=True)
    beta = 1.0 / (1.0 - jnp.sum(stationary * stationary, axis=1))
    rates = jnp.exp(beta[:, None] * lengths) - 1.0
    log_weight = jnp.log(weights / jnp.sum(weights))
    const = log_weight - beta * jnp.sum(lengths, axis=1)
    child_line = children.reshape(-1)
    rate_line = jnp.pad(rates, ((0, 0), (0, PAD - rates.shape[1]))).reshape(-1)
    codes = tip_codes.reshape(32, 8, 8, 128).transpose(0, 2, 1, 3).reshape(2048, 128)

    smem = pl.BlockSpec(memory_space=SMEM)
    vmem = pl.BlockSpec(memory_space=VMEM)
    ours = pl.pallas_call(
        lower_kernel,
        out_shape=jax.ShapeDtypeStruct((4, 4, 4, 8, 128), jnp.float32),
        in_specs=[smem, smem, smem, smem, vmem],
        out_specs=vmem,
        scratch_shapes=[
            pltpu.VMEM((32, CLS, STATES, 8, 128), jnp.float32),
            pltpu.VMEM((32, CLS, 8, 128), jnp.float32),
        ],
        name="lower_tree",
    )(group_line, child_line, rate_line, stationary.reshape(-1), codes)
    clades = lax.all_to_all(ours, "cls", split_axis=0, concat_axis=0, tiled=True)

    def spread(by_class):
        return jnp.broadcast_to(by_class[..., :, None, None], (*by_class.shape, 2, 128)).reshape(
            *by_class.shape[:-1], 8, 128
        )

    top_rates = spread(jnp.pad(rates[:, 2016:], ((0, 0), (0, 2))).T)
    site, part = pl.pallas_call(
        upper_kernel,
        out_shape=(
            jax.ShapeDtypeStruct((2, 128), jnp.float32),
            jax.ShapeDtypeStruct((1, 128), jnp.float32),
        ),
        in_specs=[smem, smem, vmem, vmem, vmem, vmem, vmem],
        out_specs=(vmem, vmem),
        scratch_shapes=[pltpu.VMEM((32, STATES, 8, 128), jnp.float32)],
        name="upper_tree",
    )(
        group_line,
        child_line,
        clades.reshape(16, 4, 8, 128),
        top_rates,
        spread(stationary.T),
        spread(const),
        counts.reshape(8, 128),
    )
    every = lax.all_to_all(
        jnp.broadcast_to(part, (128, 128)), ("cls", "site"), split_axis=0, concat_axis=0, tiled=True
    )
    sums = jnp.sum(every, axis=0)
    own = lax.dynamic_slice_in_dim(sums, group, 1, 0)
    return site.reshape(1, 256), own / sums[5], sums[4] / (sums[5] * 1024.0)


def solution(mesh):
    return jax.shard_map(
        per_device,
        mesh=mesh,
        in_specs=(P("cls", "site"), P("site"), P(), P(), P(), P()),
        out_specs=(P("cls", "site"), P("cls"), P()),
        check_vma=False,
    )
```

time: 170 us -> 55.5 us (0.33)
  blocking collectives: 39.9 us -> 0 us
  local copies, waits for them, and re-layouts: 46.3 us -> 7.97 us
  other arithmetic: 30 us -> 1.82 us
  matrix products: 22.2 us -> 0 us
  Pallas kernels: 0 us -> 9.86 us
  between operations: 15.5 us -> 5.67 us
  waiting for transfers between devices: 5.2 us -> 14.8 us
  starting transfers between devices: 10.1 us -> 15 us
    gather x55 -> x0, local copies, waits for them, and re-layouts: 41.6 us -> none  [the longest x28 21.5 us: decays_of(): left_decay = jnp.exp(-rate_scale * jnp.take(length_row, child_ids[:, 0]))]
    psum x3 -> x0, blocking collectives: 30.8 us -> none  [one_axis_at_a_time(): return functools.reduce(lax.psum, axes, array)]
    dot_general x49 -> x0, matrix products: 22.2 us -> none  [the longest x48 21.4 us: pick_rows(): jnp.einsum('kn,ans->aks', select, source, precision=lax.Precision.HIGHEST)]
    reduce_max x26 -> x0, other arithmetic: 11.1 us -> none  [join_pair(): largest = jnp.max(parent, axis=0, keepdims=True)]
    pallas_call x0 -> x2, Pallas kernels: none -> 9.86 us  [the longest x1 7.92 us: per_device(): pl.pallas_call(lower_kernel, out_shape=jax.ShapeDtypeStruct((4, 4, 4, 8,...]
    all_to_all x2, waiting for transfers between devices: 5.2 us -> 14.8 us  [the longest x1 9.64 us: per_device(): lax.all_to_all(jnp.broadcast_to(part, (128, 128)), ('cls', 'site'), split...]
    all_gather x1 -> x0, blocking collectives: 9.04 us -> none  [all_in_one(): both, at, found = (lax.all_gather(jnp.concatenate(lines), axis), 0, {})]
    reduce_sum x28 -> x3, other arithmetic: 6.95 us -> 0.35 us  [the longest x1 0.19 us: per_device(): beta = 1.0 / (1.0 - jnp.sum(stationary * stationary, axis=1))]
  transfers between devices with their start and end apart: 2 -> 2, of which waited for: 1 -> 2; matrix products, arithmetic and copies ran while one was open for 6% -> 1% of each run, Pallas kernels for 0% -> 0%
where the time goes in v1:
time: 55.5 us; the launch traced here: 55.1 us
  starting transfers between devices  15 us (27%)
  waiting for transfers between devices  14.8 us (27%)
  Pallas kernels  9.86 us (18%)
  local copies, waits for them, and re-layouts  7.97 us (14%)
  between operations  5.67 us (10%)
  other arithmetic  1.82 us (3%)
    all_to_all x1, waiting for transfers between devices, per_device(): lax.all_to_all(jnp.broadcast_to(part, (128, 128)), ('cls', 'site'), split...  9.64 us
    all_to_all x1, starting transfers between devices, per_device(): lax.all_to_all(jnp.broadcast_to(part, (128, 128)), ('cls', 'site'), split...  9.2 us
    pallas_call x1, Pallas kernels, per_device(): pl.pallas_call(lower_kernel, out_shape=jax.ShapeDtypeStruct((4, 4, 4, 8,...  7.92 us
    all_to_all x1, starting transfers between devices, per_device(): lax.all_to_all(ours, 'cls', split_axis=0, concat_axis=0, tiled=True)  5.84 us
    all_to_all x1, waiting for transfers between devices, per_device(): lax.all_to_all(ours, 'cls', split_axis=0, concat_axis=0, tiled=True)  5.15 us
    unnamed x13, local copies, waits for them, and re-layouts  2.71 us
    broadcast_in_dim x9, local copies, waits for them, and re-layouts, spread(): jnp.broadcast_to(by_class[..., :, None, None], (*by_class.shape, 2, 128))  2.41 us
    pallas_call x1, Pallas kernels, per_device(): pl.pallas_call(upper_kernel, out_shape=(jax.ShapeDtypeStruct((2, 128), jn...  1.94 us
  transfers between devices with their start and end apart: 2, of which 2 were waited for; matrix products, arithmetic and copies ran while one was open for 1% of the time, Pallas kernels for 0%

profile of v1, /device:TPU:1, one launch (start us, length us, event | category | flops | bytes accessed | tf_op | source)
XLA Modules:
  0.0 55.1 jit_solution(14858140762812633694)
XLA Ops:
  0.6 0.9 %copy.17 = s32[1023,2]{1,0:T(8,128)S(1)} copy(s32[1023,2]{0,1:T(2,128)} %param.8) | data formatting | bytes 16368 | tf_op args[2]
  1.6 0.0 copy-start.1
  1.6 0.9 %reshape.57.child_ref = s32[2046]{0:T(1024)} reshape(s32[1023,2]{1,0:T(8,128)S(1)} %copy.17) | data formatting | bytes 16368 | tf_op jit(solution)/shard_map/reshape | solution.py:184
  2.4 0.0 copy-done.1
  2.4 0.0 copy-start.4
  2.4 0.0 copy-start.2
  2.4 0.1 reduce_sum.48
  2.6 0.5 copy-done.4
  3.1 0.6 %reduce_sum.47 = f32[]{:T(128)} reduce(f32[4]{0:T(128)S(1)} %copy-done.4, f32[]{:T(128)} %constant.16.clone.1), dimensions={0}, to_apply=%region_2.0 | reduce | flops 3 | bytes 24 | tf_op jit(solution)/shard_map/reduce_sum | solution.py:182
  3.7 0.0 copy-done.2
  3.7 0.1 reduce_sum.45
  3.8 0.2 multiply_reduce_fusion
  4.0 0.7 %multiply_subtract_fusion = (f32[4]{0:T(128)S(1)}, f32[4]{0:T(128)S(1)}) fusion(f32[4]{0:T(128)S(1)} %reduce_sum.48, f32[4]{0:T(128)S(1)} %copy-done.4, f32[]{:T(128)} %reduce_sum.47, f32[4]{0:T(128)S(1)} %get-tuple-element.9), kind=kLoop, calls=%fused_computation.5 | loop fusion | flops 20 | bytes 84 | tf_op jit(solution)/shard_map/sub | solution.py:183
  4.7 0.1 exponential_add_fusion
  4.8 0.6 %copy.21 = f32[1,16,4,128]{3,1,2,0:T(8,128)} copy(f32[1,16,4,128]{3,2,1,0:T(4,128)S(1)} %pad_bitcast_fusion) | data formatting | bytes 65536
  5.4 0.6 %reshape.59.pi_ref = f32[16]{0:T(128)} reshape(f32[4,4]{1,0:T(4,128)S(1)} %get-tuple-element.10) | data formatting | bytes 128 | tf_op jit(solution)/shard_map/reshape | solution.py:200
  6.0 7.9 %lower_tree.1 = f32[4,4,4,8,128]{4,3,2,1,0:T(8,128)} custom-call(s32[1]{0:T(128)} %bitcast.group_ref, s32[2046]{0:T(1024)} %reshape.57.child_ref, f32[8192]{0:T(1024)} %bitcast.23, f32[16]{0:T(128)} %reshape.59.pi_ref, s32[2048,128]{1,0:T(8,128)} %bitcast.20), custom_call_target="tpu_custom_call" | custom-call | tf_op jit(solution)/shard_map/lower_tree/pallas_call | solution.py:190
  13.9 5.8 %all-to-all-start = ((f32[4,4,4,8,128]{4,3,2,1,0:T(8,128)}), f32[4,4,4,8,128]{4,3,2,1,0:T(8,128)S(1)}, u32[]{:S(2)}, u32[]{:S(2)}) async-start(f32[4,4,4,8,128]{4,3,2,1,0:T(8,128)} %lower_tree.1), calls=%async_computation | async-start | bytes 524288 | tf_op jit(solution)/shard_map/all_to_all | solution.py:201
  19.7 0.1 slice.13
  19.8 0.1 copy.18
  19.9 0.1 copy.19
  20.0 0.1 broadcast_in_dim.43
  20.0 0.1 broadcast_in_dim.44
  20.1 5.1 %all-to-all-done = f32[4,4,4,8,128]{4,3,2,1,0:T(8,128)S(1)} async-done(((f32[4,4,4,8,128]{4,3,2,1,0:T(8,128)}), f32[4,4,4,8,128]{4,3,2,1,0:T(8,128)S(1)}, u32[]{:S(2)}, u32[]{:S(2)}) %all-to-all-start) | async-done | bytes 262176 | tf_op jit(solution)/shard_map/all_to_all | solution.py:201
  25.3 0.0 copy-start
  25.3 0.8 %broadcast_in_dim.39.rate_ref = f32[32,8,128]{2,1,0:T(8,128)} broadcast(f32[32,8]{1,0:T(8,128)S(1)} %copy.18), dimensions={0,1} | broadcast | bytes 132096 | tf_op jit(solution)/shard_map/broadcast_in_dim | solution.py:204
  26.0 0.7 %broadcast_in_dim.42.pi_ref = f32[4,8,128]{2,1,0:T(8,128)} broadcast(f32[4,8]{1,0:T(4,128)S(1)} %copy.19), dimensions={0,1} | broadcast | bytes 16512 | tf_op jit(solution)/shard_map/broadcast_in_dim | solution.py:204
  26.7 0.7 %broadcast_in_dim.45.const_ref = f32[8,128]{1,0:T(8,128)} broadcast(f32[8]{0:T(128)S(1)} %broadcast_in_dim.44), dimensions={0} | broadcast | bytes 4128 | tf_op jit(solution)/shard_map/broadcast_in_dim | solution.py:204
  27.4 0.0 copy-done
  27.4 1.9 %upper_tree.1 = (f32[2,128]{1,0:T(2,128)}, f32[1,128]{1,0:T(1,128)}) custom-call(s32[1]{0:T(128)} %bitcast.group_ref, s32[2046]{0:T(1024)} %reshape.57.child_ref, f32[16,4,8,128]{3,2,1,0:T(8,128)} %bitcast.21, f32[32,8,128]{2,1,0:T(8,128)} %broadcast_in_dim.39.rate_ref, f32[4,8,128]{2,1,0:T(8,128)} %broadcast_in_dim.42.pi_ref, ...), custom_call_target="tpu_custom_call" | custom-call | tf_op jit(solution)/shard_map/upper_tree/pallas_call | solution.py:209
  29.3 0.0 copy-start.3
  29.3 0.7 %copy-done.3 = f32[1,128]{1,0:T(1,128)S(1)} copy-done((f32[1,128]{1,0:T(1,128)S(1)}, f32[1,128]{1,0:T(1,128)}, u32[]{:S(2)}) %copy-start.3) | copy-done | bytes 536
  30.0 0.7 %broadcast_in_dim.46 = f32[128,1,128]{2,1,0:T(1,128)} broadcast(f32[128]{0:T(128)S(1)} %bitcast.28), dimensions={2} | broadcast | bytes 66048 | tf_op jit(solution)/shard_map/broadcast_in_dim | solution.py:229
  30.6 9.2 %all-to-all-start.1 = ((f32[128,1,128]{2,1,0:T(1,128)}), f32[128,1,128]{2,1,0:T(1,128)S(1)}, u32[]{:S(2)}, u32[]{:S(2)}) async-start(f32[128,1,128]{2,1,0:T(1,128)} %broadcast_in_dim.46), calls=%async_computation.1 | async-start | bytes 131072 | tf_op jit(solution)/shard_map/all_to_all | solution.py:228
  39.8 9.6 %all-to-all-done.1 = f32[128,1,128]{2,1,0:T(1,128)S(1)} async-done(((f32[128,1,128]{2,1,0:T(1,128)}), f32[128,1,128]{2,1,0:T(1,128)S(1)}, u32[]{:S(2)}, u32[]{:S(2)}) %all-to-all-start.1) | async-done | bytes 65568 | tf_op jit(solution)/shard_map/all_to_all | solution.py:228
  49.5 0.7 %fusion = (f32[1]{0:T(128)}, f32[1]{0:T(128)}, f32[1]{0:T(128)}) fusion(f32[128]{0:T(128)S(1)} %reduce_sum.49, s32[]{:T(128)S(6)} %select_n.3), kind=kLoop, calls=%fused_computation.7 | loop fusion | bytes 28 | tf_op jit(solution)/shard_map/slice | solution.py:233
  (5 shorter events, 0.1 us)
Async XLA Ops:
  1.6 0.9 %copy-start.1 = (f32[4,2046]{1,0:T(4,128)S(1)}, f32[4,2046]{1,0:T(4,128)}, u32[]{:S(2)}) copy-start(f32[4,2046]{1,0:T(4,128)} %param.9) | copy-start | bytes 98212
  2.4 0.7 %copy-start.4 = (f32[4]{0:T(128)S(1)}, f32[4]{0:T(128)}, u32[]{:S(2)}) copy-start(f32[4]{0:T(128)} %param.11) | copy-start | bytes 52
  2.4 1.3 %copy-start.2 = (f32[4,4]{1,0:T(4,128)S(1)}, f32[4,4]{1,0:T(4,128)}, u32[]{:S(2)}) copy-start(f32[4,4]{1,0:T(4,128)} %param.10) | copy-start | bytes 196
  13.9 11.4 %all-to-all-start = ((f32[4,4,4,8,128]{4,3,2,1,0:T(8,128)}), f32[4,4,4,8,128]{4,3,2,1,0:T(8,128)S(1)}, u32[]{:S(2)}, u32[]{:S(2)}) async-start(f32[4,4,4,8,128]{4,3,2,1,0:T(8,128)} %lower_tree.1), calls=%async_computation | async-start | bytes 524288 | tf_op jit(solution)/shard_map/all_to_all | solution.py:201
  25.3 2.1 %copy-start = (f32[4,4,4,8,128]{4,3,2,1,0:T(8,128)}, f32[4,4,4,8,128]{4,3,2,1,0:T(8,128)S(1)}, u32[]{:S(2)}) copy-start(f32[4,4,4,8,128]{4,3,2,1,0:T(8,128)S(1)} %all-to-all-done) | copy-start | bytes 786436
  29.3 0.7 %copy-start.3 = (f32[1,128]{1,0:T(1,128)S(1)}, f32[1,128]{1,0:T(1,128)}, u32[]{:S(2)}) copy-start(f32[1,128]{1,0:T(1,128)} %get-tuple-element.6) | copy-start | bytes 1540
  30.6 18.8 %all-to-all-start.1 = ((f32[128,1,128]{2,1,0:T(1,128)}), f32[128,1,128]{2,1,0:T(1,128)S(1)}, u32[]{:S(2)}, u32[]{:S(2)}) async-start(f32[128,1,128]{2,1,0:T(1,128)} %broadcast_in_dim.46), calls=%async_computation.1 | async-start | bytes 131072 | tf_op jit(solution)/shard_map/all_to_all | solution.py:228

commit v2 on v1

v2 whole, which is shorter than its diff:
```python
import jax
import jax.numpy as jnp
from jax import lax
from jax.experimental import pallas as pl
from jax.experimental.pallas import tpu as pltpu
from jax.sharding import PartitionSpec as P

CLS = 4
STATES = 4
FLOAT = jnp.float32
SMEM = pltpu.MemorySpace.SMEM
VMEM = pltpu.MemorySpace.VMEM
TILE = (8, 128)
TOP_RATES, TOP_PI, TOP_CONST, TOP_WEIGHT, TOP_ROWS = 0, 30, 34, 35, 36


def mean_state(pi, values):
    return (pi[0] * values[0] + pi[1] * values[1]) + (pi[2] * values[2] + pi[3] * values[3])


def moved(values, rate, average):
    step = rate * average
    return [value + step for value in values]


def product(left, right):
    return [a * b for a, b in zip(left, right)]


def choose(selector, options):
    value = jnp.where(selector == 1, options[1], options[0])
    value = jnp.where(selector == 2, options[2], value)
    return jnp.where(selector == 3, options[3], value)


def lower_kernel(
    child_ref, freq_ref, weight_ref, lengths_ref, codes_hbm, counts_hbm,
    out_ref, top_ref,
    codes_ref, counts_ref, rate_vec, rate_ref, pi_ref, pattern_ref, mid_ref, log_ref, sems,
):
    group = lax.axis_index("cls")
    loads = [
        pltpu.make_async_copy(
            codes_hbm.at[pl.ds(512 * j, 512)], codes_ref.at[pl.ds(512 * j, 512)], sems.at[j]
        )
        for j in range(4)
    ]
    for load in loads:
        load.start()
    count_load = pltpu.make_async_copy(counts_hbm, counts_ref, sems.at[5])
    count_load.start()

    lane = lax.broadcasted_iota(jnp.int32, TILE, 1)
    sub = lax.broadcasted_iota(jnp.int32, TILE, 0)
    by_pair = lax.shift_right_logical(sub, 1)
    uniform, betas = [], []
    for c in range(CLS):
        raw = [jnp.full(TILE, freq_ref[c, i], FLOAT) for i in range(STATES)]
        inverse = 1.0 / ((raw[0] + raw[1]) + (raw[2] + raw[3]))
        uniform.append([value * inverse for value in raw])
        betas.append(1.0 / (1.0 - mean_state(uniform[c], uniform[c])))
    beta_rows = choose(lax.bitwise_and(sub, 3), betas)[:4]
    total = jnp.zeros((4, 128), FLOAT)
    for k in range(16):
        width = min(128, 2046 - 128 * k)
        part = lengths_ref[:, 128 * k : 128 * k + width]
        if width < 128:
            part = jnp.concatenate([part, jnp.zeros((4, 128 - width), FLOAT)], axis=1)
        total = total + part
        rate_vec[:, 128 * k : 128 * k + 128] = jnp.exp(beta_rows * part) - 1.0
    rate_load = pltpu.make_async_copy(rate_vec, rate_ref, sems.at[4])
    rate_load.start()

    own_state = lax.bitwise_and(lax.shift_right_logical(lane, 4), 3)
    left_code = lax.bitwise_and(lax.shift_right_logical(lane, 2), 3)
    right_code = lax.bitwise_and(lane, 3)
    left_own = own_state == left_code
    right_own = own_state == right_code
    first = lane < 64
    both_own = jnp.where(left_own, jnp.where(right_own, 1.0, 0.0), 0.0)
    for c in range(CLS):
        left_pi = choose(left_code, uniform[c])
        right_pi = choose(right_code, uniform[c])
        pattern_ref[c, 0] = jnp.where(left_own, right_pi, 0.0)
        pattern_ref[c, 1] = jnp.where(right_own, left_pi, 0.0)
        pattern_ref[c, 2] = left_pi * right_pi
        pattern_ref[c, 3] = jnp.where(left_code == right_code, left_pi, 0.0)
        for i in range(STATES):
            pi_ref[c, i] = uniform[c][i]

    for i in range(STATES):
        top_ref[TOP_PI + i] = choose(by_pair, [uniform[c][i] for c in range(CLS)])
    beta_pairs = choose(by_pair, betas)
    sums = choose(by_pair, [jnp.broadcast_to(total[c : c + 1], TILE) for c in range(CLS)])
    sums = jnp.broadcast_to(jnp.sum(sums, axis=1, keepdims=True), TILE)
    weights = [jnp.full(TILE, weight_ref[c], FLOAT) for c in range(CLS)]
    weight_sum = (weights[0] + weights[1]) + (weights[2] + weights[3])
    top_ref[TOP_CONST] = jnp.log(choose(by_pair, weights) / weight_sum) - beta_pairs * sums
    last = lengths_ref[:, 1920:2046]
    last = jnp.concatenate([last, jnp.zeros((4, 2), FLOAT)], axis=1)
    last = choose(by_pair, [jnp.broadcast_to(last[c : c + 1], TILE) for c in range(CLS)])
    last = jnp.exp(beta_pairs * last) - 1.0
    for k in range(30):
        top_ref[TOP_RATES + k] = jnp.broadcast_to(last[:, 96 + k : 97 + k], TILE)
    count_load.wait()
    quarter = counts_ref[pl.ds(2 * group, 2), :].astype(FLOAT)
    top_ref[TOP_WEIGHT] = jnp.concatenate([quarter, quarter, quarter, quarter], axis=0)
    rate_load.wait()

    def pair_of(row):
        return child_ref[0, row], child_ref[1, row]

    def tip_codes(tip):
        local = tip - group * 256
        start = lax.shift_left(lax.shift_right_logical(local, 3), 6) + lax.bitwise_and(local, 7)
        return codes_ref[pl.ds(start, 8, stride=8), :]

    def small_tree(n, _):
        row = 768 + group * 32 + n
        tops = pair_of(row)
        pairs = [pair for top in tops for pair in pair_of(top - 1024)]
        tips = [pair_of(pair - 1024) for pair in pairs]
        places = []
        for at in range(4):
            code = lax.shift_left(tip_codes(tips[at][0]), 2) + tip_codes(tips[at][1])
            places.append([code + (64 * (at % 2) + 16 * i) for i in range(STATES)])
        for c in range(CLS):
            pi = [pi_ref[c, i] for i in range(STATES)]
            halves = []
            for h in range(2):
                factors = []
                for at in (2 * h, 2 * h + 1):
                    left = rate_ref[c, tips[at][0]]
                    right = rate_ref[c, tips[at][1]]
                    own = rate_ref[c, pairs[at]]
                    both = left * right
                    factors.append((right, left, both + own * (left + right + both), own))
                table = both_own
                for k in range(4):
                    factor = jnp.where(first, factors[0][k], factors[1][k])
                    table = table + factor * pattern_ref[c, k]
                quads = [
                    [
                        jnp.take_along_axis(table, places[at][i], axis=1, mode="promise_in_bounds")
                        for i in range(STATES)
                    ]
                    for at in (2 * h, 2 * h + 1)
                ]
                joined = product(quads[0], quads[1])
                halves.append(moved(joined, rate_ref[c, tops[h]], mean_state(pi, joined)))
            joined = product(halves[0], halves[1])
            average = mean_state(pi, joined)
            inverse = 1.0 / average
            own_rate = rate_ref[c, 1024 + row]
            for i in range(STATES):
                mid_ref[n, c, i] = joined[i] * inverse + own_rate
            log_ref[n, c] = jnp.log(average)
        return 0

    def clade(j):
        root = 992 + group * 4 + j
        tops = pair_of(root)
        pairs = [pair for top in tops for pair in pair_of(top - 1024)]
        leaves = [leaf - 1792 - group * 32 for pair in pairs for leaf in pair_of(pair - 1024)]
        for c in range(CLS):
            pi = [pi_ref[c, i] for i in range(STATES)]
            scale = log_ref[leaves[0], c]
            for leaf in leaves[1:]:
                scale = scale + log_ref[leaf, c]
            halves = []
            for h in range(2):
                quads = []
                for at in (2 * h, 2 * h + 1):
                    joined = [
                        mid_ref[leaves[2 * at], c, i] * mid_ref[leaves[2 * at + 1], c, i]
                        for i in range(STATES)
                    ]
                    quads.append(moved(joined, rate_ref[c, pairs[at]], mean_state(pi, joined)))
                joined = product(quads[0], quads[1])
                halves.append(moved(joined, rate_ref[c, tops[h]], mean_state(pi, joined)))
            joined = product(halves[0], halves[1])
            inverse = 1.0 / joined[3]
            sent = [joined[0] * inverse, joined[1] * inverse, joined[2] * inverse]
            sent.append(scale + jnp.log(joined[3]))
            for v in range(4):
                for q in range(4):
                    out_ref[q, j, v, 2 * c : 2 * c + 2, :] = sent[v][2 * q : 2 * q + 2, :]

    for j in range(4):
        loads[j].wait()
        lax.fori_loop(8 * j, 8 * j + 8, small_tree, 0)

    def one_clade(j, _):
        clade(j)
        return 0

    lax.fori_loop(0, 4, one_clade, 0)


def upper_kernel(child_ref, clade_ref, top_ref, site_ref, part_ref, node_ref):
    pi = [top_ref[TOP_PI + i] for i in range(STATES)]
    scale = top_ref[TOP_CONST]
    for k in range(16):
        values = [clade_ref[k, 0], clade_ref[k, 1], clade_ref[k, 2]]
        scale = scale + clade_ref[k, 3]
        average = (pi[0] * values[0] + pi[1] * values[1]) + (pi[2] * values[2] + pi[3])
        step = top_ref[TOP_RATES + k] * average
        for i in range(3):
            node_ref[k, i] = values[i] + step
        node_ref[k, 3] = step + 1.0
    at = 16
    for level, count in ((6, 8), (7, 4), (8, 2), (9, 1)):
        begin = 1024 - (1024 >> level)
        for k in range(count):
            left = child_ref[0, begin + k] - 2016
            right = child_ref[1, begin + k] - 2016
            joined = [node_ref[left, i] * node_ref[right, i] for i in range(STATES)]
            average = mean_state(pi, joined)
            if level == 6:
                scale = scale + jnp.log(average)
                inverse = 1.0 / average
                for i in range(STATES):
                    node_ref[at, i] = joined[i] * inverse + top_ref[TOP_RATES + at]
            elif level < 9:
                step = top_ref[TOP_RATES + at] * average
                for i in range(STATES):
                    node_ref[at, i] = joined[i] + step
            else:
                scale = scale + jnp.log(average)
            at += 1
    top = jnp.maximum(scale, pltpu.roll(scale, 2, 0))
    top = jnp.maximum(top, pltpu.roll(top, 4, 0))
    share = jnp.exp(scale - top)
    mass = share + pltpu.roll(share, 2, 0)
    mass = mass + pltpu.roll(mass, 4, 0)
    total = top + jnp.log(mass)
    site_ref[...] = total[0:2] * (1.0 / 1024.0)
    weight = top_ref[TOP_WEIGHT]
    classes = weight * (share / mass)
    row = lax.broadcasted_iota(jnp.int32, TILE, 0)
    column = lax.broadcasted_iota(jnp.int32, TILE, 1)
    by_row = [
        jnp.sum(values, axis=1, keepdims=True) for values in (classes, weight * total, weight)
    ]
    by_pair = lax.shift_right_logical(row, 1)
    line = jnp.where(by_pair == column, by_row[0], 0.0)
    line = jnp.where((column == 4) & (row < 2), by_row[1], line)
    line = jnp.where((column == 5) & (row < 2), by_row[2], line)
    line = jnp.sum(line, axis=0, keepdims=True)
    for k in range(16):
        part_ref[8 * k : 8 * k + 8, :] = jnp.broadcast_to(line, TILE)


def last_kernel(every_ref, own_ref, mean_ref):
    group = lax.axis_index("cls")
    sums = every_ref[0:8, :]
    for k in range(1, 16):
        sums = sums + every_ref[8 * k : 8 * k + 8, :]
    sums = jnp.sum(sums, axis=0, keepdims=True)
    column = lax.broadcasted_iota(jnp.int32, (1, 128), 1)

    def entry(at):
        return jnp.sum(jnp.where(column == at, sums, 0.0), axis=1, keepdims=True)

    count = entry(5)
    own_ref[...] = entry(group) / count
    mean_ref[...] = entry(4) / (count * 1024.0)


def per_device(tip_codes, counts, children, lengths, frequencies, weights):
    codes = tip_codes.reshape(32, 8, 8, 128).transpose(0, 2, 1, 3).reshape(2048, 128)
    child_rows = children.T
    smem = pl.BlockSpec(memory_space=SMEM)
    vmem = pl.BlockSpec(memory_space=VMEM)
    anywhere = pl.BlockSpec(memory_space=pl.ANY)
    ours, top = pl.pallas_call(
        lower_kernel,
        out_shape=(pltpu.VMEM((4, 4, 4, 8, 128), FLOAT), pltpu.VMEM((TOP_ROWS, 8, 128), FLOAT)),
        in_specs=[smem, smem, smem, vmem, anywhere, anywhere],
        out_specs=(vmem, vmem),
        scratch_shapes=[
            pltpu.VMEM((2048, 128), jnp.int32),
            pltpu.VMEM(TILE, jnp.int32),
            pltpu.VMEM((4, 2048), FLOAT),
            pltpu.SMEM((4, 2048), FLOAT),
            pltpu.VMEM((CLS, STATES, 8, 128), FLOAT),
            pltpu.VMEM((CLS, 4, 8, 128), FLOAT),
            pltpu.VMEM((32, CLS, STATES, 8, 128), FLOAT),
            pltpu.VMEM((32, CLS, 8, 128), FLOAT),
            pltpu.SemaphoreType.DMA((6,)),
        ],
        compiler_params=pltpu.CompilerParams(vmem_limit_bytes=16 * 1024 * 1024),
        name="lower_tree",
    )(child_rows, frequencies, weights, lengths, codes, counts.reshape(8, 128))
    clades = lax.all_to_all(ours, "cls", split_axis=0, concat_axis=0, tiled=True)
    site, part = pl.pallas_call(
        upper_kernel,
        out_shape=(jax.ShapeDtypeStruct((2, 128), FLOAT), pltpu.VMEM((128, 128), FLOAT)),
        in_specs=[smem, vmem, vmem],
        out_specs=(vmem, vmem),
        scratch_shapes=[pltpu.VMEM((32, STATES, 8, 128), FLOAT)],
        compiler_params=pltpu.CompilerParams(vmem_limit_bytes=16 * 1024 * 1024),
        name="upper_tree",
    )(child_rows, clades.reshape(16, 4, 8, 128), top)
    every = lax.all_to_all(part, ("cls", "site"), split_axis=0, concat_axis=0, tiled=True)
    own, mean = pl.pallas_call(
        last_kernel,
        out_shape=(jax.ShapeDtypeStruct((1, 1), FLOAT), jax.ShapeDtypeStruct((1, 1), FLOAT)),
        in_specs=[vmem],
        out_specs=(vmem, vmem),
        compiler_params=pltpu.CompilerParams(vmem_limit_bytes=16 * 1024 * 1024),
        name="last_sums",
    )(every)
    return site.reshape(1, 256), own.reshape(1), mean.reshape(())


def solution(mesh):
    return jax.shard_map(
        per_device,
        mesh=mesh,
        in_specs=(P("cls", "site"), P("site"), P(), P(), P(), P()),
        out_specs=(P("cls", "site"), P("cls"), P()),
        check_vma=False,
    )
```

time: 55.5 us -> 49.4 us (0.89)
  blocking collectives: 0 us -> 29.8 us
  starting transfers between devices: 15 us -> 0 us
  waiting for transfers between devices: 14.8 us -> 0 us
  between operations: 5.67 us -> 0.66 us
  Pallas kernels: 9.86 us -> 14.5 us
  local copies, waits for them, and re-layouts: 7.97 us -> 4.03 us
  other arithmetic: 1.82 us -> 0 us
    all_to_all x0 -> x2, blocking collectives: none -> 29.8 us  [the longest x1 18.6 us: per_device(): lax.all_to_all(part, ('cls', 'site'), split_axis=0, concat_axis=0, tiled=...]
    all_to_all x2 -> x0, starting transfers between devices: 15 us -> none  [the longest x1 9.2 us: per_device(): lax.all_to_all(jnp.broadcast_to(part, (128, 128)), ('cls', 'site'), split...]
    all_to_all x2 -> x0, waiting for transfers between devices: 14.8 us -> none  [the longest x1 9.64 us: per_device(): lax.all_to_all(jnp.broadcast_to(part, (128, 128)), ('cls', 'site'), split...]
    pallas_call x2 -> x3, Pallas kernels: 9.86 us -> 14.5 us  [the longest x1 12.4 us: per_device(): pl.pallas_call(lower_kernel, out_shape=(pltpu.VMEM((4, 4, 4, 8, 128), FLO...]
    broadcast_in_dim x10 -> x0, local copies, waits for them, and re-layouts: 3.07 us -> none  [the longest x9 2.41 us: spread(): jnp.broadcast_to(by_class[..., :, None, None], (*by_class.shape, 2, 128))]
    reshape x2 -> x0, local copies, waits for them, and re-layouts: 1.45 us -> none  [the longest x1 0.86 us: per_device(): child_line = children.reshape(-1)]
    unnamed x13 -> x12, local copies, waits for them, and re-layouts: 2.71 us -> 4.03 us
    reduce_sum x5 -> x0, other arithmetic: 1.07 us -> none  [the longest x1 0.6 us: per_device(): log_weight = jnp.log(weights / jnp.sum(weights))]
  transfers between devices with their start and end apart: 2 -> 0, of which waited for: 2 -> 0; matrix products, arithmetic and copies ran while one was open for 1% -> 0% of each run, Pallas kernels for 0% -> 0%
where the time goes in v2:
time: 49.4 us; the launch traced here: 49 us
  blocking collectives  29.8 us (60%)
  Pallas kernels  14.5 us (29%)
  local copies, waits for them, and re-layouts  4.03 us (8%)
  between operations  0.66 us (1%)
    all_to_all x1, blocking collectives, per_device(): lax.all_to_all(part, ('cls', 'site'), split_axis=0, concat_axis=0, tiled=...  18.6 us
    pallas_call x1, Pallas kernels, per_device(): pl.pallas_call(lower_kernel, out_shape=(pltpu.VMEM((4, 4, 4, 8, 128), FLO...  12.4 us
    all_to_all x1, blocking collectives, per_device(): lax.all_to_all(ours, 'cls', split_axis=0, concat_axis=0, tiled=True)  11.2 us
    unnamed x12, local copies, waits for them, and re-layouts  4.03 us
    pallas_call x1, Pallas kernels, per_device(): pl.pallas_call(upper_kernel, out_shape=(jax.ShapeDtypeStruct((2, 128), FL...  1.5 us

profile of v2, /device:TPU:1, one launch (start us, length us, event | category | flops | bytes accessed | tf_op | source)
XLA Modules:
  0.0 49.0 jit_solution(3646867344875991335)
XLA Ops:
  0.6 0.0 copy-start.3
  0.6 0.0 copy-start.5
  0.7 0.7 %copy-done.3 = s32[1024]{0:T(1024)S(1)} copy-done((s32[1024]{0:T(1024)S(1)}, s32[1024]{0:T(1024)}, u32[]{:S(2)}) %copy-start.3) | copy-done | bytes 4120
  1.3 0.0 copy-done.5
  1.3 0.0 copy-start
  1.3 1.2 %copy-done = s32[256,1024]{1,0:T(8,128)S(1)} copy-done((s32[256,1024]{1,0:T(8,128)S(1)}, s32[256,1024]{1,0:T(8,128)}, u32[]{:S(2)}) %copy-start) | copy-done | bytes 1048600
  2.5 0.0 copy-start.1
  2.6 0.7 %copy-done.1 = s32[1023,2]{0,1:T(2,128)S(1)} copy-done((s32[1023,2]{0,1:T(2,128)S(1)}, s32[1023,2]{0,1:T(2,128)}, u32[]{:S(2)}) %copy-start.1) | copy-done | bytes 8208
  3.2 0.0 copy-start.2
  3.2 0.8 %copy-done.2 = f32[4,2046]{1,0:T(4,128)S(1)} copy-done((f32[4,2046]{1,0:T(4,128)S(1)}, f32[4,2046]{1,0:T(4,128)}, u32[]{:S(2)}) %copy-start.2) | copy-done | bytes 32760
  4.0 0.0 copy-start.4
  4.0 0.7 %copy-done.4 = f32[4,4]{1,0:T(4,128)S(1)} copy-done((f32[4,4]{1,0:T(4,128)S(1)}, f32[4,4]{1,0:T(4,128)}, u32[]{:S(2)}) %copy-start.4) | copy-done | bytes 88
  4.7 12.4 %lower_tree.1 = (f32[4,4,4,8,128]{4,3,2,1,0:T(8,128)S(1)}, f32[36,8,128]{2,1,0:T(8,128)S(1)}) custom-call(s32[2,1023]{1,0:T(2,128)S(1)} %bitcast.19, f32[4,4]{1,0:T(4,128)S(1)} %copy-done.4, f32[4]{0:T(128)S(1)} %copy-done.5, f32[4,2046]{1,0:T(4,128)S(1)} %copy-done.2, s32[2048,128]{1,0:T(8,128)S(1)} %bitcast.15, s32[8,128]{1,0:T(8,128)S(1)} %bitcast.21), custom_call_target="tpu_custom_call" | custom-call | tf_op jit(solution)/shard_map/lower_tree/pallas_call | solution.py:276
  17.1 11.2 %all_to_all.16 = f32[4,4,4,8,128]{4,3,2,1,0:T(8,128)S(1)} all-to-all(f32[4,4,4,8,128]{4,3,2,1,0:T(8,128)S(1)} %get-tuple-element.9), channel_id=1, replica_groups=mesh['cls'=4,'site'=32] {'cls'}, dimensions={0} | all-to-all | bytes 524288 | tf_op jit(solution)/shard_map/all_to_all | solution.py:295
  28.3 1.5 %upper_tree.1 = (f32[2,128]{1,0:T(2,128)}, f32[128,128]{1,0:T(8,128)S(1)}) custom-call(s32[2,1023]{1,0:T(2,128)S(1)} %bitcast.20, f32[16,4,8,128]{3,2,1,0:T(8,128)S(1)} %bitcast.16, f32[36,8,128]{2,1,0:T(8,128)S(1)} %get-tuple-element.10.top_ref), custom_call_target="tpu_custom_call" | custom-call | tf_op jit(solution)/shard_map/upper_tree/pallas_call | solution.py:296
  29.8 18.6 %all_to_all.17 = f32[128,1,128]{2,1,0:T(1,128)S(1)} all-to-all(f32[128,1,128]{2,1,0:T(1,128)S(1)} %bitcast.18), channel_id=1, replica_groups=mesh['cls'=4,'site'=32] {'cls','site'}, dimensions={0} | all-to-all | bytes 131072 | tf_op jit(solution)/shard_map/all_to_all | solution.py:305
  48.4 0.6 %last_sums.1 = (f32[1,1]{1,0:T(1,128)}, f32[1,1]{1,0:T(1,128)}) custom-call(f32[128,128]{1,0:T(8,128)S(1)} %bitcast.17), custom_call_target="tpu_custom_call" | custom-call | tf_op jit(solution)/shard_map/last_sums/pallas_call | solution.py:306
Async XLA Ops:
  0.6 0.7 %copy-start.3 = (s32[1024]{0:T(1024)S(1)}, s32[1024]{0:T(1024)}, u32[]{:S(2)}) copy-start(s32[1024]{0:T(1024)} %param.7) | copy-start | bytes 12292
  0.6 0.7 %copy-start.5 = (f32[4]{0:T(128)S(1)}, f32[4]{0:T(128)}, u32[]{:S(2)}) copy-start(f32[4]{0:T(128)} %weight_ref.1) | copy-start | bytes 52
  1.3 1.2 %copy-start = (s32[256,1024]{1,0:T(8,128)S(1)}, s32[256,1024]{1,0:T(8,128)}, u32[]{:S(2)}) copy-start(s32[256,1024]{1,0:T(8,128)} %param.6) | copy-start | bytes 3145732
  2.5 0.7 %copy-start.1 = (s32[1023,2]{0,1:T(2,128)S(1)}, s32[1023,2]{0,1:T(2,128)}, u32[]{:S(2)}) copy-start(s32[1023,2]{0,1:T(2,128)} %param.8) | copy-start | bytes 24556
  3.2 0.8 %copy-start.2 = (f32[4,2046]{1,0:T(4,128)S(1)}, f32[4,2046]{1,0:T(4,128)}, u32[]{:S(2)}) copy-start(f32[4,2046]{1,0:T(4,128)} %lengths_ref.1) | copy-start | bytes 98212
  4.0 0.7 %copy-start.4 = (f32[4,4]{1,0:T(4,128)S(1)}, f32[4,4]{1,0:T(4,128)}, u32[]{:S(2)}) copy-start(f32[4,4]{1,0:T(4,128)} %freq_ref.1) | copy-start | bytes 196

commit v3 on v2

--- a/solution.py
+++ b/solution.py
@@ -11,6 +11,8 @@
 SMEM = pltpu.MemorySpace.SMEM
 VMEM = pltpu.MemorySpace.VMEM
 TILE = (8, 128)
+BUILD = 8
+TREES = 2
 TOP_RATES, TOP_PI, TOP_CONST, TOP_WEIGHT, TOP_ROWS = 0, 30, 34, 35, 36
 
 
@@ -33,12 +35,32 @@
     return jnp.where(selector == 3, options[3], value)
 
 
+def lanes_of(rows, places):
+    return jnp.take_along_axis(rows, places, axis=1, mode="promise_in_bounds")
+
+
 def lower_kernel(
-    child_ref, freq_ref, weight_ref, lengths_ref, codes_hbm, counts_hbm,
+    child_hbm, freq_hbm, weight_hbm, lengths_hbm, codes_hbm, counts_hbm,
     out_ref, top_ref,
-    codes_ref, counts_ref, rate_vec, rate_ref, pi_ref, pattern_ref, mid_ref, log_ref, sems,
+    child_vec, freq_ref, weight_ref, lengths_ref, codes_ref, counts_ref, rate_vec,
+    spot_vec, spot_ref, step_vec, step_ref,
+    pi_ref, pattern_ref, factor_ref, table_ref, mid_ref, log_ref, sems,
 ):
     group = lax.axis_index("cls")
+    small = [
+        pltpu.make_async_copy(source, target, sems.at[4 + k])
+        for k, (source, target) in enumerate(
+            (
+                (freq_hbm, freq_ref),
+                (weight_hbm, weight_ref),
+                (lengths_hbm, lengths_ref),
+                (child_hbm, child_vec),
+                (counts_hbm, counts_ref),
+            )
+        )
+    ]
+    for load in small:
+        load.start()
     loads = [
         pltpu.make_async_copy(
             codes_hbm.at[pl.ds(512 * j, 512)], codes_ref.at[pl.ds(512 * j, 512)], sems.at[j]
@@ -47,19 +69,22 @@
     ]
     for load in loads:
         load.start()
-    count_load = pltpu.make_async_copy(counts_hbm, counts_ref, sems.at[5])
-    count_load.start()
+    for load in small:
+        load.wait()
 
     lane = lax.broadcasted_iota(jnp.int32, TILE, 1)
     sub = lax.broadcasted_iota(jnp.int32, TILE, 0)
     by_pair = lax.shift_right_logical(sub, 1)
+    by_class = lax.bitwise_and(sub, 3)
     uniform, betas = [], []
     for c in range(CLS):
         raw = [jnp.full(TILE, freq_ref[c, i], FLOAT) for i in range(STATES)]
         inverse = 1.0 / ((raw[0] + raw[1]) + (raw[2] + raw[3]))
         uniform.append([value * inverse for value in raw])
         betas.append(1.0 / (1.0 - mean_state(uniform[c], uniform[c])))
-    beta_rows = choose(lax.bitwise_and(sub, 3), betas)[:4]
+        for i in range(STATES):
+            pi_ref[c, i] = uniform[c][i]
+    beta_rows = choose(by_class, betas)[:4]
     total = jnp.zeros((4, 128), FLOAT)
     for k in range(16):
         width = min(128, 2046 - 128 * k)
@@ -68,8 +93,45 @@
             part = jnp.concatenate([part, jnp.zeros((4, 128 - width), FLOAT)], axis=1)
         total = total + part
         rate_vec[:, 128 * k : 128 * k + 128] = jnp.exp(beta_rows * part) - 1.0
-    rate_load = pltpu.make_async_copy(rate_vec, rate_ref, sems.at[4])
-    rate_load.start()
+
+    half = lax.shift_right_logical(group, 1)
+
+    def block(ref, start):
+        return ref[:, pl.ds(pl.multiple_of(start, 128), 128)]
+
+    local = block(child_vec, 128 * group) - 256 * group
+    spot_vec[0:2] = lax.shift_left(lax.shift_right_logical(local, 3), 6) + lax.bitwise_and(local, 7)
+    spot_vec[2:4] = block(child_vec, 512 + 128 * half) - (1024 + 128 * group)
+    spot_vec[4:6] = child_vec[:, 768:896] - (1536 + 128 * half)
+    spot_vec[6:8] = jnp.concatenate([child_vec[:, 896:1023], jnp.zeros((2, 1), jnp.int32)], axis=1)
+    spot_copy = pltpu.make_async_copy(spot_vec, spot_ref, sems.at[9])
+    spot_copy.start()
+    step_vec[0:4] = block(rate_vec, 1536 + 128 * half)
+    step_vec[4:8] = rate_vec[:, 1792:1920]
+    step_vec[8:12] = rate_vec[:, 1920:2048]
+    step_vec[12:16] = jnp.zeros((4, 128), FLOAT)
+    step_copy = pltpu.make_async_copy(step_vec, step_ref, sems.at[10])
+    step_copy.start()
+
+    def twice(rows):
+        return jnp.concatenate([rows, rows], axis=0)
+
+    low = twice(block(rate_vec, 256 * group))
+    high = twice(block(rate_vec, 256 * group + 128))
+    own = twice(block(rate_vec, 1024 + 128 * group))
+
+    def rates_at(places):
+        places = jnp.broadcast_to(places, TILE)
+        inside = lax.bitwise_and(places, 127)
+        return jnp.where(places < 128, lanes_of(low, inside), lanes_of(high, inside))
+
+    left = rates_at(local[0:1])
+    right = rates_at(local[1:2])
+    both = left * right
+    factor_ref[0] = right
+    factor_ref[1] = left
+    factor_ref[2] = both + own * (left + right + both)
+    factor_ref[3] = own
 
     own_state = lax.bitwise_and(lax.shift_right_logical(lane, 4), 3)
     left_code = lax.bitwise_and(lax.shift_right_logical(lane, 2), 3)
@@ -78,15 +140,13 @@
     right_own = own_state == right_code
     first = lane < 64
     both_own = jnp.where(left_own, jnp.where(right_own, 1.0, 0.0), 0.0)
-    for c in range(CLS):
-        left_pi = choose(left_code, uniform[c])
-        right_pi = choose(right_code, uniform[c])
-        pattern_ref[c, 0] = jnp.where(left_own, right_pi, 0.0)
-        pattern_ref[c, 1] = jnp.where(right_own, left_pi, 0.0)
-        pattern_ref[c, 2] = left_pi * right_pi
-        pattern_ref[c, 3] = jnp.where(left_code == right_code, left_pi, 0.0)
-        for i in range(STATES):
-            pi_ref[c, i] = uniform[c][i]
+    by_rows = [choose(by_class, [uniform[c][i] for c in range(CLS)]) for i in range(STATES)]
+    left_pi = choose(left_code, by_rows)
+    right_pi = choose(right_code, by_rows)
+    pattern_ref[0] = jnp.where(left_own, right_pi, 0.0)
+    pattern_ref[1] = jnp.where(right_own, left_pi, 0.0)
+    pattern_ref[2] = left_pi * right_pi
+    pattern_ref[3] = jnp.where(left_code == right_code, left_pi, 0.0)
 
     for i in range(STATES):
         top_ref[TOP_PI + i] = choose(by_pair, [uniform[c][i] for c in range(CLS)])
@@ -96,72 +156,85 @@
     weights = [jnp.full(TILE, weight_ref[c], FLOAT) for c in range(CLS)]
     weight_sum = (weights[0] + weights[1]) + (weights[2] + weights[3])
     top_ref[TOP_CONST] = jnp.log(choose(by_pair, weights) / weight_sum) - beta_pairs * sums
-    last = lengths_ref[:, 1920:2046]
-    last = jnp.concatenate([last, jnp.zeros((4, 2), FLOAT)], axis=1)
+    last = rate_vec[:, 1920:2048]
     last = choose(by_pair, [jnp.broadcast_to(last[c : c + 1], TILE) for c in range(CLS)])
-    last = jnp.exp(beta_pairs * last) - 1.0
     for k in range(30):
         top_ref[TOP_RATES + k] = jnp.broadcast_to(last[:, 96 + k : 97 + k], TILE)
-    count_load.wait()
     quarter = counts_ref[pl.ds(2 * group, 2), :].astype(FLOAT)
     top_ref[TOP_WEIGHT] = jnp.concatenate([quarter, quarter, quarter, quarter], axis=0)
-    rate_load.wait()
-
-    def pair_of(row):
-        return child_ref[0, row], child_ref[1, row]
-
-    def tip_codes(tip):
-        local = tip - group * 256
-        start = lax.shift_left(lax.shift_right_logical(local, 3), 6) + lax.bitwise_and(local, 7)
-        return codes_ref[pl.ds(start, 8, stride=8), :]
-
-    def small_tree(n, _):
-        row = 768 + group * 32 + n
-        tops = pair_of(row)
-        pairs = [pair for top in tops for pair in pair_of(top - 1024)]
-        tips = [pair_of(pair - 1024) for pair in pairs]
-        places = []
-        for at in range(4):
-            code = lax.shift_left(tip_codes(tips[at][0]), 2) + tip_codes(tips[at][1])
-            places.append([code + (64 * (at % 2) + 16 * i) for i in range(STATES)])
+    spot_copy.wait()
+    step_copy.wait()
+
+    def pairs_of(n):
+        tops = [spot_ref[4 + side, 32 * group + n] for side in range(2)]
+        return tops, [spot_ref[2 + side, top] for top in tops for side in range(2)]
+
+    upper_half = sub < 4
+
+    def build_table(n):
+        _, pairs = pairs_of(n)
+        places = jnp.where(
+            upper_half,
+            jnp.where(first, pairs[0], pairs[1]),
+            jnp.where(first, pairs[2], pairs[3]),
+        )
+        table = both_own
+        for k in range(4):
+            table = table + lanes_of(factor_ref[k], places) * pattern_ref[k]
+        table_ref[n] = table
+
+    def build_tables(m, _):
+        for u in range(BUILD):
+            build_table(BUILD * m + u)
+        return 0
+
+    lax.fori_loop(0, 32 // BUILD, build_tables, 0)
+
+    def small_tree(n):
+        tops, pairs = pairs_of(n)
+        joined = []
+        for h in range(2):
+            tables = [
+                jnp.broadcast_to(table_ref[n, 4 * h + c : 4 * h + c + 1, :], TILE) for c in range(CLS)
+            ]
+            quads = []
+            for p in range(2):
+                pair = pairs[2 * h + p]
+                codes = [codes_ref[pl.ds(spot_ref[side, pair], 8, stride=8), :] for side in range(2)]
+                code = lax.shift_left(codes[0], 2) + codes[1]
+                found = []
+                for i in range(STATES):
+                    place = code + (64 * p + 16 * i)
+                    found.append([lanes_of(tables[c], place) for c in range(CLS)])
+                quads.append(found)
+            halves = []
+            for c in range(CLS):
+                pi = [pi_ref[c, i] for i in range(STATES)]
+                values = [quads[0][i][c] * quads[1][i][c] for i in range(STATES)]
+                halves.append(moved(values, step_ref[c, tops[h]], mean_state(pi, values)))
+            joined.append(halves)
         for c in range(CLS):
             pi = [pi_ref[c, i] for i in range(STATES)]
-            halves = []
-            for h in range(2):
-                factors = []
-                for at in (2 * h, 2 * h + 1):
-                    left = rate_ref[c, tips[at][0]]
-                    right = rate_ref[c, tips[at][1]]
-                    own = rate_ref[c, pairs[at]]
-                    both = left * right
-                    factors.append((right, left, both + own * (left + right + both), own))
-                table = both_own
-                for k in range(4):
-                    factor = jnp.where(first, factors[0][k], factors[1][k])
-                    table = table + factor * pattern_ref[c, k]
-                quads = [
-                    [
-                        jnp.take_along_axis(table, places[at][i], axis=1, mode="promise_in_bounds")
-                        for i in range(STATES)
-                    ]
-                    for at in (2 * h, 2 * h + 1)
-                ]
-                joined = product(quads[0], quads[1])
-                halves.append(moved(joined, rate_ref[c, tops[h]], mean_state(pi, joined)))
-            joined = product(halves[0], halves[1])
-            average = mean_state(pi, joined)
+            values = product(joined[0][c], joined[1][c])
+            average = mean_state(pi, values)
             inverse = 1.0 / average
-            own_rate = rate_ref[c, 1024 + row]
+            own_rate = step_ref[4 + c, 32 * group + n]
             for i in range(STATES):
-                mid_ref[n, c, i] = joined[i] * inverse + own_rate
+                mid_ref[n, c, i] = values[i] * inverse + own_rate
             log_ref[n, c] = jnp.log(average)
+
+    def small_trees(m, _):
+        for u in range(TREES):
+            small_tree(TREES * m + u)
         return 0
 
-    def clade(j):
-        root = 992 + group * 4 + j
-        tops = pair_of(root)
-        pairs = [pair for top in tops for pair in pair_of(top - 1024)]
-        leaves = [leaf - 1792 - group * 32 for pair in pairs for leaf in pair_of(pair - 1024)]
+    def tail_pair(at):
+        return [spot_ref[6 + side, at] for side in range(2)]
+
+    def clade(j, _):
+        tops = [top - 1920 for top in tail_pair(96 + 4 * group + j)]
+        pairs = [pair - 1920 for top in tops for pair in tail_pair(top)]
+        leaves = [leaf - 1792 - group * 32 for pair in pairs for leaf in tail_pair(pair)]
         for c in range(CLS):
             pi = [pi_ref[c, i] for i in range(STATES)]
             scale = log_ref[leaves[0], c]
@@ -175,9 +248,9 @@
                         mid_ref[leaves[2 * at], c, i] * mid_ref[leaves[2 * at + 1], c, i]
                         for i in range(STATES)
                     ]
-                    quads.append(moved(joined, rate_ref[c, pairs[at]], mean_state(pi, joined)))
+                    quads.append(moved(joined, step_ref[8 + c, pairs[at]], mean_state(pi, joined)))
                 joined = product(quads[0], quads[1])
-                halves.append(moved(joined, rate_ref[c, tops[h]], mean_state(pi, joined)))
+                halves.append(moved(joined, step_ref[8 + c, tops[h]], mean_state(pi, joined)))
             joined = product(halves[0], halves[1])
             inverse = 1.0 / joined[3]
             sent = [joined[0] * inverse, joined[1] * inverse, joined[2] * inverse]
@@ -185,16 +258,12 @@
             for v in range(4):
                 for q in range(4):
                     out_ref[q, j, v, 2 * c : 2 * c + 2, :] = sent[v][2 * q : 2 * q + 2, :]
-
-    for j in range(4):
-        loads[j].wait()
-        lax.fori_loop(8 * j, 8 * j + 8, small_tree, 0)
-
-    def one_clade(j, _):
-        clade(j)
         return 0
 
-    lax.fori_loop(0, 4, one_clade, 0)
+    for load in loads:
+        load.wait()
+    lax.fori_loop(0, 32 // TREES, small_trees, 0)
+    lax.fori_loop(0, 4, clade, 0)
 
 
 def upper_kernel(child_ref, clade_ref, top_ref, site_ref, part_ref, node_ref):
@@ -272,22 +341,31 @@
     child_rows = children.T
     smem = pl.BlockSpec(memory_space=SMEM)
     vmem = pl.BlockSpec(memory_space=VMEM)
-    anywhere = pl.BlockSpec(memory_space=pl.ANY)
+    hbm = pl.BlockSpec(memory_space=pltpu.MemorySpace.HBM)
     ours, top = pl.pallas_call(
         lower_kernel,
         out_shape=(pltpu.VMEM((4, 4, 4, 8, 128), FLOAT), pltpu.VMEM((TOP_ROWS, 8, 128), FLOAT)),
-        in_specs=[smem, smem, smem, vmem, anywhere, anywhere],
+        in_specs=[hbm] * 6,
         out_specs=(vmem, vmem),
         scratch_shapes=[
+            pltpu.VMEM((2, 1023), jnp.int32),
+            pltpu.SMEM((4, 4), FLOAT),
+            pltpu.SMEM((4,), FLOAT),
+            pltpu.VMEM((4, 2046), FLOAT),
             pltpu.VMEM((2048, 128), jnp.int32),
             pltpu.VMEM(TILE, jnp.int32),
             pltpu.VMEM((4, 2048), FLOAT),
-            pltpu.SMEM((4, 2048), FLOAT),
+            pltpu.VMEM(TILE, jnp.int32),
+            pltpu.SMEM(TILE, jnp.int32),
+            pltpu.VMEM((16, 128), FLOAT),
+            pltpu.SMEM((16, 128), FLOAT),
             pltpu.VMEM((CLS, STATES, 8, 128), FLOAT),
-            pltpu.VMEM((CLS, 4, 8, 128), FLOAT),
+            pltpu.VMEM((4, 8, 128), FLOAT),
+            pltpu.VMEM((4, 8, 128), FLOAT),
+            pltpu.VMEM((32, 8, 128), FLOAT),
             pltpu.VMEM((32, CLS, STATES, 8, 128), FLOAT),
             pltpu.VMEM((32, CLS, 8, 128), FLOAT),
-            pltpu.SemaphoreType.DMA((6,)),
+            pltpu.SemaphoreType.DMA((11,)),
         ],
         compiler_params=pltpu.CompilerParams(vmem_limit_bytes=16 * 1024 * 1024),
         name="lower_tree",

time: 49.4 us -> 45.1 us (0.913)
  Pallas kernels: 14.5 us -> 10.2 us
    pallas_call x1, Pallas kernels: 12.4 us -> 8.11 us  [per_device(): pl.pallas_call(lower_kernel, out_shape=(pltpu.VMEM((4, 4, 4, 8, 128), FLO...]
where the time goes in v3:
time: 45.1 us; the launch traced here: 44.8 us
  blocking collectives  29.8 us (66%)
  Pallas kernels  10.2 us (23%)
  local copies, waits for them, and re-layouts  4.03 us (9%)
  between operations  0.66 us (1%)
    all_to_all x1, blocking collectives, per_device(): lax.all_to_all(part, ('cls', 'site'), split_axis=0, concat_axis=0, tiled=...  18.6 us
    all_to_all x1, blocking collectives, per_device(): lax.all_to_all(ours, 'cls', split_axis=0, concat_axis=0, tiled=True)  11.2 us
    pallas_call x1, Pallas kernels, per_device(): pl.pallas_call(lower_kernel, out_shape=(pltpu.VMEM((4, 4, 4, 8, 128), FLO...  8.11 us
    unnamed x12, local copies, waits for them, and re-layouts  4.03 us
    pallas_call x1, Pallas kernels, per_device(): pl.pallas_call(upper_kernel, out_shape=(jax.ShapeDtypeStruct((2, 128), FL...  1.49 us

profile of v3, /device:TPU:1, one launch (start us, length us, event | category | flops | bytes accessed | tf_op | source)
XLA Modules:
  0.0 44.8 jit_solution(10941836621242278281)
XLA Ops:
  0.6 0.0 copy-start.3
  0.6 0.0 copy-start.5
  0.7 0.7 %copy-done.3 = s32[1024]{0:T(1024)S(1)} copy-done((s32[1024]{0:T(1024)S(1)}, s32[1024]{0:T(1024)}, u32[]{:S(2)}) %copy-start.3) | copy-done | bytes 4120
  1.3 0.0 copy-done.5
  1.3 0.0 copy-start
  1.3 1.2 %copy-done = s32[256,1024]{1,0:T(8,128)S(1)} copy-done((s32[256,1024]{1,0:T(8,128)S(1)}, s32[256,1024]{1,0:T(8,128)}, u32[]{:S(2)}) %copy-start) | copy-done | bytes 1048600
  2.5 0.0 copy-start.1
  2.6 0.7 %copy-done.1 = s32[1023,2]{0,1:T(2,128)S(1)} copy-done((s32[1023,2]{0,1:T(2,128)S(1)}, s32[1023,2]{0,1:T(2,128)}, u32[]{:S(2)}) %copy-start.1) | copy-done | bytes 8208
  3.2 0.0 copy-start.2
  3.2 0.8 %copy-done.2 = f32[4,2046]{1,0:T(4,128)S(1)} copy-done((f32[4,2046]{1,0:T(4,128)S(1)}, f32[4,2046]{1,0:T(4,128)}, u32[]{:S(2)}) %copy-start.2) | copy-done | bytes 32760
  4.0 0.0 copy-start.4
  4.0 0.7 %copy-done.4 = f32[4,4]{1,0:T(4,128)S(1)} copy-done((f32[4,4]{1,0:T(4,128)S(1)}, f32[4,4]{1,0:T(4,128)}, u32[]{:S(2)}) %copy-start.4) | copy-done | bytes 88
  4.7 8.1 %lower_tree.1 = (f32[4,4,4,8,128]{4,3,2,1,0:T(8,128)S(1)}, f32[36,8,128]{2,1,0:T(8,128)S(1)}) custom-call(s32[2,1023]{1,0:T(2,128)S(1)} %bitcast.19, f32[4,4]{1,0:T(4,128)S(1)} %copy-done.4, f32[4]{0:T(128)S(1)} %copy-done.5, f32[4,2046]{1,0:T(4,128)S(1)} %copy-done.2, s32[2048,128]{1,0:T(8,128)S(1)} %bitcast.15, s32[8,128]{1,0:T(8,128)S(1)} %bitcast.21), custom_call_target="tpu_custom_call" | custom-call | tf_op jit(solution)/shard_map/lower_tree/pallas_call | solution.py:345
  12.8 11.2 %all_to_all.16 = f32[4,4,4,8,128]{4,3,2,1,0:T(8,128)S(1)} all-to-all(f32[4,4,4,8,128]{4,3,2,1,0:T(8,128)S(1)} %get-tuple-element.9), channel_id=1, replica_groups=mesh['cls'=4,'site'=32] {'cls'}, dimensions={0} | all-to-all | bytes 524288 | tf_op jit(solution)/shard_map/all_to_all | solution.py:373
  24.0 1.5 %upper_tree.1 = (f32[2,128]{1,0:T(2,128)}, f32[128,128]{1,0:T(8,128)S(1)}) custom-call(s32[2,1023]{1,0:T(2,128)S(1)} %bitcast.20, f32[16,4,8,128]{3,2,1,0:T(8,128)S(1)} %bitcast.16, f32[36,8,128]{2,1,0:T(8,128)S(1)} %get-tuple-element.10.top_ref), custom_call_target="tpu_custom_call" | custom-call | tf_op jit(solution)/shard_map/upper_tree/pallas_call | solution.py:374
  25.5 18.6 %all_to_all.17 = f32[128,1,128]{2,1,0:T(1,128)S(1)} all-to-all(f32[128,1,128]{2,1,0:T(1,128)S(1)} %bitcast.18), channel_id=1, replica_groups=mesh['cls'=4,'site'=32] {'cls','site'}, dimensions={0} | all-to-all | bytes 131072 | tf_op jit(solution)/shard_map/all_to_all | solution.py:383
  44.1 0.6 %last_sums.1 = (f32[1,1]{1,0:T(1,128)}, f32[1,1]{1,0:T(1,128)}) custom-call(f32[128,128]{1,0:T(8,128)S(1)} %bitcast.17), custom_call_target="tpu_custom_call" | custom-call | tf_op jit(solution)/shard_map/last_sums/pallas_call | solution.py:384
Async XLA Ops:
  0.6 0.7 %copy-start.3 = (s32[1024]{0:T(1024)S(1)}, s32[1024]{0:T(1024)}, u32[]{:S(2)}) copy-start(s32[1024]{0:T(1024)} %param.7) | copy-start | bytes 12292
  0.6 0.7 %copy-start.5 = (f32[4]{0:T(128)S(1)}, f32[4]{0:T(128)}, u32[]{:S(2)}) copy-start(f32[4]{0:T(128)} %weight_hbm.1) | copy-start | bytes 52
  1.3 1.2 %copy-start = (s32[256,1024]{1,0:T(8,128)S(1)}, s32[256,1024]{1,0:T(8,128)}, u32[]{:S(2)}) copy-start(s32[256,1024]{1,0:T(8,128)} %param.6) | copy-start | bytes 3145732
  2.5 0.7 %copy-start.1 = (s32[1023,2]{0,1:T(2,128)S(1)}, s32[1023,2]{0,1:T(2,128)}, u32[]{:S(2)}) copy-start(s32[1023,2]{0,1:T(2,128)} %param.8) | copy-start | bytes 24556
  3.2 0.8 %copy-start.2 = (f32[4,2046]{1,0:T(4,128)S(1)}, f32[4,2046]{1,0:T(4,128)}, u32[]{:S(2)}) copy-start(f32[4,2046]{1,0:T(4,128)} %lengths_hbm.1) | copy-start | bytes 98212
  4.0 0.7 %copy-start.4 = (f32[4,4]{1,0:T(4,128)S(1)}, f32[4,4]{1,0:T(4,128)}, u32[]{:S(2)}) copy-start(f32[4,4]{1,0:T(4,128)} %freq_hbm.1) | copy-start | bytes 196

commit v4 on v3

--- a/solution.py
+++ b/solution.py
@@ -369,7 +369,12 @@
         ],
         compiler_params=pltpu.CompilerParams(vmem_limit_bytes=16 * 1024 * 1024),
         name="lower_tree",
-    )(child_rows, frequencies, weights, lengths, codes, counts.reshape(8, 128))
+    )(
+        *(
+            pltpu.with_memory_space_constraint(array, pltpu.MemorySpace.HBM)
+            for array in (child_rows, frequencies, weights, lengths, codes, counts.reshape(8, 128))
+        )
+    )
     clades = lax.all_to_all(ours, "cls", split_axis=0, concat_axis=0, tiled=True)
     site, part = pl.pallas_call(
         upper_kernel,

time: 45.1 us -> 41.1 us (0.911)
  local copies, waits for them, and re-layouts: 4.03 us -> 0.01 us
    unnamed x12 -> x2, local copies, waits for them, and re-layouts: 4.03 us -> 0.01 us
where the time goes in v4:
time: 41.1 us; the launch traced here: 40.9 us
  blocking collectives  29.8 us (73%)
  Pallas kernels  10.4 us (25%)
  between operations  0.65 us (2%)
    all_to_all x1, blocking collectives, per_device(): lax.all_to_all(part, ('cls', 'site'), split_axis=0, concat_axis=0, tiled=...  18.6 us
    all_to_all x1, blocking collectives, per_device(): lax.all_to_all(ours, 'cls', split_axis=0, concat_axis=0, tiled=True)  11.2 us
    pallas_call x1, Pallas kernels, per_device(): pl.pallas_call(lower_kernel, out_shape=(pltpu.VMEM((4, 4, 4, 8, 128), FLO...  8.3 us
    pallas_call x1, Pallas kernels, per_device(): pl.pallas_call(upper_kernel, out_shape=(jax.ShapeDtypeStruct((2, 128), FL...  1.5 us

profile of v4, /device:TPU:1, one launch (start us, length us, event | category | flops | bytes accessed | tf_op | source)
XLA Modules:
  0.0 40.9 jit_solution(3306259535091721523)
XLA Ops:
  0.6 8.3 %lower_tree.1 = (f32[4,4,4,8,128]{4,3,2,1,0:T(8,128)S(1)}, f32[36,8,128]{2,1,0:T(8,128)S(1)}) custom-call(s32[2,1023]{1,0:T(2,128)} %bitcast.18, f32[4,4]{1,0:T(4,128)} %freq_hbm.1, f32[4]{0:T(128)} %weight_hbm.1, f32[4,2046]{1,0:T(4,128)} %lengths_hbm.1, s32[2048,128]{1,0:T(8,128)} %bitcast.20, s32[8,128]{1,0:T(8,128)} %bitcast.21), custom_call_target="tpu_custom_call" | custom-call | tf_op jit(solution)/shard_map/lower_tree/pallas_call | solution.py:345
  8.9 0.0 copy-start
  9.0 11.2 %all_to_all.16 = f32[4,4,4,8,128]{4,3,2,1,0:T(8,128)S(1)} all-to-all(f32[4,4,4,8,128]{4,3,2,1,0:T(8,128)S(1)} %get-tuple-element.9), channel_id=1, replica_groups=mesh['cls'=4,'site'=32] {'cls'}, dimensions={0} | all-to-all | bytes 524288 | tf_op jit(solution)/shard_map/all_to_all | solution.py:378
  20.2 0.0 copy-done
  20.2 1.5 %upper_tree.1 = (f32[2,128]{1,0:T(2,128)}, f32[128,128]{1,0:T(8,128)S(1)}) custom-call(s32[2,1023]{1,0:T(2,128)S(1)} %bitcast.19, f32[16,4,8,128]{3,2,1,0:T(8,128)S(1)} %bitcast.15, f32[36,8,128]{2,1,0:T(8,128)S(1)} %get-tuple-element.10.top_ref), custom_call_target="tpu_custom_call" | custom-call | tf_op jit(solution)/shard_map/upper_tree/pallas_call | solution.py:379
  21.7 18.6 %all_to_all.17 = f32[128,1,128]{2,1,0:T(1,128)S(1)} all-to-all(f32[128,1,128]{2,1,0:T(1,128)S(1)} %bitcast.17), channel_id=1, replica_groups=mesh['cls'=4,'site'=32] {'cls','site'}, dimensions={0} | all-to-all | bytes 131072 | tf_op jit(solution)/shard_map/all_to_all | solution.py:388
  40.3 0.6 %last_sums.1 = (f32[1,1]{1,0:T(1,128)}, f32[1,1]{1,0:T(1,128)}) custom-call(f32[128,128]{1,0:T(8,128)S(1)} %bitcast.16), custom_call_target="tpu_custom_call" | custom-call | tf_op jit(solution)/shard_map/last_sums/pallas_call | solution.py:389
Async XLA Ops:
  8.9 11.2 %copy-start = (s32[1023,2]{0,1:T(2,128)S(1)}, s32[1023,2]{0,1:T(2,128)}, u32[]{:S(2)}) copy-start(s32[1023,2]{0,1:T(2,128)} %param.8) | copy-start | bytes 24556

commit v5 on v4

--- a/solution.py
+++ b/solution.py
@@ -12,7 +12,6 @@
 VMEM = pltpu.MemorySpace.VMEM
 TILE = (8, 128)
 BUILD = 8
-TREES = 2
 TOP_RATES, TOP_PI, TOP_CONST, TOP_WEIGHT, TOP_ROWS = 0, 30, 34, 35, 36
 
 
@@ -44,7 +43,7 @@
     out_ref, top_ref,
     child_vec, freq_ref, weight_ref, lengths_ref, codes_ref, counts_ref, rate_vec,
     spot_vec, spot_ref, step_vec, step_ref,
-    pi_ref, pattern_ref, factor_ref, table_ref, mid_ref, log_ref, sems,
+    pi_ref, pattern_ref, factor_ref, table_ref, even_ref, odd_ref, mid_ref, log_ref, sems,
 ):
     group = lax.axis_index("cls")
     small = [
@@ -190,32 +189,33 @@
 
     lax.fori_loop(0, 32 // BUILD, build_tables, 0)
 
-    def small_tree(n):
-        tops, pairs = pairs_of(n)
-        joined = []
+    def gather_tree(n, buffer):
+        _, pairs = pairs_of(n)
         for h in range(2):
             tables = [
                 jnp.broadcast_to(table_ref[n, 4 * h + c : 4 * h + c + 1, :], TILE) for c in range(CLS)
             ]
-            quads = []
+            codes = []
             for p in range(2):
                 pair = pairs[2 * h + p]
-                codes = [codes_ref[pl.ds(spot_ref[side, pair], 8, stride=8), :] for side in range(2)]
-                code = lax.shift_left(codes[0], 2) + codes[1]
-                found = []
-                for i in range(STATES):
-                    place = code + (64 * p + 16 * i)
-                    found.append([lanes_of(tables[c], place) for c in range(CLS)])
-                quads.append(found)
-            halves = []
-            for c in range(CLS):
-                pi = [pi_ref[c, i] for i in range(STATES)]
-                values = [quads[0][i][c] * quads[1][i][c] for i in range(STATES)]
-                halves.append(moved(values, step_ref[c, tops[h]], mean_state(pi, values)))
-            joined.append(halves)
+                sides = [codes_ref[pl.ds(spot_ref[side, pair], 8, stride=8), :] for side in range(2)]
+                codes.append(lax.shift_left(sides[0], 2) + sides[1])
+            for i in range(STATES):
+                places = [codes[p] + (64 * p + 16 * i) for p in range(2)]
+                lefts = [lanes_of(tables[c], places[0]) for c in range(CLS)]
+                rights = [lanes_of(tables[c], places[1]) for c in range(CLS)]
+                for c in range(CLS):
+                    buffer[h, c, i] = lefts[c] * rights[c]
+
+    def finish_tree(n, buffer):
+        tops, _ = pairs_of(n)
         for c in range(CLS):
             pi = [pi_ref[c, i] for i in range(STATES)]
-            values = product(joined[0][c], joined[1][c])
+            halves = []
+            for h in range(2):
+                values = [buffer[h, c, i] for i in range(STATES)]
+                halves.append(moved(values, step_ref[c, tops[h]], mean_state(pi, values)))
+            values = product(halves[0], halves[1])
             average = mean_state(pi, values)
             inverse = 1.0 / average
             own_rate = step_ref[4 + c, 32 * group + n]
@@ -224,8 +224,10 @@
             log_ref[n, c] = jnp.log(average)
 
     def small_trees(m, _):
-        for u in range(TREES):
-            small_tree(TREES * m + u)
+        finish_tree(2 * m, even_ref)
+        gather_tree(2 * m + 1, odd_ref)
+        finish_tree(2 * m + 1, odd_ref)
+        gather_tree(jnp.minimum(2 * m + 2, 31), even_ref)
         return 0
 
     def tail_pair(at):
@@ -257,26 +259,30 @@
             sent.append(scale + jnp.log(joined[3]))
             for v in range(4):
                 for q in range(4):
-                    out_ref[q, j, v, 2 * c : 2 * c + 2, :] = sent[v][2 * q : 2 * q + 2, :]
+                    out_ref[lax.bitwise_and(q - group, 3), j, v, 2 * c : 2 * c + 2, :] = sent[v][2 * q : 2 * q + 2, :]
         return 0
 
     for load in loads:
         load.wait()
-    lax.fori_loop(0, 32 // TREES, small_trees, 0)
+    gather_tree(0, even_ref)
+    lax.fori_loop(0, 16, small_trees, 0)
     lax.fori_loop(0, 4, clade, 0)
 
 
-def upper_kernel(child_ref, clade_ref, top_ref, site_ref, part_ref, node_ref):
+def upper_kernel(child_ref, own_ref, one_ref, two_ref, three_ref, top_ref, site_ref, part_ref, node_ref):
+    group = lax.axis_index("cls")
     pi = [top_ref[TOP_PI + i] for i in range(STATES)]
     scale = top_ref[TOP_CONST]
-    for k in range(16):
-        values = [clade_ref[k, 0], clade_ref[k, 1], clade_ref[k, 2]]
-        scale = scale + clade_ref[k, 3]
-        average = (pi[0] * values[0] + pi[1] * values[1]) + (pi[2] * values[2] + pi[3])
-        step = top_ref[TOP_RATES + k] * average
-        for i in range(3):
-            node_ref[k, i] = values[i] + step
-        node_ref[k, 3] = step + 1.0
+    for hop, piece_ref in enumerate((own_ref, one_ref, two_ref, three_ref)):
+        source = 4 * lax.bitwise_and(group - hop, 3)
+        for j in range(4):
+            values = [piece_ref[j, 0], piece_ref[j, 1], piece_ref[j, 2]]
+            scale = scale + piece_ref[j, 3]
+            average = (pi[0] * values[0] + pi[1] * values[1]) + (pi[2] * values[2] + pi[3])
+            step = top_ref[TOP_RATES + source + j] * average
+            for i in range(3):
+                node_ref[source + j, i] = values[i] + step
+            node_ref[source + j, 3] = step + 1.0
     at = 16
     for level, count in ((6, 8), (7, 4), (8, 2), (9, 1)):
         begin = 1024 - (1024 >> level)
@@ -363,6 +369,8 @@
             pltpu.VMEM((4, 8, 128), FLOAT),
             pltpu.VMEM((4, 8, 128), FLOAT),
             pltpu.VMEM((32, 8, 128), FLOAT),
+            pltpu.VMEM((2, CLS, STATES, 8, 128), FLOAT),
+            pltpu.VMEM((2, CLS, STATES, 8, 128), FLOAT),
             pltpu.VMEM((32, CLS, STATES, 8, 128), FLOAT),
             pltpu.VMEM((32, CLS, 8, 128), FLOAT),
             pltpu.SemaphoreType.DMA((11,)),
@@ -375,16 +383,18 @@
             for array in (child_rows, frequencies, weights, lengths, codes, counts.reshape(8, 128))
         )
     )
-    clades = lax.all_to_all(ours, "cls", split_axis=0, concat_axis=0, tiled=True)
+    pieces = [ours[0]]
+    for hop in range(1, 4):
+        pieces.append(lax.ppermute(ours[hop], "cls", [(k, (k + hop) % 4) for k in range(4)]))
     site, part = pl.pallas_call(
         upper_kernel,
         out_shape=(jax.ShapeDtypeStruct((2, 128), FLOAT), pltpu.VMEM((128, 128), FLOAT)),
-        in_specs=[smem, vmem, vmem],
+        in_specs=[smem] + [vmem] * 5,
         out_specs=(vmem, vmem),
         scratch_shapes=[pltpu.VMEM((32, STATES, 8, 128), FLOAT)],
         compiler_params=pltpu.CompilerParams(vmem_limit_bytes=16 * 1024 * 1024),
         name="upper_tree",
-    )(child_rows, clades.reshape(16, 4, 8, 128), top)
+    )(child_rows, *pieces, top)
     every = lax.all_to_all(part, ("cls", "site"), split_axis=0, concat_axis=0, tiled=True)
     own, mean = pl.pallas_call(
         last_kernel,

time: 41.1 us -> 39.8 us (0.968)
  blocking collectives: 29.8 us -> 19.1 us
  starting transfers between devices: 0 us -> 5.34 us
  waiting for transfers between devices: 0 us -> 4.33 us
    all_to_all x1 -> x0, blocking collectives: 11.2 us -> none  [per_device(): lax.all_to_all(ours, 'cls', split_axis=0, concat_axis=0, tiled=True)]
    ppermute x0 -> x3, starting transfers between devices: none -> 5.34 us  [per_device(): lax.ppermute(ours[hop], 'cls', [(k, (k + hop) % 4) for k in range(4)])]
    ppermute x0 -> x3, waiting for transfers between devices: none -> 4.33 us  [per_device(): lax.ppermute(ours[hop], 'cls', [(k, (k + hop) % 4) for k in range(4)])]
    all_to_all x1, blocking collectives: 18.6 us -> 19.1 us  [per_device(): lax.all_to_all(part, ('cls', 'site'), split_axis=0, concat_axis=0, tiled=...]
  transfers between devices with their start and end apart: 0 -> 3, of which waited for: 0 -> 3; matrix products, arithmetic and copies ran while one was open for 0% -> 0% of each run, Pallas kernels for 0% -> 0%
where the time goes in v5:
time: 39.8 us; the launch traced here: 39.6 us
  blocking collectives  19.1 us (48%)
  Pallas kernels  10.2 us (26%)
  starting transfers between devices  5.34 us (13%)
  waiting for transfers between devices  4.33 us (11%)
  between operations  0.66 us (2%)
    all_to_all x1, blocking collectives, per_device(): lax.all_to_all(part, ('cls', 'site'), split_axis=0, concat_axis=0, tiled=...  19.1 us
    pallas_call x1, Pallas kernels, per_device(): pl.pallas_call(lower_kernel, out_shape=(pltpu.VMEM((4, 4, 4, 8, 128), FLO...  8.06 us
    ppermute x3, starting transfers between devices, per_device(): lax.ppermute(ours[hop], 'cls', [(k, (k + hop) % 4) for k in range(4)])  5.34 us
    ppermute x3, waiting for transfers between devices, per_device(): lax.ppermute(ours[hop], 'cls', [(k, (k + hop) % 4) for k in range(4)])  4.33 us
    pallas_call x1, Pallas kernels, per_device(): pl.pallas_call(upper_kernel, out_shape=(jax.ShapeDtypeStruct((2, 128), FL...  1.5 us
  transfers between devices with their start and end apart: 3, of which 3 were waited for; matrix products, arithmetic and copies ran while one was open for 0% of the time, Pallas kernels for 0%

profile of v5, /device:TPU:1, one launch (start us, length us, event | category | flops | bytes accessed | tf_op | source)
XLA Modules:
  0.0 39.6 jit_solution(7149351084441161590)
XLA Ops:
  0.6 8.1 %lower_tree.1 = (f32[4,4,4,8,128]{4,3,2,1,0:T(8,128)S(1)}, f32[36,8,128]{2,1,0:T(8,128)S(1)}) custom-call(s32[2,1023]{1,0:T(2,128)} %bitcast.24, f32[4,4]{1,0:T(4,128)} %freq_hbm.1, f32[4]{0:T(128)} %weight_hbm.1, f32[4,2046]{1,0:T(4,128)} %lengths_hbm.1, s32[2048,128]{1,0:T(8,128)} %bitcast.26, s32[8,128]{1,0:T(8,128)} %bitcast.27), custom_call_target="tpu_custom_call" | custom-call | tf_op jit(solution)/shard_map/lower_tree/pallas_call | solution.py:351
  8.7 0.0 copy-start
  8.7 4.6 %collective-permute-start.2 = (f32[4,4,8,128]{3,2,1,0:T(8,128)S(1)}, f32[4,4,8,128]{3,2,1,0:T(8,128)S(1)}, u32[]{:S(2)}, u32[]{:S(2)}) collective-permute-start(f32[4,4,8,128]{3,2,1,0:T(8,128)S(1)} %get-tuple-element.15), channel_id=1, source_target_pairs={{0,96},{32,0},{64,32},{96,64},{1,97},{33,1},{65,33},{97,65},{2,98}... | collective-permute-start | bytes 196616 | tf_op jit(solution)/shard_map/ppermute | solution.py:388
  13.4 0.0 collective-permute-start.1
  13.4 0.7 %collective-permute-start = (f32[4,4,8,128]{3,2,1,0:T(8,128)S(1)}, f32[4,4,8,128]{3,2,1,0:T(8,128)S(1)}, u32[]{:S(2)}, u32[]{:S(2)}) collective-permute-start(f32[4,4,8,128]{3,2,1,0:T(8,128)S(1)} %get-tuple-element.17), channel_id=1, source_target_pairs={{0,32},{32,64},{64,96},{96,0},{1,33},{33,65},{65,97},{97,1},{2,34}... | collective-permute-start | bytes 196616 | tf_op jit(solution)/shard_map/ppermute | solution.py:388
  14.1 0.6 %collective-permute-done.2.three_ref = f32[4,4,8,128]{3,2,1,0:T(8,128)S(1)} collective-permute-done((f32[4,4,8,128]{3,2,1,0:T(8,128)S(1)}, f32[4,4,8,128]{3,2,1,0:T(8,128)S(1)}, u32[]{:S(2)}, u32[]{:S(2)}) %collective-permute-start.2) | collective-permute-done | bytes 65568 | tf_op jit(solution)/shard_map/ppermute | solution.py:388
  14.7 3.4 %collective-permute-done.1.two_ref = f32[4,4,8,128]{3,2,1,0:T(8,128)S(1)} collective-permute-done((f32[4,4,8,128]{3,2,1,0:T(8,128)S(1)}, f32[4,4,8,128]{3,2,1,0:T(8,128)S(1)}, u32[]{:S(2)}, u32[]{:S(2)}) %collective-permute-start.1) | collective-permute-done | bytes 65568 | tf_op jit(solution)/shard_map/ppermute | solution.py:388
  18.1 0.3 collective-permute-done.one_ref
  18.4 0.0 copy-done
  18.4 1.5 %upper_tree.1 = (f32[2,128]{1,0:T(2,128)}, f32[128,128]{1,0:T(8,128)S(1)}) custom-call(s32[2,1023]{1,0:T(2,128)S(1)} %bitcast.25, f32[4,4,8,128]{3,2,1,0:T(8,128)S(1)} %get-tuple-element.18.own_ref, f32[4,4,8,128]{3,2,1,0:T(8,128)S(1)} %collective-permute-done.one_ref, f32[4,4,8,128]{3,2,1,0:T(8,128)S(1)} %collective-permute-done.1.two_ref, ...), custom_call_target="tpu_custom_call" | custom-call | tf_op jit(solution)/shard_map/upper_tree/pallas_call | solution.py:389
  19.9 19.1 %all_to_all.11 = f32[128,1,128]{2,1,0:T(1,128)S(1)} all-to-all(f32[128,1,128]{2,1,0:T(1,128)S(1)} %bitcast.23), channel_id=1, replica_groups=mesh['cls'=4,'site'=32] {'cls','site'}, dimensions={0} | all-to-all | bytes 131072 | tf_op jit(solution)/shard_map/all_to_all | solution.py:398
  39.0 0.6 %last_sums.1 = (f32[1,1]{1,0:T(1,128)}, f32[1,1]{1,0:T(1,128)}) custom-call(f32[128,128]{1,0:T(8,128)S(1)} %bitcast.22), custom_call_target="tpu_custom_call" | custom-call | tf_op jit(solution)/shard_map/last_sums/pallas_call | solution.py:399
  (1 shorter events, 0.0 us)
Async XLA Ops:
  8.7 9.7 %copy-start = (s32[1023,2]{0,1:T(2,128)S(1)}, s32[1023,2]{0,1:T(2,128)}, u32[]{:S(2)}) copy-start(s32[1023,2]{0,1:T(2,128)} %param.8) | copy-start | bytes 24556
  8.7 6.0 %collective-permute-start.2 = (f32[4,4,8,128]{3,2,1,0:T(8,128)S(1)}, f32[4,4,8,128]{3,2,1,0:T(8,128)S(1)}, u32[]{:S(2)}, u32[]{:S(2)}) collective-permute-start(f32[4,4,8,128]{3,2,1,0:T(8,128)S(1)} %get-tuple-element.15), channel_id=1, source_target_pairs={{0,96},{32,0},{64,32},{96,64},{1,97},{33,1},{65,33},{97,65},{2,98}... | collective-permute-start | bytes 196616 | tf_op jit(solution)/shard_map/ppermute | solution.py:388
  13.4 4.7 %collective-permute-start.1 = (f32[4,4,8,128]{3,2,1,0:T(8,128)S(1)}, f32[4,4,8,128]{3,2,1,0:T(8,128)S(1)}, u32[]{:S(2)}, u32[]{:S(2)}) collective-permute-start(f32[4,4,8,128]{3,2,1,0:T(8,128)S(1)} %get-tuple-element.16), channel_id=1, source_target_pairs={{0,64},{32,96},{64,0},{96,32},{1,65},{33,97},{65,1},{97,33},{2,66}... | collective-permute-start | bytes 196616 | tf_op jit(solution)/shard_map/ppermute | solution.py:388
  13.4 5.0 %collective-permute-start = (f32[4,4,8,128]{3,2,1,0:T(8,128)S(1)}, f32[4,4,8,128]{3,2,1,0:T(8,128)S(1)}, u32[]{:S(2)}, u32[]{:S(2)}) collective-permute-start(f32[4,4,8,128]{3,2,1,0:T(8,128)S(1)} %get-tuple-element.17), channel_id=1, source_target_pairs={{0,32},{32,64},{64,96},{96,0},{1,33},{33,65},{65,97},{97,1},{2,34}... | collective-permute-start | bytes 196616 | tf_op jit(solution)/shard_map/ppermute | solution.py:388

commit v6 on v5

--- a/solution.py
+++ b/solution.py
@@ -43,7 +43,7 @@
     out_ref, top_ref,
     child_vec, freq_ref, weight_ref, lengths_ref, codes_ref, counts_ref, rate_vec,
     spot_vec, spot_ref, step_vec, step_ref,
-    pi_ref, pattern_ref, factor_ref, table_ref, even_ref, odd_ref, mid_ref, log_ref, sems,
+    pi_ref, pattern_ref, factor_ref, table_ref, rate4_vec, rate4_ref, mid_ref, log_ref, sems,
 ):
     group = lax.axis_index("cls")
     small = [
@@ -131,6 +131,10 @@
     factor_ref[1] = left
     factor_ref[2] = both + own * (left + right + both)
     factor_ref[3] = own
+    for k in range(4):
+        rate4_vec[4 * k : 4 * k + 4] = factor_ref[k, 0:4]
+    rate4_copy = pltpu.make_async_copy(rate4_vec, rate4_ref, sems.at[11])
+    rate4_copy.start()
 
     own_state = lax.bitwise_and(lax.shift_right_logical(lane, 4), 3)
     left_code = lax.bitwise_and(lax.shift_right_logical(lane, 2), 3)
@@ -163,6 +167,7 @@
     top_ref[TOP_WEIGHT] = jnp.concatenate([quarter, quarter, quarter, quarter], axis=0)
     spot_copy.wait()
     step_copy.wait()
+    rate4_copy.wait()
 
     def pairs_of(n):
         tops = [spot_ref[4 + side, 32 * group + n] for side in range(2)]
@@ -170,52 +175,85 @@
 
     upper_half = sub < 4
 
-    def build_table(n):
-        _, pairs = pairs_of(n)
+    def build_table(m):
+        pairs = [pairs_of(2 * m + u)[1] for u in range(2)]
         places = jnp.where(
             upper_half,
-            jnp.where(first, pairs[0], pairs[1]),
-            jnp.where(first, pairs[2], pairs[3]),
+            jnp.where(first, pairs[0][0], pairs[0][2]),
+            jnp.where(first, pairs[1][0], pairs[1][2]),
         )
         table = both_own
         for k in range(4):
             table = table + lanes_of(factor_ref[k], places) * pattern_ref[k]
-        table_ref[n] = table
+        table_ref[m] = table
 
     def build_tables(m, _):
         for u in range(BUILD):
             build_table(BUILD * m + u)
         return 0
 
-    lax.fori_loop(0, 32 // BUILD, build_tables, 0)
-
-    def gather_tree(n, buffer):
-        _, pairs = pairs_of(n)
-        for h in range(2):
-            tables = [
-                jnp.broadcast_to(table_ref[n, 4 * h + c : 4 * h + c + 1, :], TILE) for c in range(CLS)
-            ]
-            codes = []
-            for p in range(2):
-                pair = pairs[2 * h + p]
-                sides = [codes_ref[pl.ds(spot_ref[side, pair], 8, stride=8), :] for side in range(2)]
-                codes.append(lax.shift_left(sides[0], 2) + sides[1])
-            for i in range(STATES):
-                places = [codes[p] + (64 * p + 16 * i) for p in range(2)]
-                lefts = [lanes_of(tables[c], places[0]) for c in range(CLS)]
-                rights = [lanes_of(tables[c], places[1]) for c in range(CLS)]
-                for c in range(CLS):
-                    buffer[h, c, i] = lefts[c] * rights[c]
-
-    def finish_tree(n, buffer):
-        tops, _ = pairs_of(n)
+    lax.fori_loop(0, 16 // BUILD, build_tables, 0)
+
+    def codes_of(pair):
+        return [codes_ref[pl.ds(spot_ref[side, pair], 8, stride=8), :] for side in range(2)]
+
+    def chosen_pair(pair):
+        left, right = codes_of(pair)
+        left_odd = lax.bitwise_and(left, 1) == 1
+        right_odd = lax.bitwise_and(right, 1) == 1
+        left_high = left >= 2
+        right_high = right >= 2
+        same = left == right
+        left_is = [left == i for i in range(STATES)]
+        right_is = [right == i for i in range(STATES)]
+        found = []
         for c in range(CLS):
             pi = [pi_ref[c, i] for i in range(STATES)]
-            halves = []
-            for h in range(2):
-                values = [buffer[h, c, i] for i in range(STATES)]
-                halves.append(moved(values, step_ref[c, tops[h]], mean_state(pi, values)))
-            values = product(halves[0], halves[1])
+            left_pi = jnp.where(
+                left_high, jnp.where(left_odd, pi[3], pi[2]), jnp.where(left_odd, pi[1], pi[0])
+            )
+            right_pi = jnp.where(
+                right_high, jnp.where(right_odd, pi[3], pi[2]), jnp.where(right_odd, pi[1], pi[0])
+            )
+            left_step = rate4_ref[4 + c, pair] * left_pi
+            right_step = rate4_ref[c, pair] * right_pi
+            base = rate4_ref[8 + c, pair] * (left_pi * right_pi)
+            base = base + jnp.where(same, rate4_ref[12 + c, pair] * left_pi, 0.0)
+            at_right = base + left_step
+            at_left = base + right_step
+            at_left = jnp.where(same, at_left + (left_step + 1.0), at_left)
+            found.append(
+                [
+                    jnp.where(left_is[i], at_left, jnp.where(right_is[i], at_right, base))
+                    for i in range(STATES)
+                ]
+            )
+        return found
+
+    def small_tree(m, u):
+        n = 2 * m + u
+        tops, pairs = pairs_of(n)
+        tables = [
+            jnp.broadcast_to(table_ref[m, 4 * u + c : 4 * u + c + 1, :], TILE) for c in range(CLS)
+        ]
+        halves = []
+        for h in range(2):
+            sides = codes_of(pairs[2 * h])
+            code = lax.shift_left(sides[0], 2) + sides[1] + 64 * h
+            looked = []
+            for i in range(STATES):
+                place = code + 16 * i if i else code
+                looked.append([lanes_of(tables[c], place) for c in range(CLS)])
+            chosen = chosen_pair(pairs[2 * h + 1])
+            parts = []
+            for c in range(CLS):
+                pi = [pi_ref[c, i] for i in range(STATES)]
+                values = [looked[i][c] * chosen[c][i] for i in range(STATES)]
+                parts.append(moved(values, step_ref[c, tops[h]], mean_state(pi, values)))
+            halves.append(parts)
+        for c in range(CLS):
+            pi = [pi_ref[c, i] for i in range(STATES)]
+            values = product(halves[0][c], halves[1][c])
             average = mean_state(pi, values)
             inverse = 1.0 / average
             own_rate = step_ref[4 + c, 32 * group + n]
@@ -224,10 +262,8 @@
             log_ref[n, c] = jnp.log(average)
 
     def small_trees(m, _):
-        finish_tree(2 * m, even_ref)
-        gather_tree(2 * m + 1, odd_ref)
-        finish_tree(2 * m + 1, odd_ref)
-        gather_tree(jnp.minimum(2 * m + 2, 31), even_ref)
+        for u in range(2):
+            small_tree(m, u)
         return 0
 
     def tail_pair(at):
@@ -264,7 +300,6 @@
 
     for load in loads:
         load.wait()
-    gather_tree(0, even_ref)
     lax.fori_loop(0, 16, small_trees, 0)
     lax.fori_loop(0, 4, clade, 0)
 
@@ -368,12 +403,12 @@
             pltpu.VMEM((CLS, STATES, 8, 128), FLOAT),
             pltpu.VMEM((4, 8, 128), FLOAT),
             pltpu.VMEM((4, 8, 128), FLOAT),
-            pltpu.VMEM((32, 8, 128), FLOAT),
-            pltpu.VMEM((2, CLS, STATES, 8, 128), FLOAT),
-            pltpu.VMEM((2, CLS, STATES, 8, 128), FLOAT),
+            pltpu.VMEM((16, 8, 128), FLOAT),
+            pltpu.VMEM((16, 128), FLOAT),
+            pltpu.SMEM((16, 128), FLOAT),
             pltpu.VMEM((32, CLS, STATES, 8, 128), FLOAT),
             pltpu.VMEM((32, CLS, 8, 128), FLOAT),
-            pltpu.SemaphoreType.DMA((11,)),
+            pltpu.SemaphoreType.DMA((12,)),
         ],
         compiler_params=pltpu.CompilerParams(vmem_limit_bytes=16 * 1024 * 1024),
         name="lower_tree",

time: 39.8 us -> 38.1 us (0.957)
  Pallas kernels: 10.2 us -> 8.48 us
    pallas_call x1, Pallas kernels: 8.06 us -> 6.37 us  [per_device(): pl.pallas_call(lower_kernel, out_shape=(pltpu.VMEM((4, 4, 4, 8, 128), FLO...]
where the time goes in v6:
time: 38.1 us; the launch traced here: 38 us
  blocking collectives  19.1 us (50%)
  Pallas kernels  8.48 us (22%)
  starting transfers between devices  5.34 us (14%)
  waiting for transfers between devices  4.33 us (11%)
  between operations  0.66 us (2%)
    all_to_all x1, blocking collectives, per_device(): lax.all_to_all(part, ('cls', 'site'), split_axis=0, concat_axis=0, tiled=...  19.1 us
    pallas_call x1, Pallas kernels, per_device(): pl.pallas_call(lower_kernel, out_shape=(pltpu.VMEM((4, 4, 4, 8, 128), FLO...  6.37 us
    ppermute x3, starting transfers between devices, per_device(): lax.ppermute(ours[hop], 'cls', [(k, (k + hop) % 4) for k in range(4)])  5.34 us
    ppermute x3, waiting for transfers between devices, per_device(): lax.ppermute(ours[hop], 'cls', [(k, (k + hop) % 4) for k in range(4)])  4.33 us
    pallas_call x1, Pallas kernels, per_device(): pl.pallas_call(upper_kernel, out_shape=(jax.ShapeDtypeStruct((2, 128), FL...  1.49 us
  transfers between devices with their start and end apart: 3, of which 3 were waited for; matrix products, arithmetic and copies ran while one was open for 0% of the time, Pallas kernels for 0%

profile of v6, /device:TPU:1, one launch (start us, length us, event | category | flops | bytes accessed | tf_op | source)
XLA Modules:
  0.0 38.0 jit_solution(10459728699507491991)
XLA Ops:
  0.6 6.4 %lower_tree.1 = (f32[4,4,4,8,128]{4,3,2,1,0:T(8,128)S(1)}, f32[36,8,128]{2,1,0:T(8,128)S(1)}) custom-call(s32[2,1023]{1,0:T(2,128)} %bitcast.24, f32[4,4]{1,0:T(4,128)} %freq_hbm.1, f32[4]{0:T(128)} %weight_hbm.1, f32[4,2046]{1,0:T(4,128)} %lengths_hbm.1, s32[2048,128]{1,0:T(8,128)} %bitcast.26, s32[8,128]{1,0:T(8,128)} %bitcast.27), custom_call_target="tpu_custom_call" | custom-call | tf_op jit(solution)/shard_map/lower_tree/pallas_call | solution.py:386
  7.0 0.0 copy-start
  7.1 4.6 %collective-permute-start.2 = (f32[4,4,8,128]{3,2,1,0:T(8,128)S(1)}, f32[4,4,8,128]{3,2,1,0:T(8,128)S(1)}, u32[]{:S(2)}, u32[]{:S(2)}) collective-permute-start(f32[4,4,8,128]{3,2,1,0:T(8,128)S(1)} %get-tuple-element.15), channel_id=1, source_target_pairs={{0,96},{32,0},{64,32},{96,64},{1,97},{33,1},{65,33},{97,65},{2,98}... | collective-permute-start | bytes 196616 | tf_op jit(solution)/shard_map/ppermute | solution.py:423
  11.7 0.0 collective-permute-start.1
  11.7 0.7 %collective-permute-start = (f32[4,4,8,128]{3,2,1,0:T(8,128)S(1)}, f32[4,4,8,128]{3,2,1,0:T(8,128)S(1)}, u32[]{:S(2)}, u32[]{:S(2)}) collective-permute-start(f32[4,4,8,128]{3,2,1,0:T(8,128)S(1)} %get-tuple-element.17), channel_id=1, source_target_pairs={{0,32},{32,64},{64,96},{96,0},{1,33},{33,65},{65,97},{97,1},{2,34}... | collective-permute-start | bytes 196616 | tf_op jit(solution)/shard_map/ppermute | solution.py:423
  12.4 0.6 %collective-permute-done.2.three_ref = f32[4,4,8,128]{3,2,1,0:T(8,128)S(1)} collective-permute-done((f32[4,4,8,128]{3,2,1,0:T(8,128)S(1)}, f32[4,4,8,128]{3,2,1,0:T(8,128)S(1)}, u32[]{:S(2)}, u32[]{:S(2)}) %collective-permute-start.2) | collective-permute-done | bytes 65568 | tf_op jit(solution)/shard_map/ppermute | solution.py:423
  13.0 3.4 %collective-permute-done.1.two_ref = f32[4,4,8,128]{3,2,1,0:T(8,128)S(1)} collective-permute-done((f32[4,4,8,128]{3,2,1,0:T(8,128)S(1)}, f32[4,4,8,128]{3,2,1,0:T(8,128)S(1)}, u32[]{:S(2)}, u32[]{:S(2)}) %collective-permute-start.1) | collective-permute-done | bytes 65568 | tf_op jit(solution)/shard_map/ppermute | solution.py:423
  16.4 0.3 collective-permute-done.one_ref
  16.7 0.0 copy-done
  16.7 1.5 %upper_tree.1 = (f32[2,128]{1,0:T(2,128)}, f32[128,128]{1,0:T(8,128)S(1)}) custom-call(s32[2,1023]{1,0:T(2,128)S(1)} %bitcast.25, f32[4,4,8,128]{3,2,1,0:T(8,128)S(1)} %get-tuple-element.18.own_ref, f32[4,4,8,128]{3,2,1,0:T(8,128)S(1)} %collective-permute-done.one_ref, f32[4,4,8,128]{3,2,1,0:T(8,128)S(1)} %collective-permute-done.1.two_ref, ...), custom_call_target="tpu_custom_call" | custom-call | tf_op jit(solution)/shard_map/upper_tree/pallas_call | solution.py:424
  18.2 19.1 %all_to_all.11 = f32[128,1,128]{2,1,0:T(1,128)S(1)} all-to-all(f32[128,1,128]{2,1,0:T(1,128)S(1)} %bitcast.23), channel_id=1, replica_groups=mesh['cls'=4,'site'=32] {'cls','site'}, dimensions={0} | all-to-all | bytes 131072 | tf_op jit(solution)/shard_map/all_to_all | solution.py:433
  37.3 0.6 %last_sums.1 = (f32[1,1]{1,0:T(1,128)}, f32[1,1]{1,0:T(1,128)}) custom-call(f32[128,128]{1,0:T(8,128)S(1)} %bitcast.22), custom_call_target="tpu_custom_call" | custom-call | tf_op jit(solution)/shard_map/last_sums/pallas_call | solution.py:434
  (1 shorter events, 0.0 us)
Async XLA Ops:
  7.0 9.7 %copy-start = (s32[1023,2]{0,1:T(2,128)S(1)}, s32[1023,2]{0,1:T(2,128)}, u32[]{:S(2)}) copy-start(s32[1023,2]{0,1:T(2,128)} %param.8) | copy-start | bytes 24556
  7.1 6.0 %collective-permute-start.2 = (f32[4,4,8,128]{3,2,1,0:T(8,128)S(1)}, f32[4,4,8,128]{3,2,1,0:T(8,128)S(1)}, u32[]{:S(2)}, u32[]{:S(2)}) collective-permute-start(f32[4,4,8,128]{3,2,1,0:T(8,128)S(1)} %get-tuple-element.15), channel_id=1, source_target_pairs={{0,96},{32,0},{64,32},{96,64},{1,97},{33,1},{65,33},{97,65},{2,98}... | collective-permute-start | bytes 196616 | tf_op jit(solution)/shard_map/ppermute | solution.py:423
  11.7 4.7 %collective-permute-start.1 = (f32[4,4,8,128]{3,2,1,0:T(8,128)S(1)}, f32[4,4,8,128]{3,2,1,0:T(8,128)S(1)}, u32[]{:S(2)}, u32[]{:S(2)}) collective-permute-start(f32[4,4,8,128]{3,2,1,0:T(8,128)S(1)} %get-tuple-element.16), channel_id=1, source_target_pairs={{0,64},{32,96},{64,0},{96,32},{1,65},{33,97},{65,1},{97,33},{2,66}... | collective-permute-start | bytes 196616 | tf_op jit(solution)/shard_map/ppermute | solution.py:423
  11.7 5.0 %collective-permute-start = (f32[4,4,8,128]{3,2,1,0:T(8,128)S(1)}, f32[4,4,8,128]{3,2,1,0:T(8,128)S(1)}, u32[]{:S(2)}, u32[]{:S(2)}) collective-permute-start(f32[4,4,8,128]{3,2,1,0:T(8,128)S(1)} %get-tuple-element.17), channel_id=1, source_target_pairs={{0,32},{32,64},{64,96},{96,0},{1,33},{33,65},{65,97},{97,1},{2,34}... | collective-permute-start | bytes 196616 | tf_op jit(solution)/shard_map/ppermute | solution.py:423

commit v7 on v6

--- a/solution.py
+++ b/solution.py
@@ -32,6 +32,12 @@
     value = jnp.where(selector == 1, options[1], options[0])
     value = jnp.where(selector == 2, options[2], value)
     return jnp.where(selector == 3, options[3], value)
+
+
+def pick(masks, options):
+    value = jnp.where(masks[1], options[1], options[0])
+    value = jnp.where(masks[2], options[2], value)
+    return jnp.where(masks[3], options[3], value)
 
 
 def lanes_of(rows, places):
@@ -50,10 +56,10 @@
         pltpu.make_async_copy(source, target, sems.at[4 + k])
         for k, (source, target) in enumerate(
             (
+                (child_hbm, child_vec),
+                (lengths_hbm, lengths_ref),
                 (freq_hbm, freq_ref),
                 (weight_hbm, weight_ref),
-                (lengths_hbm, lengths_ref),
-                (child_hbm, child_vec),
                 (counts_hbm, counts_ref),
             )
         )
@@ -68,7 +74,20 @@
     ]
     for load in loads:
         load.start()
-    for load in small:
+    small[0].wait()
+    half = lax.shift_right_logical(group, 1)
+
+    def block(ref, start):
+        return ref[:, pl.ds(pl.multiple_of(start, 128), 128)]
+
+    local = block(child_vec, 128 * group) - 256 * group
+    spot_vec[0:2] = lax.shift_left(lax.shift_right_logical(local, 3), 6) + lax.bitwise_and(local, 7)
+    spot_vec[2:4] = block(child_vec, 512 + 128 * half) - (1024 + 128 * group)
+    spot_vec[4:6] = child_vec[:, 768:896] - (1536 + 128 * half)
+    spot_vec[6:8] = jnp.concatenate([child_vec[:, 896:1023], jnp.zeros((2, 1), jnp.int32)], axis=1)
+    spot_copy = pltpu.make_async_copy(spot_vec, spot_ref, sems.at[9])
+    spot_copy.start()
+    for load in small[1:]:
         load.wait()
 
     lane = lax.broadcasted_iota(jnp.int32, TILE, 1)
@@ -93,18 +112,6 @@
         total = total + part
         rate_vec[:, 128 * k : 128 * k + 128] = jnp.exp(beta_rows * part) - 1.0
 
-    half = lax.shift_right_logical(group, 1)
-
-    def block(ref, start):
-        return ref[:, pl.ds(pl.multiple_of(start, 128), 128)]
-
-    local = block(child_vec, 128 * group) - 256 * group
-    spot_vec[0:2] = lax.shift_left(lax.shift_right_logical(local, 3), 6) + lax.bitwise_and(local, 7)
-    spot_vec[2:4] = block(child_vec, 512 + 128 * half) - (1024 + 128 * group)
-    spot_vec[4:6] = child_vec[:, 768:896] - (1536 + 128 * half)
-    spot_vec[6:8] = jnp.concatenate([child_vec[:, 896:1023], jnp.zeros((2, 1), jnp.int32)], axis=1)
-    spot_copy = pltpu.make_async_copy(spot_vec, spot_ref, sems.at[9])
-    spot_copy.start()
     step_vec[0:4] = block(rate_vec, 1536 + 128 * half)
     step_vec[4:8] = rate_vec[:, 1792:1920]
     step_vec[8:12] = rate_vec[:, 1920:2048]
@@ -166,8 +173,6 @@
     quarter = counts_ref[pl.ds(2 * group, 2), :].astype(FLOAT)
     top_ref[TOP_WEIGHT] = jnp.concatenate([quarter, quarter, quarter, quarter], axis=0)
     spot_copy.wait()
-    step_copy.wait()
-    rate4_copy.wait()
 
     def pairs_of(n):
         tops = [spot_ref[4 + side, 32 * group + n] for side in range(2)]
@@ -199,22 +204,14 @@
 
     def chosen_pair(pair):
         left, right = codes_of(pair)
-        left_odd = lax.bitwise_and(left, 1) == 1
-        right_odd = lax.bitwise_and(right, 1) == 1
-        left_high = left >= 2
-        right_high = right >= 2
         same = left == right
         left_is = [left == i for i in range(STATES)]
         right_is = [right == i for i in range(STATES)]
         found = []
         for c in range(CLS):
             pi = [pi_ref[c, i] for i in range(STATES)]
-            left_pi = jnp.where(
-                left_high, jnp.where(left_odd, pi[3], pi[2]), jnp.where(left_odd, pi[1], pi[0])
-            )
-            right_pi = jnp.where(
-                right_high, jnp.where(right_odd, pi[3], pi[2]), jnp.where(right_odd, pi[1], pi[0])
-            )
+            left_pi = pick(left_is, pi)
+            right_pi = pick(right_is, pi)
             left_step = rate4_ref[4 + c, pair] * left_pi
             right_step = rate4_ref[c, pair] * right_pi
             base = rate4_ref[8 + c, pair] * (left_pi * right_pi)
@@ -262,8 +259,8 @@
             log_ref[n, c] = jnp.log(average)
 
     def small_trees(m, _):
-        for u in range(2):
-            small_tree(m, u)
+        for u in range(8):
+            small_tree(4 * m + u // 2, u % 2)
         return 0
 
     def tail_pair(at):
@@ -298,13 +295,17 @@
                     out_ref[lax.bitwise_and(q - group, 3), j, v, 2 * c : 2 * c + 2, :] = sent[v][2 * q : 2 * q + 2, :]
         return 0
 
+    step_copy.wait()
+    rate4_copy.wait()
     for load in loads:
         load.wait()
-    lax.fori_loop(0, 16, small_trees, 0)
+    lax.fori_loop(0, 4, small_trees, 0)
     lax.fori_loop(0, 4, clade, 0)
 
 
-def upper_kernel(child_ref, own_ref, one_ref, two_ref, three_ref, top_ref, site_ref, part_ref, node_ref):
+def upper_kernel(
+    child_ref, own_ref, one_ref, two_ref, three_ref, top_ref, site_hbm, part_ref, node_ref, site_ref, sem
+):
     group = lax.axis_index("cls")
     pi = [top_ref[TOP_PI + i] for i in range(STATES)]
     scale = top_ref[TOP_CONST]
@@ -345,6 +346,8 @@
     mass = mass + pltpu.roll(mass, 4, 0)
     total = top + jnp.log(mass)
     site_ref[...] = total[0:2] * (1.0 / 1024.0)
+    site_copy = pltpu.make_async_copy(site_ref, site_hbm, sem)
+    site_copy.start()
     weight = top_ref[TOP_WEIGHT]
     classes = weight * (share / mass)
     row = lax.broadcasted_iota(jnp.int32, TILE, 0)
@@ -359,9 +362,10 @@
     line = jnp.sum(line, axis=0, keepdims=True)
     for k in range(16):
         part_ref[8 * k : 8 * k + 8, :] = jnp.broadcast_to(line, TILE)
-
-
-def last_kernel(every_ref, own_ref, mean_ref):
+    site_copy.wait()
+
+
+def last_kernel(every_ref, own_hbm, mean_hbm, own_ref, mean_ref, sems):
     group = lax.axis_index("cls")
     sums = every_ref[0:8, :]
     for k in range(1, 16):
@@ -375,6 +379,12 @@
     count = entry(5)
     own_ref[...] = entry(group) / count
     mean_ref[...] = entry(4) / (count * 1024.0)
+    own_copy = pltpu.make_async_copy(own_ref, own_hbm, sems.at[0])
+    mean_copy = pltpu.make_async_copy(mean_ref, mean_hbm, sems.at[1])
+    own_copy.start()
+    mean_copy.start()
+    own_copy.wait()
+    mean_copy.wait()
 
 
 def per_device(tip_codes, counts, children, lengths, frequencies, weights):
@@ -425,8 +435,12 @@
         upper_kernel,
         out_shape=(jax.ShapeDtypeStruct((2, 128), FLOAT), pltpu.VMEM((128, 128), FLOAT)),
         in_specs=[smem] + [vmem] * 5,
-        out_specs=(vmem, vmem),
-        scratch_shapes=[pltpu.VMEM((32, STATES, 8, 128), FLOAT)],
+        out_specs=(hbm, vmem),
+        scratch_shapes=[
+            pltpu.VMEM((32, STATES, 8, 128), FLOAT),
+            pltpu.VMEM((2, 128), FLOAT),
+            pltpu.SemaphoreType.DMA,
+        ],
         compiler_params=pltpu.CompilerParams(vmem_limit_bytes=16 * 1024 * 1024),
         name="upper_tree",
     )(child_rows, *pieces, top)
@@ -435,7 +449,12 @@
         last_kernel,
         out_shape=(jax.ShapeDtypeStruct((1, 1), FLOAT), jax.ShapeDtypeStruct((1, 1), FLOAT)),
         in_specs=[vmem],
-        out_specs=(vmem, vmem),
+        out_specs=(hbm, hbm),
+        scratch_shapes=[
+            pltpu.VMEM((1, 1), FLOAT),
+            pltpu.VMEM((1, 1), FLOAT),
+            pltpu.SemaphoreType.DMA((2,)),
+        ],
         compiler_params=pltpu.CompilerParams(vmem_limit_bytes=16 * 1024 * 1024),
         name="last_sums",
     )(every)

time: 38.1 us -> 36.8 us (0.966)
  Pallas kernels: 8.48 us -> 7.13 us
    pallas_call x1, Pallas kernels: 6.37 us -> 4.99 us  [per_device(): pl.pallas_call(lower_kernel, out_shape=(pltpu.VMEM((4, 4, 4, 8, 128), FLO...]
where the time goes in v7:
time: 36.8 us; the launch traced here: 36.6 us
  blocking collectives  19.1 us (52%)
  Pallas kernels  7.13 us (19%)
  starting transfers between devices  5.34 us (15%)
  waiting for transfers between devices  4.33 us (12%)
  between operations  0.67 us (2%)
    all_to_all x1, blocking collectives, per_device(): lax.all_to_all(part, ('cls', 'site'), split_axis=0, concat_axis=0, tiled=...  19.1 us
    ppermute x3, starting transfers between devices, per_device(): lax.ppermute(ours[hop], 'cls', [(k, (k + hop) % 4) for k in range(4)])  5.34 us
    pallas_call x1, Pallas kernels, per_device(): pl.pallas_call(lower_kernel, out_shape=(pltpu.VMEM((4, 4, 4, 8, 128), FLO...  4.99 us
    ppermute x3, waiting for transfers between devices, per_device(): lax.ppermute(ours[hop], 'cls', [(k, (k + hop) % 4) for k in range(4)])  4.33 us
    pallas_call x1, Pallas kernels, per_device(): pl.pallas_call(upper_kernel, out_shape=(jax.ShapeDtypeStruct((2, 128), FL...  1.5 us
  transfers between devices with their start and end apart: 3, of which 3 were waited for; matrix products, arithmetic and copies ran while one was open for 0% of the time, Pallas kernels for 0%

profile of v7, /device:TPU:1, one launch (start us, length us, event | category | flops | bytes accessed | tf_op | source)
XLA Modules:
  0.0 36.6 jit_solution(6032285968131091310)
XLA Ops:
  0.6 5.0 %lower_tree.1 = (f32[4,4,4,8,128]{4,3,2,1,0:T(8,128)S(1)}, f32[36,8,128]{2,1,0:T(8,128)S(1)}) custom-call(s32[2,1023]{1,0:T(2,128)} %bitcast.24, f32[4,4]{1,0:T(4,128)} %freq_hbm.1, f32[4]{0:T(128)} %weight_hbm.1, f32[4,2046]{1,0:T(4,128)} %lengths_hbm.1, s32[2048,128]{1,0:T(8,128)} %bitcast.26, s32[8,128]{1,0:T(8,128)} %bitcast.27), custom_call_target="tpu_custom_call" | custom-call | tf_op jit(solution)/shard_map/lower_tree/pallas_call | solution.py:396
  5.7 0.0 copy-start
  5.7 4.6 %collective-permute-start.2 = (f32[4,4,8,128]{3,2,1,0:T(8,128)S(1)}, f32[4,4,8,128]{3,2,1,0:T(8,128)S(1)}, u32[]{:S(2)}, u32[]{:S(2)}) collective-permute-start(f32[4,4,8,128]{3,2,1,0:T(8,128)S(1)} %get-tuple-element.15), channel_id=1, source_target_pairs={{0,96},{32,0},{64,32},{96,64},{1,97},{33,1},{65,33},{97,65},{2,98}... | collective-permute-start | bytes 196616 | tf_op jit(solution)/shard_map/ppermute | solution.py:433
  10.3 0.0 collective-permute-start.1
  10.3 0.7 %collective-permute-start = (f32[4,4,8,128]{3,2,1,0:T(8,128)S(1)}, f32[4,4,8,128]{3,2,1,0:T(8,128)S(1)}, u32[]{:S(2)}, u32[]{:S(2)}) collective-permute-start(f32[4,4,8,128]{3,2,1,0:T(8,128)S(1)} %get-tuple-element.17), channel_id=1, source_target_pairs={{0,32},{32,64},{64,96},{96,0},{1,33},{33,65},{65,97},{97,1},{2,34}... | collective-permute-start | bytes 196616 | tf_op jit(solution)/shard_map/ppermute | solution.py:433
  11.0 0.6 %collective-permute-done.2.three_ref = f32[4,4,8,128]{3,2,1,0:T(8,128)S(1)} collective-permute-done((f32[4,4,8,128]{3,2,1,0:T(8,128)S(1)}, f32[4,4,8,128]{3,2,1,0:T(8,128)S(1)}, u32[]{:S(2)}, u32[]{:S(2)}) %collective-permute-start.2) | collective-permute-done | bytes 65568 | tf_op jit(solution)/shard_map/ppermute | solution.py:433
  11.6 3.4 %collective-permute-done.1.two_ref = f32[4,4,8,128]{3,2,1,0:T(8,128)S(1)} collective-permute-done((f32[4,4,8,128]{3,2,1,0:T(8,128)S(1)}, f32[4,4,8,128]{3,2,1,0:T(8,128)S(1)}, u32[]{:S(2)}, u32[]{:S(2)}) %collective-permute-start.1) | collective-permute-done | bytes 65568 | tf_op jit(solution)/shard_map/ppermute | solution.py:433
  15.0 0.3 collective-permute-done.one_ref
  15.3 0.0 copy-done
  15.3 1.5 %upper_tree.1 = (f32[2,128]{1,0:T(2,128)}, f32[128,128]{1,0:T(8,128)S(1)}) custom-call(s32[2,1023]{1,0:T(2,128)S(1)} %bitcast.25, f32[4,4,8,128]{3,2,1,0:T(8,128)S(1)} %get-tuple-element.18.own_ref, f32[4,4,8,128]{3,2,1,0:T(8,128)S(1)} %collective-permute-done.one_ref, f32[4,4,8,128]{3,2,1,0:T(8,128)S(1)} %collective-permute-done.1.two_ref, ...), custom_call_target="tpu_custom_call" | custom-call | tf_op jit(solution)/shard_map/upper_tree/pallas_call | solution.py:434
  16.9 19.1 %all_to_all.11 = f32[128,1,128]{2,1,0:T(1,128)S(1)} all-to-all(f32[128,1,128]{2,1,0:T(1,128)S(1)} %bitcast.23), channel_id=1, replica_groups=mesh['cls'=4,'site'=32] {'cls','site'}, dimensions={0} | all-to-all | bytes 131072 | tf_op jit(solution)/shard_map/all_to_all | solution.py:447
  36.0 0.6 %last_sums.1 = (f32[1,1]{1,0:T(1,128)}, f32[1,1]{1,0:T(1,128)}) custom-call(f32[128,128]{1,0:T(8,128)S(1)} %bitcast.22), custom_call_target="tpu_custom_call" | custom-call | tf_op jit(solution)/shard_map/last_sums/pallas_call | solution.py:448
  (1 shorter events, 0.0 us)
Async XLA Ops:
  5.7 9.7 %copy-start = (s32[1023,2]{0,1:T(2,128)S(1)}, s32[1023,2]{0,1:T(2,128)}, u32[]{:S(2)}) copy-start(s32[1023,2]{0,1:T(2,128)} %param.8) | copy-start | bytes 24556
  5.7 6.0 %collective-permute-start.2 = (f32[4,4,8,128]{3,2,1,0:T(8,128)S(1)}, f32[4,4,8,128]{3,2,1,0:T(8,128)S(1)}, u32[]{:S(2)}, u32[]{:S(2)}) collective-permute-start(f32[4,4,8,128]{3,2,1,0:T(8,128)S(1)} %get-tuple-element.15), channel_id=1, source_target_pairs={{0,96},{32,0},{64,32},{96,64},{1,97},{33,1},{65,33},{97,65},{2,98}... | collective-permute-start | bytes 196616 | tf_op jit(solution)/shard_map/ppermute | solution.py:433
  10.3 4.7 %collective-permute-start.1 = (f32[4,4,8,128]{3,2,1,0:T(8,128)S(1)}, f32[4,4,8,128]{3,2,1,0:T(8,128)S(1)}, u32[]{:S(2)}, u32[]{:S(2)}) collective-permute-start(f32[4,4,8,128]{3,2,1,0:T(8,128)S(1)} %get-tuple-element.16), channel_id=1, source_target_pairs={{0,64},{32,96},{64,0},{96,32},{1,65},{33,97},{65,1},{97,33},{2,66}... | collective-permute-start | bytes 196616 | tf_op jit(solution)/shard_map/ppermute | solution.py:433
  10.3 5.0 %collective-permute-start = (f32[4,4,8,128]{3,2,1,0:T(8,128)S(1)}, f32[4,4,8,128]{3,2,1,0:T(8,128)S(1)}, u32[]{:S(2)}, u32[]{:S(2)}) collective-permute-start(f32[4,4,8,128]{3,2,1,0:T(8,128)S(1)} %get-tuple-element.17), channel_id=1, source_target_pairs={{0,32},{32,64},{64,96},{96,0},{1,33},{33,65},{65,97},{97,1},{2,34}... | collective-permute-start | bytes 196616 | tf_op jit(solution)/shard_map/ppermute | solution.py:433

commit v8 on v7

--- a/solution.py
+++ b/solution.py
@@ -46,7 +46,7 @@
 
 def lower_kernel(
     child_hbm, freq_hbm, weight_hbm, lengths_hbm, codes_hbm, counts_hbm,
-    out_ref, top_ref,
+    out_ref, top_ref, place_ref,
     child_vec, freq_ref, weight_ref, lengths_ref, codes_ref, counts_ref, rate_vec,
     spot_vec, spot_ref, step_vec, step_ref,
     pi_ref, pattern_ref, factor_ref, table_ref, rate4_vec, rate4_ref, mid_ref, log_ref, sems,
@@ -173,6 +173,10 @@
     quarter = counts_ref[pl.ds(2 * group, 2), :].astype(FLOAT)
     top_ref[TOP_WEIGHT] = jnp.concatenate([quarter, quarter, quarter, quarter], axis=0)
     spot_copy.wait()
+
+    for k in range(15):
+        for side in range(2):
+            place_ref[2 * k + side] = spot_ref[6 + side, 112 + k] - 2016
 
     def pairs_of(n):
         tops = [spot_ref[4 + side, 32 * group + n] for side in range(2)]
@@ -304,7 +308,7 @@
 
 
 def upper_kernel(
-    child_ref, own_ref, one_ref, two_ref, three_ref, top_ref, site_hbm, part_ref, node_ref, site_ref, sem
+    place_ref, own_ref, one_ref, two_ref, three_ref, top_ref, site_ref, part_ref, node_ref
 ):
     group = lax.axis_index("cls")
     pi = [top_ref[TOP_PI + i] for i in range(STATES)]
@@ -321,10 +325,9 @@
             node_ref[source + j, 3] = step + 1.0
     at = 16
     for level, count in ((6, 8), (7, 4), (8, 2), (9, 1)):
-        begin = 1024 - (1024 >> level)
         for k in range(count):
-            left = child_ref[0, begin + k] - 2016
-            right = child_ref[1, begin + k] - 2016
+            left = place_ref[2 * (at - 16)]
+            right = place_ref[2 * (at - 16) + 1]
             joined = [node_ref[left, i] * node_ref[right, i] for i in range(STATES)]
             average = mean_state(pi, joined)
             if level == 6:
@@ -346,8 +349,6 @@
     mass = mass + pltpu.roll(mass, 4, 0)
     total = top + jnp.log(mass)
     site_ref[...] = total[0:2] * (1.0 / 1024.0)
-    site_copy = pltpu.make_async_copy(site_ref, site_hbm, sem)
-    site_copy.start()
     weight = top_ref[TOP_WEIGHT]
     classes = weight * (share / mass)
     row = lax.broadcasted_iota(jnp.int32, TILE, 0)
@@ -362,10 +363,11 @@
     line = jnp.sum(line, axis=0, keepdims=True)
     for k in range(16):
         part_ref[8 * k : 8 * k + 8, :] = jnp.broadcast_to(line, TILE)
-    site_copy.wait()
-
-
-def last_kernel(every_ref, own_hbm, mean_hbm, own_ref, mean_ref, sems):
+
+
+def last_kernel(every_ref, site_ref, own_hbm, mean_hbm, site_hbm, own_ref, mean_ref, sems):
+    site_copy = pltpu.make_async_copy(site_ref, site_hbm, sems.at[2])
+    site_copy.start()
     group = lax.axis_index("cls")
     sums = every_ref[0:8, :]
     for k in range(1, 16):
@@ -385,6 +387,7 @@
     mean_copy.start()
     own_copy.wait()
     mean_copy.wait()
+    site_copy.wait()
 
 
 def per_device(tip_codes, counts, children, lengths, frequencies, weights):
@@ -393,11 +396,11 @@
     smem = pl.BlockSpec(memory_space=SMEM)
     vmem = pl.BlockSpec(memory_space=VMEM)
     hbm = pl.BlockSpec(memory_space=pltpu.MemorySpace.HBM)
-    ours, top = pl.pallas_call(
+    ours, top, places = pl.pallas_call(
         lower_kernel,
-        out_shape=(pltpu.VMEM((4, 4, 4, 8, 128), FLOAT), pltpu.VMEM((TOP_ROWS, 8, 128), FLOAT)),
+        out_shape=(pltpu.VMEM((4, 4, 4, 8, 128), FLOAT), pltpu.VMEM((TOP_ROWS, 8, 128), FLOAT), pltpu.SMEM((32,), jnp.int32)),
         in_specs=[hbm] * 6,
-        out_specs=(vmem, vmem),
+        out_specs=(vmem, vmem, smem),
         scratch_shapes=[
             pltpu.VMEM((2, 1023), jnp.int32),
             pltpu.SMEM((4, 4), FLOAT),
@@ -433,31 +436,27 @@
         pieces.append(lax.ppermute(ours[hop], "cls", [(k, (k + hop) % 4) for k in range(4)]))
     site, part = pl.pallas_call(
         upper_kernel,
-        out_shape=(jax.ShapeDtypeStruct((2, 128), FLOAT), pltpu.VMEM((128, 128), FLOAT)),
+        out_shape=(pltpu.VMEM((2, 128), FLOAT), pltpu.VMEM((128, 128), FLOAT)),
         in_specs=[smem] + [vmem] * 5,
-        out_specs=(hbm, vmem),
-        scratch_shapes=[
-            pltpu.VMEM((32, STATES, 8, 128), FLOAT),
-            pltpu.VMEM((2, 128), FLOAT),
-            pltpu.SemaphoreType.DMA,
-        ],
+        out_specs=(vmem, vmem),
+        scratch_shapes=[pltpu.VMEM((32, STATES, 8, 128), FLOAT)],
         compiler_params=pltpu.CompilerParams(vmem_limit_bytes=16 * 1024 * 1024),
         name="upper_tree",
-    )(child_rows, *pieces, top)
+    )(places, *pieces, top)
     every = lax.all_to_all(part, ("cls", "site"), split_axis=0, concat_axis=0, tiled=True)
-    own, mean = pl.pallas_call(
+    own, mean, site = pl.pallas_call(
         last_kernel,
-        out_shape=(jax.ShapeDtypeStruct((1, 1), FLOAT), jax.ShapeDtypeStruct((1, 1), FLOAT)),
-        in_specs=[vmem],
-        out_specs=(hbm, hbm),
+        out_shape=tuple(jax.ShapeDtypeStruct(shape, FLOAT) for shape in ((1, 1), (1, 1), (2, 128))),
+        in_specs=[vmem, vmem],
+        out_specs=(hbm, hbm, hbm),
         scratch_shapes=[
             pltpu.VMEM((1, 1), FLOAT),
             pltpu.VMEM((1, 1), FLOAT),
-            pltpu.SemaphoreType.DMA((2,)),
+            pltpu.SemaphoreType.DMA((3,)),
         ],
         compiler_params=pltpu.CompilerParams(vmem_limit_bytes=16 * 1024 * 1024),
         name="last_sums",
-    )(every)
+    )(every, site)
     return site.reshape(1, 256), own.reshape(1), mean.reshape(())
 
 

time: 36.8 us -> 35.7 us (0.970)
  Pallas kernels: 7.13 us -> 6.02 us
    pallas_call x2, Pallas kernels: 2.14 us -> 1.01 us  [the longest x1 0.65 us: per_device(): pl.pallas_call(last_kernel, out_shape=tuple((jax.ShapeDtypeStruct(shape,...]
where the time goes in v8:
time: 35.7 us; the launch traced here: 35.5 us
  blocking collectives  19.1 us (54%)
  Pallas kernels  6.02 us (17%)
  starting transfers between devices  5.35 us (15%)
  waiting for transfers between devices  4.33 us (12%)
  between operations  0.66 us (2%)
    all_to_all x1, blocking collectives, per_device(): lax.all_to_all(part, ('cls', 'site'), split_axis=0, concat_axis=0, tiled=...  19.1 us
    ppermute x3, starting transfers between devices, per_device(): lax.ppermute(ours[hop], 'cls', [(k, (k + hop) % 4) for k in range(4)])  5.35 us
    pallas_call x1, Pallas kernels, per_device(): pl.pallas_call(lower_kernel, out_shape=(pltpu.VMEM((4, 4, 4, 8, 128), FLO...  5.02 us
    ppermute x3, waiting for transfers between devices, per_device(): lax.ppermute(ours[hop], 'cls', [(k, (k + hop) % 4) for k in range(4)])  4.33 us
  transfers between devices with their start and end apart: 3, of which 3 were waited for; matrix products, arithmetic and copies ran while one was open for 0% of the time, Pallas kernels for 0%

profile of v8, /device:TPU:1, one launch (start us, length us, event | category | flops | bytes accessed | tf_op | source)
XLA Modules:
  0.0 35.5 jit_solution(15218746832949487139)
XLA Ops:
  0.6 5.0 %lower_tree.1 = (f32[4,4,4,8,128]{4,3,2,1,0:T(8,128)S(1)}, f32[36,8,128]{2,1,0:T(8,128)S(1)}, s32[32]{0:T(128)S(4)}) custom-call(s32[2,1023]{1,0:T(2,128)} %bitcast.25, f32[4,4]{1,0:T(4,128)} %freq_hbm.1, f32[4]{0:T(128)} %weight_hbm.1, f32[4,2046]{1,0:T(4,128)} %lengths_hbm.1, s32[2048,128]{1,0:T(8,128)} %bitcast.24, s32[8,128]{1,0:T(8,128)} %bitcast.26), custom_call_target="tpu_custom_call" | custom-call | tf_op jit(solution)/shard_map/lower_tree/pallas_call | solution.py:399
  5.7 4.6 %collective-permute-start.2 = (f32[4,4,8,128]{3,2,1,0:T(8,128)S(1)}, f32[4,4,8,128]{3,2,1,0:T(8,128)S(1)}, u32[]{:S(2)}, u32[]{:S(2)}) collective-permute-start(f32[4,4,8,128]{3,2,1,0:T(8,128)S(1)} %get-tuple-element.19), channel_id=1, source_target_pairs={{0,96},{32,0},{64,32},{96,64},{1,97},{33,1},{65,33},{97,65},{2,98}... | collective-permute-start | bytes 196616 | tf_op jit(solution)/shard_map/ppermute | solution.py:436
  10.3 0.0 collective-permute-start.1
  10.3 0.7 %collective-permute-start = (f32[4,4,8,128]{3,2,1,0:T(8,128)S(1)}, f32[4,4,8,128]{3,2,1,0:T(8,128)S(1)}, u32[]{:S(2)}, u32[]{:S(2)}) collective-permute-start(f32[4,4,8,128]{3,2,1,0:T(8,128)S(1)} %get-tuple-element.21), channel_id=1, source_target_pairs={{0,32},{32,64},{64,96},{96,0},{1,33},{33,65},{65,97},{97,1},{2,34}... | collective-permute-start | bytes 196616 | tf_op jit(solution)/shard_map/ppermute | solution.py:436
  11.0 0.6 %collective-permute-done.2.three_ref = f32[4,4,8,128]{3,2,1,0:T(8,128)S(1)} collective-permute-done((f32[4,4,8,128]{3,2,1,0:T(8,128)S(1)}, f32[4,4,8,128]{3,2,1,0:T(8,128)S(1)}, u32[]{:S(2)}, u32[]{:S(2)}) %collective-permute-start.2) | collective-permute-done | bytes 65568 | tf_op jit(solution)/shard_map/ppermute | solution.py:436
  11.7 3.4 %collective-permute-done.1.two_ref = f32[4,4,8,128]{3,2,1,0:T(8,128)S(1)} collective-permute-done((f32[4,4,8,128]{3,2,1,0:T(8,128)S(1)}, f32[4,4,8,128]{3,2,1,0:T(8,128)S(1)}, u32[]{:S(2)}, u32[]{:S(2)}) %collective-permute-start.1) | collective-permute-done | bytes 65568 | tf_op jit(solution)/shard_map/ppermute | solution.py:436
  15.1 0.3 collective-permute-done.one_ref
  15.4 0.4 %upper_tree.1 = (f32[2,128]{1,0:T(2,128)S(1)}, f32[128,128]{1,0:T(8,128)S(1)}) custom-call(s32[32]{0:T(128)S(4)} %get-tuple-element.11.place_ref, f32[4,4,8,128]{3,2,1,0:T(8,128)S(1)} %get-tuple-element.22.own_ref, f32[4,4,8,128]{3,2,1,0:T(8,128)S(1)} %collective-permute-done.one_ref, f32[4,4,8,128]{3,2,1,0:T(8,128)S(1)} %collective-permute-done.1.two_ref, ...), custom_call_target="tpu_custom_call" | custom-call | tf_op jit(solution)/shard_map/upper_tree/pallas_call | solution.py:437
  15.7 19.1 %all_to_all.11 = f32[128,1,128]{2,1,0:T(1,128)S(1)} all-to-all(f32[128,1,128]{2,1,0:T(1,128)S(1)} %bitcast.23), channel_id=1, replica_groups=mesh['cls'=4,'site'=32] {'cls','site'}, dimensions={0} | all-to-all | bytes 131072 | tf_op jit(solution)/shard_map/all_to_all | solution.py:446
  34.9 0.6 %last_sums.1 = (f32[1,1]{1,0:T(1,128)}, f32[1,1]{1,0:T(1,128)}, f32[2,128]{1,0:T(2,128)}) custom-call(f32[128,128]{1,0:T(8,128)S(1)} %bitcast.22, f32[2,128]{1,0:T(2,128)S(1)} %get-tuple-element.15.site_ref), custom_call_target="tpu_custom_call" | custom-call | tf_op jit(solution)/shard_map/last_sums/pallas_call | solution.py:447
  (1 shorter events, 0.0 us)
Async XLA Ops:
  5.7 6.0 %collective-permute-start.2 = (f32[4,4,8,128]{3,2,1,0:T(8,128)S(1)}, f32[4,4,8,128]{3,2,1,0:T(8,128)S(1)}, u32[]{:S(2)}, u32[]{:S(2)}) collective-permute-start(f32[4,4,8,128]{3,2,1,0:T(8,128)S(1)} %get-tuple-element.19), channel_id=1, source_target_pairs={{0,96},{32,0},{64,32},{96,64},{1,97},{33,1},{65,33},{97,65},{2,98}... | collective-permute-start | bytes 196616 | tf_op jit(solution)/shard_map/ppermute | solution.py:436
  10.3 4.7 %collective-permute-start.1 = (f32[4,4,8,128]{3,2,1,0:T(8,128)S(1)}, f32[4,4,8,128]{3,2,1,0:T(8,128)S(1)}, u32[]{:S(2)}, u32[]{:S(2)}) collective-permute-start(f32[4,4,8,128]{3,2,1,0:T(8,128)S(1)} %get-tuple-element.20), channel_id=1, source_target_pairs={{0,64},{32,96},{64,0},{96,32},{1,65},{33,97},{65,1},{97,33},{2,66}... | collective-permute-start | bytes 196616 | tf_op jit(solution)/shard_map/ppermute | solution.py:436
  10.3 5.0 %collective-permute-start = (f32[4,4,8,128]{3,2,1,0:T(8,128)S(1)}, f32[4,4,8,128]{3,2,1,0:T(8,128)S(1)}, u32[]{:S(2)}, u32[]{:S(2)}) collective-permute-start(f32[4,4,8,128]{3,2,1,0:T(8,128)S(1)} %get-tuple-element.21), channel_id=1, source_target_pairs={{0,32},{32,64},{64,96},{96,0},{1,33},{33,65},{65,97},{97,1},{2,34}... | collective-permute-start | bytes 196616 | tf_op jit(solution)/shard_map/ppermute | solution.py:436

commit v9 on v8

--- a/solution.py
+++ b/solution.py
@@ -19,6 +19,10 @@
     return (pi[0] * values[0] + pi[1] * values[1]) + (pi[2] * values[2] + pi[3] * values[3])
 
 
+def mean_by_last(ratios, values):
+    return (ratios[0] * values[0] + ratios[1] * values[1]) + (ratios[2] * values[2] + values[3])
+
+
 def moved(values, rate, average):
     step = rate * average
     return [value + step for value in values]
@@ -41,7 +45,19 @@
 
 
 def lanes_of(rows, places):
-    return jnp.take_along_axis(rows, places, axis=1, mode="promise_in_bounds")
+    return lax.gather(
+        rows,
+        places[..., None],
+        lax.GatherDimensionNumbers(
+            offset_dims=(),
+            collapsed_slice_dims=(1,),
+            start_index_map=(1,),
+            operand_batching_dims=(0,),
+            start_indices_batching_dims=(0,),
+        ),
+        slice_sizes=(1, 1),
+        mode=lax.GatherScatterMode.PROMISE_IN_BOUNDS,
+    )
 
 
 def lower_kernel(
@@ -49,7 +65,7 @@
     out_ref, top_ref, place_ref,
     child_vec, freq_ref, weight_ref, lengths_ref, codes_ref, counts_ref, rate_vec,
     spot_vec, spot_ref, step_vec, step_ref,
-    pi_ref, pattern_ref, factor_ref, table_ref, rate4_vec, rate4_ref, mid_ref, log_ref, sems,
+    pi_ref, ratio_ref, pattern_ref, factor_ref, table_ref, rate4_vec, rate4_ref, mid_ref, log_ref, sems,
 ):
     group = lax.axis_index("cls")
     small = [
@@ -102,6 +118,8 @@
         betas.append(1.0 / (1.0 - mean_state(uniform[c], uniform[c])))
         for i in range(STATES):
             pi_ref[c, i] = uniform[c][i]
+        for i in range(3):
+            ratio_ref[c, i] = uniform[c][i] / uniform[c][3]
     beta_rows = choose(by_class, betas)[:4]
     total = jnp.zeros((4, 128), FLOAT)
     for k in range(16):
@@ -112,9 +130,10 @@
         total = total + part
         rate_vec[:, 128 * k : 128 * k + 128] = jnp.exp(beta_rows * part) - 1.0
 
-    step_vec[0:4] = block(rate_vec, 1536 + 128 * half)
-    step_vec[4:8] = rate_vec[:, 1792:1920]
-    step_vec[8:12] = rate_vec[:, 1920:2048]
+    last_pi = choose(by_class, [uniform[c][3] for c in range(CLS)])[:4]
+    step_vec[0:4] = block(rate_vec, 1536 + 128 * half) * last_pi
+    step_vec[4:8] = rate_vec[:, 1792:1920] * last_pi
+    step_vec[8:12] = rate_vec[:, 1920:2048] * last_pi
     step_vec[12:16] = jnp.zeros((4, 128), FLOAT)
     step_copy = pltpu.make_async_copy(step_vec, step_ref, sems.at[10])
     step_copy.start()
@@ -248,14 +267,14 @@
             chosen = chosen_pair(pairs[2 * h + 1])
             parts = []
             for c in range(CLS):
-                pi = [pi_ref[c, i] for i in range(STATES)]
+                ratios = [ratio_ref[c, i] for i in range(3)]
                 values = [looked[i][c] * chosen[c][i] for i in range(STATES)]
-                parts.append(moved(values, step_ref[c, tops[h]], mean_state(pi, values)))
+                parts.append(moved(values, step_ref[c, tops[h]], mean_by_last(ratios, values)))
             halves.append(parts)
         for c in range(CLS):
-            pi = [pi_ref[c, i] for i in range(STATES)]
+            ratios = [ratio_ref[c, i] for i in range(3)]
             values = product(halves[0][c], halves[1][c])
-            average = mean_state(pi, values)
+            average = mean_by_last(ratios, values)
             inverse = 1.0 / average
             own_rate = step_ref[4 + c, 32 * group + n]
             for i in range(STATES):
@@ -270,12 +289,16 @@
     def tail_pair(at):
         return [spot_ref[6 + side, at] for side in range(2)]
 
-    def clade(j, _):
+    def send(at, c, value):
+        for q in range(4):
+            out_ref[lax.bitwise_and(q - group, 3), at, 2 * c : 2 * c + 2, :] = value[2 * q : 2 * q + 2, :]
+
+    def clade(j, totals):
         tops = [top - 1920 for top in tail_pair(96 + 4 * group + j)]
         pairs = [pair - 1920 for top in tops for pair in tail_pair(top)]
         leaves = [leaf - 1792 - group * 32 for pair in pairs for leaf in tail_pair(pair)]
         for c in range(CLS):
-            pi = [pi_ref[c, i] for i in range(STATES)]
+            ratios = [ratio_ref[c, i] for i in range(3)]
             scale = log_ref[leaves[0], c]
             for leaf in leaves[1:]:
                 scale = scale + log_ref[leaf, c]
@@ -287,24 +310,26 @@
                         mid_ref[leaves[2 * at], c, i] * mid_ref[leaves[2 * at + 1], c, i]
                         for i in range(STATES)
                     ]
-                    quads.append(moved(joined, step_ref[8 + c, pairs[at]], mean_state(pi, joined)))
+                    quads.append(moved(joined, step_ref[8 + c, pairs[at]], mean_by_last(ratios, joined)))
                 joined = product(quads[0], quads[1])
-                halves.append(moved(joined, step_ref[8 + c, tops[h]], mean_state(pi, joined)))
+                halves.append(moved(joined, step_ref[8 + c, tops[h]], mean_by_last(ratios, joined)))
             joined = product(halves[0], halves[1])
             inverse = 1.0 / joined[3]
-            sent = [joined[0] * inverse, joined[1] * inverse, joined[2] * inverse]
-            sent.append(scale + jnp.log(joined[3]))
-            for v in range(4):
-                for q in range(4):
-                    out_ref[lax.bitwise_and(q - group, 3), j, v, 2 * c : 2 * c + 2, :] = sent[v][2 * q : 2 * q + 2, :]
-        return 0
+            for v in range(3):
+                send(3 * j + v, c, joined[v] * inverse)
+            scale = scale + jnp.log(joined[3])
+            totals[c] = scale if j == 0 else totals[c] + scale
 
     step_copy.wait()
     rate4_copy.wait()
     for load in loads:
         load.wait()
     lax.fori_loop(0, 4, small_trees, 0)
-    lax.fori_loop(0, 4, clade, 0)
+    totals = [None] * CLS
+    for j in range(4):
+        clade(j, totals)
+    for c in range(CLS):
+        send(12, c, totals[c])
 
 
 def upper_kernel(
@@ -314,10 +339,10 @@
     pi = [top_ref[TOP_PI + i] for i in range(STATES)]
     scale = top_ref[TOP_CONST]
     for hop, piece_ref in enumerate((own_ref, one_ref, two_ref, three_ref)):
+        scale = scale + piece_ref[12]
         source = 4 * lax.bitwise_and(group - hop, 3)
         for j in range(4):
-            values = [piece_ref[j, 0], piece_ref[j, 1], piece_ref[j, 2]]
-            scale = scale + piece_ref[j, 3]
+            values = [piece_ref[3 * j + i] for i in range(3)]
             average = (pi[0] * values[0] + pi[1] * values[1]) + (pi[2] * values[2] + pi[3])
             step = top_ref[TOP_RATES + source + j] * average
             for i in range(3):
@@ -398,7 +423,7 @@
     hbm = pl.BlockSpec(memory_space=pltpu.MemorySpace.HBM)
     ours, top, places = pl.pallas_call(
         lower_kernel,
-        out_shape=(pltpu.VMEM((4, 4, 4, 8, 128), FLOAT), pltpu.VMEM((TOP_ROWS, 8, 128), FLOAT), pltpu.SMEM((32,), jnp.int32)),
+        out_shape=(pltpu.VMEM((4, 13, 8, 128), FLOAT), pltpu.VMEM((TOP_ROWS, 8, 128), FLOAT), pltpu.SMEM((32,), jnp.int32)),
         in_specs=[hbm] * 6,
         out_specs=(vmem, vmem, smem),
         scratch_shapes=[
@@ -414,6 +439,7 @@
             pltpu.VMEM((16, 128), FLOAT),
             pltpu.SMEM((16, 128), FLOAT),
             pltpu.VMEM((CLS, STATES, 8, 128), FLOAT),
+            pltpu.VMEM((CLS, 3, 8, 128), FLOAT),
             pltpu.VMEM((4, 8, 128), FLOAT),
             pltpu.VMEM((4, 8, 128), FLOAT),
             pltpu.VMEM((16, 8, 128), FLOAT),

time: 35.7 us -> 35.2 us (0.986)
  no operation moved by 1% of the time
where the time goes in v9:
time: 35.2 us; the launch traced here: 35.1 us
  blocking collectives  19.3 us (55%)
  Pallas kernels  5.75 us (16%)
  starting transfers between devices  5.35 us (15%)
  waiting for transfers between devices  4.06 us (12%)
  between operations  0.66 us (2%)
    all_to_all x1, blocking collectives, per_device(): lax.all_to_all(part, ('cls', 'site'), split_axis=0, concat_axis=0, tiled=...  19.3 us
    ppermute x3, starting transfers between devices, per_device(): lax.ppermute(ours[hop], 'cls', [(k, (k + hop) % 4) for k in range(4)])  5.35 us
    pallas_call x1, Pallas kernels, per_device(): pl.pallas_call(lower_kernel, out_shape=(pltpu.VMEM((4, 13, 8, 128), FLOAT...  4.74 us
    ppermute x3, waiting for transfers between devices, per_device(): lax.ppermute(ours[hop], 'cls', [(k, (k + hop) % 4) for k in range(4)])  4.06 us
  transfers between devices with their start and end apart: 3, of which 3 were waited for; matrix products, arithmetic and copies ran while one was open for 0% of the time, Pallas kernels for 0%

profile of v9, /device:TPU:1, one launch (start us, length us, event | category | flops | bytes accessed | tf_op | source)
XLA Modules:
  0.0 35.1 jit_solution(18205706300667270837)
XLA Ops:
  0.6 4.7 %lower_tree.1 = (f32[4,13,8,128]{3,2,1,0:T(8,128)S(1)}, f32[36,8,128]{2,1,0:T(8,128)S(1)}, s32[32]{0:T(128)S(4)}) custom-call(s32[2,1023]{1,0:T(2,128)} %bitcast.25, f32[4,4]{1,0:T(4,128)} %freq_hbm.1, f32[4]{0:T(128)} %weight_hbm.1, f32[4,2046]{1,0:T(4,128)} %lengths_hbm.1, s32[2048,128]{1,0:T(8,128)} %bitcast.24, s32[8,128]{1,0:T(8,128)} %bitcast.26), custom_call_target="tpu_custom_call" | custom-call | tf_op jit(solution)/shard_map/lower_tree/pallas_call | solution.py:424
  5.4 4.6 %collective-permute-start.2 = (f32[13,8,128]{2,1,0:T(8,128)S(1)}, f32[13,8,128]{2,1,0:T(8,128)S(1)}, u32[]{:S(2)}, u32[]{:S(2)}) collective-permute-start(f32[13,8,128]{2,1,0:T(8,128)S(1)} %get-tuple-element.19), channel_id=1, source_target_pairs={{0,96},{32,0},{64,32},{96,64},{1,97},{33,1},{65,33},{97,65},{2,98}... | collective-permute-start | bytes 159752 | tf_op jit(solution)/shard_map/ppermute | solution.py:462
  10.1 0.0 collective-permute-start.1
  10.1 0.7 %collective-permute-start = (f32[13,8,128]{2,1,0:T(8,128)S(1)}, f32[13,8,128]{2,1,0:T(8,128)S(1)}, u32[]{:S(2)}, u32[]{:S(2)}) collective-permute-start(f32[13,8,128]{2,1,0:T(8,128)S(1)} %get-tuple-element.21), channel_id=1, source_target_pairs={{0,32},{32,64},{64,96},{96,0},{1,33},{33,65},{65,97},{97,1},{2,34}... | collective-permute-start | bytes 159752 | tf_op jit(solution)/shard_map/ppermute | solution.py:462
  10.8 0.5 %collective-permute-done.2.three_ref = f32[13,8,128]{2,1,0:T(8,128)S(1)} collective-permute-done((f32[13,8,128]{2,1,0:T(8,128)S(1)}, f32[13,8,128]{2,1,0:T(8,128)S(1)}, u32[]{:S(2)}, u32[]{:S(2)}) %collective-permute-start.2) | collective-permute-done | bytes 53280 | tf_op jit(solution)/shard_map/ppermute | solution.py:462
  11.3 3.4 %collective-permute-done.1.two_ref = f32[13,8,128]{2,1,0:T(8,128)S(1)} collective-permute-done((f32[13,8,128]{2,1,0:T(8,128)S(1)}, f32[13,8,128]{2,1,0:T(8,128)S(1)}, u32[]{:S(2)}, u32[]{:S(2)}) %collective-permute-start.1) | collective-permute-done | bytes 53280 | tf_op jit(solution)/shard_map/ppermute | solution.py:462
  14.6 0.2 collective-permute-done.one_ref
  14.8 0.4 %upper_tree.1 = (f32[2,128]{1,0:T(2,128)S(1)}, f32[128,128]{1,0:T(8,128)S(1)}) custom-call(s32[32]{0:T(128)S(4)} %get-tuple-element.11.place_ref, f32[13,8,128]{2,1,0:T(8,128)S(1)} %get-tuple-element.22.own_ref, f32[13,8,128]{2,1,0:T(8,128)S(1)} %collective-permute-done.one_ref, f32[13,8,128]{2,1,0:T(8,128)S(1)} %collective-permute-done.1.two_ref, ...), custom_call_target="tpu_custom_call" | custom-call | tf_op jit(solution)/shard_map/upper_tree/pallas_call | solution.py:463
  15.2 19.3 %all_to_all.11 = f32[128,1,128]{2,1,0:T(1,128)S(1)} all-to-all(f32[128,1,128]{2,1,0:T(1,128)S(1)} %bitcast.23), channel_id=1, replica_groups=mesh['cls'=4,'site'=32] {'cls','site'}, dimensions={0} | all-to-all | bytes 131072 | tf_op jit(solution)/shard_map/all_to_all | solution.py:472
  34.4 0.6 %last_sums.1 = (f32[1,1]{1,0:T(1,128)}, f32[1,1]{1,0:T(1,128)}, f32[2,128]{1,0:T(2,128)}) custom-call(f32[128,128]{1,0:T(8,128)S(1)} %bitcast.22, f32[2,128]{1,0:T(2,128)S(1)} %get-tuple-element.15.site_ref), custom_call_target="tpu_custom_call" | custom-call | tf_op jit(solution)/shard_map/last_sums/pallas_call | solution.py:473
  (1 shorter events, 0.0 us)
Async XLA Ops:
  5.4 5.9 %collective-permute-start.2 = (f32[13,8,128]{2,1,0:T(8,128)S(1)}, f32[13,8,128]{2,1,0:T(8,128)S(1)}, u32[]{:S(2)}, u32[]{:S(2)}) collective-permute-start(f32[13,8,128]{2,1,0:T(8,128)S(1)} %get-tuple-element.19), channel_id=1, source_target_pairs={{0,96},{32,0},{64,32},{96,64},{1,97},{33,1},{65,33},{97,65},{2,98}... | collective-permute-start | bytes 159752 | tf_op jit(solution)/shard_map/ppermute | solution.py:462
  10.1 4.6 %collective-permute-start.1 = (f32[13,8,128]{2,1,0:T(8,128)S(1)}, f32[13,8,128]{2,1,0:T(8,128)S(1)}, u32[]{:S(2)}, u32[]{:S(2)}) collective-permute-start(f32[13,8,128]{2,1,0:T(8,128)S(1)} %get-tuple-element.20), channel_id=1, source_target_pairs={{0,64},{32,96},{64,0},{96,32},{1,65},{33,97},{65,1},{97,33},{2,66}... | collective-permute-start | bytes 159752 | tf_op jit(solution)/shard_map/ppermute | solution.py:462
  10.1 4.8 %collective-permute-start = (f32[13,8,128]{2,1,0:T(8,128)S(1)}, f32[13,8,128]{2,1,0:T(8,128)S(1)}, u32[]{:S(2)}, u32[]{:S(2)}) collective-permute-start(f32[13,8,128]{2,1,0:T(8,128)S(1)} %get-tuple-element.21), channel_id=1, source_target_pairs={{0,32},{32,64},{64,96},{96,0},{1,33},{33,65},{65,97},{97,1},{2,34}... | collective-permute-start | bytes 159752 | tf_op jit(solution)/shard_map/ppermute | solution.py:462

commit v10 on v9

--- a/solution.py
+++ b/solution.py
@@ -128,7 +128,8 @@
         if width < 128:
             part = jnp.concatenate([part, jnp.zeros((4, 128 - width), FLOAT)], axis=1)
         total = total + part
-        rate_vec[:, 128 * k : 128 * k + 128] = jnp.exp(beta_rows * part) - 1.0
+        decay = jnp.exp(-(beta_rows * part))
+        rate_vec[:, 128 * k : 128 * k + 128] = (1.0 - decay) / decay
 
     last_pi = choose(by_class, [uniform[c][3] for c in range(CLS)])[:4]
     step_vec[0:4] = block(rate_vec, 1536 + 128 * half) * last_pi
@@ -282,8 +283,8 @@
             log_ref[n, c] = jnp.log(average)
 
     def small_trees(m, _):
-        for u in range(8):
-            small_tree(4 * m + u // 2, u % 2)
+        for u in range(16):
+            small_tree(8 * m + u // 2, u % 2)
         return 0
 
     def tail_pair(at):
@@ -324,7 +325,7 @@
     rate4_copy.wait()
     for load in loads:
         load.wait()
-    lax.fori_loop(0, 4, small_trees, 0)
+    lax.fori_loop(0, 2, small_trees, 0)
     totals = [None] * CLS
     for j in range(4):
         clade(j, totals)

time: 35.2 us -> 35.1 us (level)
  no operation moved by 1% of the time
where the time goes in v10:
time: 35.1 us; the launch traced here: 35 us
  blocking collectives  19.3 us (55%)
  Pallas kernels  5.64 us (16%)
  starting transfers between devices  5.34 us (15%)
  waiting for transfers between devices  4.06 us (12%)
  between operations  0.66 us (2%)
    all_to_all x1, blocking collectives, per_device(): lax.all_to_all(part, ('cls', 'site'), split_axis=0, concat_axis=0, tiled=...  19.3 us
    ppermute x3, starting transfers between devices, per_device(): lax.ppermute(ours[hop], 'cls', [(k, (k + hop) % 4) for k in range(4)])  5.34 us
    pallas_call x1, Pallas kernels, per_device(): pl.pallas_call(lower_kernel, out_shape=(pltpu.VMEM((4, 13, 8, 128), FLOAT...  4.64 us
    ppermute x3, waiting for transfers between devices, per_device(): lax.ppermute(ours[hop], 'cls', [(k, (k + hop) % 4) for k in range(4)])  4.06 us
  transfers between devices with their start and end apart: 3, of which 3 were waited for; matrix products, arithmetic and copies ran while one was open for 0% of the time, Pallas kernels for 0%

profile of v10, /device:TPU:1, one launch (start us, length us, event | category | flops | bytes accessed | tf_op | source)
XLA Modules:
  0.0 35.0 jit_solution(5159134087173813323)
XLA Ops:
  0.6 4.6 %lower_tree.1 = (f32[4,13,8,128]{3,2,1,0:T(8,128)S(1)}, f32[36,8,128]{2,1,0:T(8,128)S(1)}, s32[32]{0:T(128)S(4)}) custom-call(s32[2,1023]{1,0:T(2,128)} %bitcast.25, f32[4,4]{1,0:T(4,128)} %freq_hbm.1, f32[4]{0:T(128)} %weight_hbm.1, f32[4,2046]{1,0:T(4,128)} %lengths_hbm.1, s32[2048,128]{1,0:T(8,128)} %bitcast.24, s32[8,128]{1,0:T(8,128)} %bitcast.26), custom_call_target="tpu_custom_call" | custom-call | tf_op jit(solution)/shard_map/lower_tree/pallas_call | solution.py:425
  5.3 4.6 %collective-permute-start.2 = (f32[13,8,128]{2,1,0:T(8,128)S(1)}, f32[13,8,128]{2,1,0:T(8,128)S(1)}, u32[]{:S(2)}, u32[]{:S(2)}) collective-permute-start(f32[13,8,128]{2,1,0:T(8,128)S(1)} %get-tuple-element.19), channel_id=1, source_target_pairs={{0,96},{32,0},{64,32},{96,64},{1,97},{33,1},{65,33},{97,65},{2,98}... | collective-permute-start | bytes 159752 | tf_op jit(solution)/shard_map/ppermute | solution.py:463
  10.0 0.0 collective-permute-start.1
  10.0 0.7 %collective-permute-start = (f32[13,8,128]{2,1,0:T(8,128)S(1)}, f32[13,8,128]{2,1,0:T(8,128)S(1)}, u32[]{:S(2)}, u32[]{:S(2)}) collective-permute-start(f32[13,8,128]{2,1,0:T(8,128)S(1)} %get-tuple-element.21), channel_id=1, source_target_pairs={{0,32},{32,64},{64,96},{96,0},{1,33},{33,65},{65,97},{97,1},{2,34}... | collective-permute-start | bytes 159752 | tf_op jit(solution)/shard_map/ppermute | solution.py:463
  10.7 0.5 %collective-permute-done.2.three_ref = f32[13,8,128]{2,1,0:T(8,128)S(1)} collective-permute-done((f32[13,8,128]{2,1,0:T(8,128)S(1)}, f32[13,8,128]{2,1,0:T(8,128)S(1)}, u32[]{:S(2)}, u32[]{:S(2)}) %collective-permute-start.2) | collective-permute-done | bytes 53280 | tf_op jit(solution)/shard_map/ppermute | solution.py:463
  11.2 3.4 %collective-permute-done.1.two_ref = f32[13,8,128]{2,1,0:T(8,128)S(1)} collective-permute-done((f32[13,8,128]{2,1,0:T(8,128)S(1)}, f32[13,8,128]{2,1,0:T(8,128)S(1)}, u32[]{:S(2)}, u32[]{:S(2)}) %collective-permute-start.1) | collective-permute-done | bytes 53280 | tf_op jit(solution)/shard_map/ppermute | solution.py:463
  14.5 0.2 collective-permute-done.one_ref
  14.7 0.4 %upper_tree.1 = (f32[2,128]{1,0:T(2,128)S(1)}, f32[128,128]{1,0:T(8,128)S(1)}) custom-call(s32[32]{0:T(128)S(4)} %get-tuple-element.11.place_ref, f32[13,8,128]{2,1,0:T(8,128)S(1)} %get-tuple-element.22.own_ref, f32[13,8,128]{2,1,0:T(8,128)S(1)} %collective-permute-done.one_ref, f32[13,8,128]{2,1,0:T(8,128)S(1)} %collective-permute-done.1.two_ref, ...), custom_call_target="tpu_custom_call" | custom-call | tf_op jit(solution)/shard_map/upper_tree/pallas_call | solution.py:464
  15.1 19.3 %all_to_all.11 = f32[128,1,128]{2,1,0:T(1,128)S(1)} all-to-all(f32[128,1,128]{2,1,0:T(1,128)S(1)} %bitcast.23), channel_id=1, replica_groups=mesh['cls'=4,'site'=32] {'cls','site'}, dimensions={0} | all-to-all | bytes 131072 | tf_op jit(solution)/shard_map/all_to_all | solution.py:473
  34.3 0.6 %last_sums.1 = (f32[1,1]{1,0:T(1,128)}, f32[1,1]{1,0:T(1,128)}, f32[2,128]{1,0:T(2,128)}) custom-call(f32[128,128]{1,0:T(8,128)S(1)} %bitcast.22, f32[2,128]{1,0:T(2,128)S(1)} %get-tuple-element.15.site_ref), custom_call_target="tpu_custom_call" | custom-call | tf_op jit(solution)/shard_map/last_sums/pallas_call | solution.py:474
  (1 shorter events, 0.0 us)
Async XLA Ops:
  5.3 5.9 %collective-permute-start.2 = (f32[13,8,128]{2,1,0:T(8,128)S(1)}, f32[13,8,128]{2,1,0:T(8,128)S(1)}, u32[]{:S(2)}, u32[]{:S(2)}) collective-permute-start(f32[13,8,128]{2,1,0:T(8,128)S(1)} %get-tuple-element.19), channel_id=1, source_target_pairs={{0,96},{32,0},{64,32},{96,64},{1,97},{33,1},{65,33},{97,65},{2,98}... | collective-permute-start | bytes 159752 | tf_op jit(solution)/shard_map/ppermute | solution.py:463
  10.0 4.6 %collective-permute-start.1 = (f32[13,8,128]{2,1,0:T(8,128)S(1)}, f32[13,8,128]{2,1,0:T(8,128)S(1)}, u32[]{:S(2)}, u32[]{:S(2)}) collective-permute-start(f32[13,8,128]{2,1,0:T(8,128)S(1)} %get-tuple-element.20), channel_id=1, source_target_pairs={{0,64},{32,96},{64,0},{96,32},{1,65},{33,97},{65,1},{97,33},{2,66}... | collective-permute-start | bytes 159752 | tf_op jit(solution)/shard_map/ppermute | solution.py:463
  10.0 4.8 %collective-permute-start = (f32[13,8,128]{2,1,0:T(8,128)S(1)}, f32[13,8,128]{2,1,0:T(8,128)S(1)}, u32[]{:S(2)}, u32[]{:S(2)}) collective-permute-start(f32[13,8,128]{2,1,0:T(8,128)S(1)} %get-tuple-element.21), channel_id=1, source_target_pairs={{0,32},{32,64},{64,96},{96,0},{1,33},{33,65},{65,97},{97,1},{2,34}... | collective-permute-start | bytes 159752 | tf_op jit(solution)/shard_map/ppermute | solution.py:463

commit v11 on v10

--- a/solution.py
+++ b/solution.py
@@ -11,7 +11,7 @@
 SMEM = pltpu.MemorySpace.SMEM
 VMEM = pltpu.MemorySpace.VMEM
 TILE = (8, 128)
-BUILD = 8
+BUILD = 16
 TOP_RATES, TOP_PI, TOP_CONST, TOP_WEIGHT, TOP_ROWS = 0, 30, 34, 35, 36
 
 

time: 35.1 us -> 35.1 us (level)
  no operation moved by 1% of the time
where the time goes in v11:
time: 35.1 us; the launch traced here: 34.9 us
  blocking collectives  19.2 us (55%)
  Pallas kernels  5.59 us (16%)
  starting transfers between devices  5.34 us (15%)
  waiting for transfers between devices  4.07 us (12%)
  between operations  0.66 us (2%)
    all_to_all x1, blocking collectives, per_device(): lax.all_to_all(part, ('cls', 'site'), split_axis=0, concat_axis=0, tiled=...  19.2 us
    ppermute x3, starting transfers between devices, per_device(): lax.ppermute(ours[hop], 'cls', [(k, (k + hop) % 4) for k in range(4)])  5.34 us
    pallas_call x1, Pallas kernels, per_device(): pl.pallas_call(lower_kernel, out_shape=(pltpu.VMEM((4, 13, 8, 128), FLOAT...  4.58 us
    ppermute x3, waiting for transfers between devices, per_device(): lax.ppermute(ours[hop], 'cls', [(k, (k + hop) % 4) for k in range(4)])  4.07 us
  transfers between devices with their start and end apart: 3, of which 3 were waited for; matrix products, arithmetic and copies ran while one was open for 0% of the time, Pallas kernels for 0%

profile of v11, /device:TPU:1, one launch (start us, length us, event | category | flops | bytes accessed | tf_op | source)
XLA Modules:
  0.0 34.9 jit_solution(16739603178611590582)
XLA Ops:
  0.6 4.6 %lower_tree.1 = (f32[4,13,8,128]{3,2,1,0:T(8,128)S(1)}, f32[36,8,128]{2,1,0:T(8,128)S(1)}, s32[32]{0:T(128)S(4)}) custom-call(s32[2,1023]{1,0:T(2,128)} %bitcast.25, f32[4,4]{1,0:T(4,128)} %freq_hbm.1, f32[4]{0:T(128)} %weight_hbm.1, f32[4,2046]{1,0:T(4,128)} %lengths_hbm.1, s32[2048,128]{1,0:T(8,128)} %bitcast.24, s32[8,128]{1,0:T(8,128)} %bitcast.26), custom_call_target="tpu_custom_call" | custom-call | tf_op jit(solution)/shard_map/lower_tree/pallas_call | solution.py:425
  5.2 4.6 %collective-permute-start.2 = (f32[13,8,128]{2,1,0:T(8,128)S(1)}, f32[13,8,128]{2,1,0:T(8,128)S(1)}, u32[]{:S(2)}, u32[]{:S(2)}) collective-permute-start(f32[13,8,128]{2,1,0:T(8,128)S(1)} %get-tuple-element.19), channel_id=1, source_target_pairs={{0,96},{32,0},{64,32},{96,64},{1,97},{33,1},{65,33},{97,65},{2,98}... | collective-permute-start | bytes 159752 | tf_op jit(solution)/shard_map/ppermute | solution.py:463
  9.9 0.0 collective-permute-start.1
  9.9 0.7 %collective-permute-start = (f32[13,8,128]{2,1,0:T(8,128)S(1)}, f32[13,8,128]{2,1,0:T(8,128)S(1)}, u32[]{:S(2)}, u32[]{:S(2)}) collective-permute-start(f32[13,8,128]{2,1,0:T(8,128)S(1)} %get-tuple-element.21), channel_id=1, source_target_pairs={{0,32},{32,64},{64,96},{96,0},{1,33},{33,65},{65,97},{97,1},{2,34}... | collective-permute-start | bytes 159752 | tf_op jit(solution)/shard_map/ppermute | solution.py:463
  10.6 0.5 %collective-permute-done.2.three_ref = f32[13,8,128]{2,1,0:T(8,128)S(1)} collective-permute-done((f32[13,8,128]{2,1,0:T(8,128)S(1)}, f32[13,8,128]{2,1,0:T(8,128)S(1)}, u32[]{:S(2)}, u32[]{:S(2)}) %collective-permute-start.2) | collective-permute-done | bytes 53280 | tf_op jit(solution)/shard_map/ppermute | solution.py:463
  11.1 3.4 %collective-permute-done.1.two_ref = f32[13,8,128]{2,1,0:T(8,128)S(1)} collective-permute-done((f32[13,8,128]{2,1,0:T(8,128)S(1)}, f32[13,8,128]{2,1,0:T(8,128)S(1)}, u32[]{:S(2)}, u32[]{:S(2)}) %collective-permute-start.1) | collective-permute-done | bytes 53280 | tf_op jit(solution)/shard_map/ppermute | solution.py:463
  14.5 0.2 collective-permute-done.one_ref
  14.7 0.4 %upper_tree.1 = (f32[2,128]{1,0:T(2,128)S(1)}, f32[128,128]{1,0:T(8,128)S(1)}) custom-call(s32[32]{0:T(128)S(4)} %get-tuple-element.11.place_ref, f32[13,8,128]{2,1,0:T(8,128)S(1)} %get-tuple-element.22.own_ref, f32[13,8,128]{2,1,0:T(8,128)S(1)} %collective-permute-done.one_ref, f32[13,8,128]{2,1,0:T(8,128)S(1)} %collective-permute-done.1.two_ref, ...), custom_call_target="tpu_custom_call" | custom-call | tf_op jit(solution)/shard_map/upper_tree/pallas_call | solution.py:464
  15.0 19.2 %all_to_all.11 = f32[128,1,128]{2,1,0:T(1,128)S(1)} all-to-all(f32[128,1,128]{2,1,0:T(1,128)S(1)} %bitcast.23), channel_id=1, replica_groups=mesh['cls'=4,'site'=32] {'cls','site'}, dimensions={0} | all-to-all | bytes 131072 | tf_op jit(solution)/shard_map/all_to_all | solution.py:473
  34.3 0.6 %last_sums.1 = (f32[1,1]{1,0:T(1,128)}, f32[1,1]{1,0:T(1,128)}, f32[2,128]{1,0:T(2,128)}) custom-call(f32[128,128]{1,0:T(8,128)S(1)} %bitcast.22, f32[2,128]{1,0:T(2,128)S(1)} %get-tuple-element.15.site_ref), custom_call_target="tpu_custom_call" | custom-call | tf_op jit(solution)/shard_map/last_sums/pallas_call | solution.py:474
  (1 shorter events, 0.0 us)
Async XLA Ops:
  5.2 5.9 %collective-permute-start.2 = (f32[13,8,128]{2,1,0:T(8,128)S(1)}, f32[13,8,128]{2,1,0:T(8,128)S(1)}, u32[]{:S(2)}, u32[]{:S(2)}) collective-permute-start(f32[13,8,128]{2,1,0:T(8,128)S(1)} %get-tuple-element.19), channel_id=1, source_target_pairs={{0,96},{32,0},{64,32},{96,64},{1,97},{33,1},{65,33},{97,65},{2,98}... | collective-permute-start | bytes 159752 | tf_op jit(solution)/shard_map/ppermute | solution.py:463
  9.9 4.6 %collective-permute-start.1 = (f32[13,8,128]{2,1,0:T(8,128)S(1)}, f32[13,8,128]{2,1,0:T(8,128)S(1)}, u32[]{:S(2)}, u32[]{:S(2)}) collective-permute-start(f32[13,8,128]{2,1,0:T(8,128)S(1)} %get-tuple-element.20), channel_id=1, source_target_pairs={{0,64},{32,96},{64,0},{96,32},{1,65},{33,97},{65,1},{97,33},{2,66}... | collective-permute-start | bytes 159752 | tf_op jit(solution)/shard_map/ppermute | solution.py:463
  9.9 4.8 %collective-permute-start = (f32[13,8,128]{2,1,0:T(8,128)S(1)}, f32[13,8,128]{2,1,0:T(8,128)S(1)}, u32[]{:S(2)}, u32[]{:S(2)}) collective-permute-start(f32[13,8,128]{2,1,0:T(8,128)S(1)} %get-tuple-element.21), channel_id=1, source_target_pairs={{0,32},{32,64},{64,96},{96,0},{1,33},{33,65},{65,97},{97,1},{2,34}... | collective-permute-start | bytes 159752 | tf_op jit(solution)/shard_map/ppermute | solution.py:463

commit v12 on v11

--- a/solution.py
+++ b/solution.py
@@ -103,7 +103,7 @@
     spot_vec[6:8] = jnp.concatenate([child_vec[:, 896:1023], jnp.zeros((2, 1), jnp.int32)], axis=1)
     spot_copy = pltpu.make_async_copy(spot_vec, spot_ref, sems.at[9])
     spot_copy.start()
-    for load in small[1:]:
+    for load in small[1:4]:
         load.wait()
 
     lane = lax.broadcasted_iota(jnp.int32, TILE, 1)
@@ -190,6 +190,7 @@
     last = choose(by_pair, [jnp.broadcast_to(last[c : c + 1], TILE) for c in range(CLS)])
     for k in range(30):
         top_ref[TOP_RATES + k] = jnp.broadcast_to(last[:, 96 + k : 97 + k], TILE)
+    small[4].wait()
     quarter = counts_ref[pl.ds(2 * group, 2), :].astype(FLOAT)
     top_ref[TOP_WEIGHT] = jnp.concatenate([quarter, quarter, quarter, quarter], axis=0)
     spot_copy.wait()

time: 35.1 us -> 35.1 us (level)
  no operation moved by 1% of the time
where the time goes in v12:
time: 35.1 us; the launch traced here: 34.9 us
  blocking collectives  19.2 us (55%)
  Pallas kernels  5.59 us (16%)
  starting transfers between devices  5.35 us (15%)
  waiting for transfers between devices  4.06 us (12%)
  between operations  0.66 us (2%)
    all_to_all x1, blocking collectives, per_device(): lax.all_to_all(part, ('cls', 'site'), split_axis=0, concat_axis=0, tiled=...  19.2 us
    ppermute x3, starting transfers between devices, per_device(): lax.ppermute(ours[hop], 'cls', [(k, (k + hop) % 4) for k in range(4)])  5.35 us
    pallas_call x1, Pallas kernels, per_device(): pl.pallas_call(lower_kernel, out_shape=(pltpu.VMEM((4, 13, 8, 128), FLOAT...  4.58 us
    ppermute x3, waiting for transfers between devices, per_device(): lax.ppermute(ours[hop], 'cls', [(k, (k + hop) % 4) for k in range(4)])  4.06 us
  transfers between devices with their start and end apart: 3, of which 3 were waited for; matrix products, arithmetic and copies ran while one was open for 0% of the time, Pallas kernels for 0%

profile of v12, /device:TPU:1, one launch (start us, length us, event | category | flops | bytes accessed | tf_op | source)
XLA Modules:
  0.0 34.9 jit_solution(5292707979389490976)
XLA Ops:
  0.6 4.6 %lower_tree.1 = (f32[4,13,8,128]{3,2,1,0:T(8,128)S(1)}, f32[36,8,128]{2,1,0:T(8,128)S(1)}, s32[32]{0:T(128)S(4)}) custom-call(s32[2,1023]{1,0:T(2,128)} %bitcast.25, f32[4,4]{1,0:T(4,128)} %freq_hbm.1, f32[4]{0:T(128)} %weight_hbm.1, f32[4,2046]{1,0:T(4,128)} %lengths_hbm.1, s32[2048,128]{1,0:T(8,128)} %bitcast.24, s32[8,128]{1,0:T(8,128)} %bitcast.26), custom_call_target="tpu_custom_call" | custom-call | tf_op jit(solution)/shard_map/lower_tree/pallas_call | solution.py:426
  5.2 4.6 %collective-permute-start.2 = (f32[13,8,128]{2,1,0:T(8,128)S(1)}, f32[13,8,128]{2,1,0:T(8,128)S(1)}, u32[]{:S(2)}, u32[]{:S(2)}) collective-permute-start(f32[13,8,128]{2,1,0:T(8,128)S(1)} %get-tuple-element.19), channel_id=1, source_target_pairs={{0,96},{32,0},{64,32},{96,64},{1,97},{33,1},{65,33},{97,65},{2,98}... | collective-permute-start | bytes 159752 | tf_op jit(solution)/shard_map/ppermute | solution.py:464
  9.9 0.0 collective-permute-start.1
  9.9 0.7 %collective-permute-start = (f32[13,8,128]{2,1,0:T(8,128)S(1)}, f32[13,8,128]{2,1,0:T(8,128)S(1)}, u32[]{:S(2)}, u32[]{:S(2)}) collective-permute-start(f32[13,8,128]{2,1,0:T(8,128)S(1)} %get-tuple-element.21), channel_id=1, source_target_pairs={{0,32},{32,64},{64,96},{96,0},{1,33},{33,65},{65,97},{97,1},{2,34}... | collective-permute-start | bytes 159752 | tf_op jit(solution)/shard_map/ppermute | solution.py:464
  10.6 0.5 %collective-permute-done.2.three_ref = f32[13,8,128]{2,1,0:T(8,128)S(1)} collective-permute-done((f32[13,8,128]{2,1,0:T(8,128)S(1)}, f32[13,8,128]{2,1,0:T(8,128)S(1)}, u32[]{:S(2)}, u32[]{:S(2)}) %collective-permute-start.2) | collective-permute-done | bytes 53280 | tf_op jit(solution)/shard_map/ppermute | solution.py:464
  11.1 3.4 %collective-permute-done.1.two_ref = f32[13,8,128]{2,1,0:T(8,128)S(1)} collective-permute-done((f32[13,8,128]{2,1,0:T(8,128)S(1)}, f32[13,8,128]{2,1,0:T(8,128)S(1)}, u32[]{:S(2)}, u32[]{:S(2)}) %collective-permute-start.1) | collective-permute-done | bytes 53280 | tf_op jit(solution)/shard_map/ppermute | solution.py:464
  14.5 0.2 collective-permute-done.one_ref
  14.7 0.4 %upper_tree.1 = (f32[2,128]{1,0:T(2,128)S(1)}, f32[128,128]{1,0:T(8,128)S(1)}) custom-call(s32[32]{0:T(128)S(4)} %get-tuple-element.11.place_ref, f32[13,8,128]{2,1,0:T(8,128)S(1)} %get-tuple-element.22.own_ref, f32[13,8,128]{2,1,0:T(8,128)S(1)} %collective-permute-done.one_ref, f32[13,8,128]{2,1,0:T(8,128)S(1)} %collective-permute-done.1.two_ref, ...), custom_call_target="tpu_custom_call" | custom-call | tf_op jit(solution)/shard_map/upper_tree/pallas_call | solution.py:465
  15.0 19.2 %all_to_all.11 = f32[128,1,128]{2,1,0:T(1,128)S(1)} all-to-all(f32[128,1,128]{2,1,0:T(1,128)S(1)} %bitcast.23), channel_id=1, replica_groups=mesh['cls'=4,'site'=32] {'cls','site'}, dimensions={0} | all-to-all | bytes 131072 | tf_op jit(solution)/shard_map/all_to_all | solution.py:474
  34.3 0.6 %last_sums.1 = (f32[1,1]{1,0:T(1,128)}, f32[1,1]{1,0:T(1,128)}, f32[2,128]{1,0:T(2,128)}) custom-call(f32[128,128]{1,0:T(8,128)S(1)} %bitcast.22, f32[2,128]{1,0:T(2,128)S(1)} %get-tuple-element.15.site_ref), custom_call_target="tpu_custom_call" | custom-call | tf_op jit(solution)/shard_map/last_sums/pallas_call | solution.py:475
  (1 shorter events, 0.0 us)
Async XLA Ops:
  5.2 5.9 %collective-permute-start.2 = (f32[13,8,128]{2,1,0:T(8,128)S(1)}, f32[13,8,128]{2,1,0:T(8,128)S(1)}, u32[]{:S(2)}, u32[]{:S(2)}) collective-permute-start(f32[13,8,128]{2,1,0:T(8,128)S(1)} %get-tuple-element.19), channel_id=1, source_target_pairs={{0,96},{32,0},{64,32},{96,64},{1,97},{33,1},{65,33},{97,65},{2,98}... | collective-permute-start | bytes 159752 | tf_op jit(solution)/shard_map/ppermute | solution.py:464
  9.9 4.6 %collective-permute-start.1 = (f32[13,8,128]{2,1,0:T(8,128)S(1)}, f32[13,8,128]{2,1,0:T(8,128)S(1)}, u32[]{:S(2)}, u32[]{:S(2)}) collective-permute-start(f32[13,8,128]{2,1,0:T(8,128)S(1)} %get-tuple-element.20), channel_id=1, source_target_pairs={{0,64},{32,96},{64,0},{96,32},{1,65},{33,97},{65,1},{97,33},{2,66}... | collective-permute-start | bytes 159752 | tf_op jit(solution)/shard_map/ppermute | solution.py:464
  9.9 4.8 %collective-permute-start = (f32[13,8,128]{2,1,0:T(8,128)S(1)}, f32[13,8,128]{2,1,0:T(8,128)S(1)}, u32[]{:S(2)}, u32[]{:S(2)}) collective-permute-start(f32[13,8,128]{2,1,0:T(8,128)S(1)} %get-tuple-element.21), channel_id=1, source_target_pairs={{0,32},{32,64},{64,96},{96,0},{1,33},{33,65},{65,97},{97,1},{2,34}... | collective-permute-start | bytes 159752 | tf_op jit(solution)/shard_map/ppermute | solution.py:464
